TPU v7x, 64 devices: a 2x2x8 block of a 4x4x8 slice. The times are simulated.
64 devices in a mesh: dp: 4 (over x, y), sp: 16 (over z, core).
Axes of the slice: x: 2, y: 2, z: 8, core: 2. Of those that a mesh axis runs over, the one named last changes fastest.
The devices are a block of a 4x4x8 slice.
Arguments:
- hidden: bfloat16 [4, 4096, 2048], P('dp', 'sp'), parts along dimension 0
- d_out: bfloat16 [4, 4096, 2048], P('dp', 'sp'), parts along dimension 0
- positions: int32 [4, 4096], P('dp', 'sp'), parts along dimension 0
- norm_gain: bfloat16 [2048], replicated
- w_query: bfloat16 [2048, 2048], replicated
- b_query: bfloat16 [2048], replicated
- w_key: bfloat16 [2048, 256], replicated
- b_key: bfloat16 [256], replicated
- w_value: bfloat16 [2048, 256], replicated
- b_value: bfloat16 [256], replicated
- w_out: bfloat16 [2048, 2048], replicated
Outputs:
- output 1: bfloat16 [4, 4096, 2048], P('dp', 'sp'), parts along dimension 0
- output 2: bfloat16 [4, 4096, 2048], P('dp', 'sp'), parts along dimension 0
- output 3: float32 [8192], P('dp'), parts along dimension 0
- output 4: float32 [8192, 2048], P('dp'), parts along dimension 0
- output 5: float32 [8192], P('dp'), parts along dimension 0
- output 6: float32 [8192, 256], P('dp'), parts along dimension 0
- output 7: float32 [1024], P('dp'), parts along dimension 0
- output 8: float32 [8192, 256], P('dp'), parts along dimension 0
- output 9: float32 [1024], P('dp'), parts along dimension 0
- output 10: float32 [8192, 2048], P('dp'), parts along dimension 0
There are 4 independent parts. A program takes and returns all parts, laid end to end along the dimension named above; an argument that names none is the same for every part.
All inputs are finite; a program needn't handle non-finite values.
Results may differ from a plain program's by a relative error of at most 0.02.
Values are sent between devices in bfloat16 or wider.
A program may use at most 768 MiB of HBM per device.

v0:
```python
import math
import jax
import jax.numpy as jnp
from jax import lax
from jax.sharding import PartitionSpec as P

HEAD_DIM = 128
ROPE_BASE = 1000000.0
NORM_EPS = 1e-6


def rope_tables(positions):
    half_dim = HEAD_DIM // 2
    inv_freq = ROPE_BASE ** (-jnp.arange(half_dim, dtype=jnp.float32) * (2.0 / HEAD_DIM))
    angles = positions.astype(jnp.float32)[..., None] * inv_freq
    return jnp.cos(angles)[:, :, None, :], jnp.sin(angles)[:, :, None, :]


def rotate(vec, cosine, sine):
    half_dim = vec.shape[-1] // 2
    first = vec[..., :half_dim]
    second = vec[..., half_dim:]
    return jnp.concatenate([first * cosine - second * sine, second * cosine + first * sine], axis=-1)


def norm_forward(hidden, norm_gain):
    hidden_f = hidden.astype(jnp.float32)
    inv_rms = lax.rsqrt(jnp.mean(hidden_f * hidden_f, axis=-1, keepdims=True) + NORM_EPS)
    unit = hidden_f * inv_rms
    return (unit * norm_gain.astype(jnp.float32)).astype(jnp.bfloat16), unit, inv_rms


def norm_backward(d_normed, unit, inv_rms, norm_gain):
    d_unit = d_normed * norm_gain.astype(jnp.float32)
    d_input = inv_rms * (d_unit - unit * jnp.mean(d_unit * unit, axis=-1, keepdims=True))
    return d_input, d_normed * unit


def block_size(batch, heads, seq):
    return math.gcd(seq, max(8, (1 << 24) // (batch * heads * seq)))


def attn_forward(query, keys, values):
    batch, seq, kv_local, group, head_dim = query.shape
    block_len = block_size(batch, kv_local * group, seq)
    n_blocks = seq // block_len
    scale = head_dim ** -0.5
    key_pos = jnp.arange(seq)

    def one_block(index):
        q_block = lax.dynamic_slice_in_dim(query, index * block_len, block_len, axis=1)
        scores = jnp.einsum('bqkgd,bskd->bkgqs', q_block, keys, preferred_element_type=jnp.float32) * scale
        q_pos = index * block_len + jnp.arange(block_len)
        scores = jnp.where(key_pos[None, :] <= q_pos[:, None], scores, -1e30)
        peak = jnp.max(scores, axis=-1, keepdims=True)
        exp_scores = jnp.exp(scores - peak)
        total = jnp.sum(exp_scores, axis=-1, keepdims=True)
        probs = (exp_scores / total).astype(jnp.bfloat16)
        out_block = jnp.einsum('bkgqs,bskd->bqkgd', probs, values, preferred_element_type=jnp.float32)
        return out_block.astype(jnp.bfloat16), (peak + jnp.log(total))[..., 0]

    out_blocks, lse_blocks = lax.map(one_block, jnp.arange(n_blocks))
    attended = jnp.moveaxis(out_blocks, 0, 1).reshape(batch, seq, kv_local, group, head_dim)
    return attended, lse_blocks


def attn_backward(query, keys, values, lse_blocks, d_att, delta):
    batch, seq, kv_local, group, head_dim = query.shape
    block_len = block_size(batch, kv_local * group, seq)
    n_blocks = seq // block_len
    scale = head_dim ** -0.5
    key_pos = jnp.arange(seq)

    def one_block(carry, index):
        d_keys, d_values = carry
        start = index * block_len
        q_block = lax.dynamic_slice_in_dim(query, start, block_len, axis=1)
        do_block = lax.dynamic_slice_in_dim(d_att, start, block_len, axis=1)
        delta_block = lax.dynamic_slice_in_dim(delta, start, block_len, axis=3)
        lse_block = lax.dynamic_index_in_dim(lse_blocks, index, axis=0, keepdims=False)
        scores = jnp.einsum('bqkgd,bskd->bkgqs', q_block, keys, preferred_element_type=jnp.float32) * scale
        q_pos = start + jnp.arange(block_len)
        scores = jnp.where(key_pos[None, :] <= q_pos[:, None], scores, -1e30)
        probs = jnp.exp(scores - lse_block[..., None])
        d_probs = jnp.einsum('bqkgd,bskd->bkgqs', do_block, values, preferred_element_type=jnp.float32)
        d_scores = (probs * (d_probs - delta_block[..., None]) * scale).astype(jnp.bfloat16)
        d_values = d_values + jnp.einsum('bkgqs,bqkgd->bskd', probs.astype(jnp.bfloat16), do_block,
                                         preferred_element_type=jnp.float32)
        d_keys = d_keys + jnp.einsum('bkgqs,bqkgd->bskd', d_scores, q_block, preferred_element_type=jnp.float32)
        dq_block = jnp.einsum('bkgqs,bskd->bqkgd', d_scores, keys, preferred_element_type=jnp.float32)
        return (d_keys, d_values), dq_block.astype(jnp.bfloat16)

    zeros = jnp.zeros(keys.shape, jnp.float32)
    (d_keys, d_values), dq_blocks = lax.scan(one_block, (zeros, zeros), jnp.arange(n_blocks))
    d_query = jnp.moveaxis(dq_blocks, 0, 1).reshape(query.shape)
    return d_query, d_keys, d_values


def solution(mesh):
    sp_size = mesh.shape['sp']

    def device_step(hidden, d_out, positions, norm_gain, w_query, b_query, w_key, b_key, w_value, b_value, w_out):
        batch, tokens, d_model = hidden.shape
        seq = tokens * sp_size
        q_heads = d_model // HEAD_DIM
        kv_heads = w_key.shape[1] // HEAD_DIM
        kv_width = kv_heads * HEAD_DIM
        kv_dup = max(kv_heads, sp_size)
        copies = kv_dup // kv_heads
        heads_local = q_heads // sp_size
        kv_local = kv_dup // sp_size
        group = heads_local // kv_local
        cosine, sine = rope_tables(positions)

        normed, unit, inv_rms = norm_forward(hidden, norm_gain)
        q_pre = jnp.einsum('btd,de->bte', normed, w_query, preferred_element_type=jnp.float32) + b_query.astype(jnp.float32)
        query = rotate(q_pre.reshape(batch, tokens, q_heads, HEAD_DIM), cosine, sine).astype(jnp.bfloat16)
        k_pre = jnp.einsum('btd,de->bte', normed, w_key, preferred_element_type=jnp.float32) + b_key.astype(jnp.float32)
        keys = rotate(k_pre.reshape(batch, tokens, kv_heads, HEAD_DIM), cosine, sine).astype(jnp.bfloat16)
        v_pre = jnp.einsum('btd,de->bte', normed, w_value, preferred_element_type=jnp.float32) + b_value.astype(jnp.float32)
        values = v_pre.astype(jnp.bfloat16).reshape(batch, tokens, kv_heads, HEAD_DIM)
        if copies > 1:
            keys = jnp.repeat(keys, copies, axis=2)
            values = jnp.repeat(values, copies, axis=2)

        query_h = lax.all_to_all(query, 'sp', 2, 1, tiled=True).reshape(batch, seq, kv_local, group, HEAD_DIM)
        keys_h = lax.all_to_all(keys, 'sp', 2, 1, tiled=True)
        values_h = lax.all_to_all(values, 'sp', 2, 1, tiled=True)
        attended_h, lse_blocks = attn_forward(query_h, keys_h, values_h)
        attended = lax.all_to_all(attended_h.reshape(batch, seq, heads_local, HEAD_DIM), 'sp', 1, 2, tiled=True)
        attended = attended.reshape(batch, tokens, d_model)
        proj = jnp.einsum('btd,de->bte', attended, w_out, preferred_element_type=jnp.float32)
        block_out = (hidden.astype(jnp.float32) + proj).astype(jnp.bfloat16)

        d_w_out = jnp.einsum('btd,bte->de', attended, d_out, preferred_element_type=jnp.float32)
        d_att = jnp.einsum('bte,de->btd', d_out, w_out, preferred_element_type=jnp.float32).astype(jnp.bfloat16)
        d_att_h = lax.all_to_all(d_att.reshape(batch, tokens, q_heads, HEAD_DIM), 'sp', 2, 1, tiled=True)
        d_att_h = d_att_h.reshape(batch, seq, kv_local, group, HEAD_DIM)
        delta = jnp.einsum('bskgd,bskgd->bkgs', d_att_h, attended_h, preferred_element_type=jnp.float32)
        dq_h, dk_h, dv_h = attn_backward(query_h, keys_h, values_h, lse_blocks, d_att_h, delta)

        d_query = lax.all_to_all(dq_h.reshape(batch, seq, heads_local, HEAD_DIM), 'sp', 1, 2, tiled=True)
        wire_type = jnp.float32 if copies > 1 else jnp.bfloat16
        d_keys = lax.all_to_all(dk_h.astype(wire_type), 'sp', 1, 2, tiled=True)
        d_values = lax.all_to_all(dv_h.astype(wire_type), 'sp', 1, 2, tiled=True)
        if copies > 1:
            d_keys = jnp.sum(d_keys.reshape(batch, tokens, kv_heads, copies, HEAD_DIM), axis=3)
            d_values = jnp.sum(d_values.reshape(batch, tokens, kv_heads, copies, HEAD_DIM), axis=3)

        dq_pre = rotate(d_query.astype(jnp.float32), cosine, -sine).reshape(batch, tokens, d_model)
        dk_pre = rotate(d_keys.astype(jnp.float32), cosine, -sine).reshape(batch, tokens, kv_width)
        dv_pre = d_values.astype(jnp.float32).reshape(batch, tokens, kv_width)
        dq_bf = dq_pre.astype(jnp.bfloat16)
        dk_bf = dk_pre.astype(jnp.bfloat16)
        dv_bf = dv_pre.astype(jnp.bfloat16)
        d_w_query = jnp.einsum('btd,bte->de', normed, dq_bf, preferred_element_type=jnp.float32)
        d_w_key = jnp.einsum('btd,bte->de', normed, dk_bf, preferred_element_type=jnp.float32)
        d_w_value = jnp.einsum('btd,bte->de', normed, dv_bf, preferred_element_type=jnp.float32)
        d_normed = (jnp.einsum('bte,de->btd', dq_bf, w_query, preferred_element_type=jnp.float32)
                    + jnp.einsum('bte,de->btd', dk_bf, w_key, preferred_element_type=jnp.float32)
                    + jnp.einsum('bte,de->btd', dv_bf, w_value, preferred_element_type=jnp.float32))
        d_input, gain_terms = norm_backward(d_normed, unit, inv_rms, norm_gain)
        d_hidden = (d_out.astype(jnp.float32) + d_input).astype(jnp.bfloat16)
        grads = lax.psum((jnp.sum(gain_terms, axis=(0, 1)), d_w_query, jnp.sum(dq_pre, axis=(0, 1)),
                          d_w_key, jnp.sum(dk_pre, axis=(0, 1)), d_w_value, jnp.sum(dv_pre, axis=(0, 1)),
                          d_w_out), 'sp')
        return (block_out, d_hidden) + tuple(grads)

    seq_spec = P('dp', 'sp', None)
    in_specs = (seq_spec, seq_spec, P('dp', 'sp'), P(), P(), P(), P(), P(), P(), P(), P())
    out_specs = (seq_spec, seq_spec, P('dp'), P('dp', None), P('dp'), P('dp', None), P('dp'),
                 P('dp', None), P('dp'), P('dp', None))
    return jax.shard_map(device_step, mesh=mesh, in_specs=in_specs, out_specs=out_specs, check_vma=False)
```

profile of v0, /device:TPU:21, one launch (start us, length us, event | category | flops | bytes accessed | tf_op | source)
XLA Modules:
  0.0 912.1 jit_solution(6525993380806893562)
XLA Ops:
  10.9 2.2 convolution_add_fusion.3
  15.8 10.7 %all-to-all-start.1 = ((bf16[1,256,16,128]{3,1,0,2:T(8,128)(2,1)}), bf16[1,256,16,128]{3,1,0,2:T(8,128)(2,1)S(1)}, u32[]{:S(2)}, u32[]{:S(2)}) async-start(bf16[1,256,16,128]{3,1,0,2:T(8,128)(2,1)} %bitcast.202), calls=%async_computation.1 | async-start | bytes 2097152 | tf_op jit(solution)/shard_map/all_to_all | solution.py:127
  26.6 5.7 fusion.43
  33.8 20.6 %all-to-all-done.1 = bf16[1,256,16,128]{3,1,0,2:T(8,128)(2,1)S(1)} async-done(((bf16[1,256,16,128]{3,1,0,2:T(8,128)(2,1)}), bf16[1,256,16,128]{3,1,0,2:T(8,128)(2,1)S(1)}, u32[]{:S(2)}, u32[]{:S(2)}) %all-to-all-start.1) | async-done | bytes 1048608 | tf_op jit(solution)/shard_map/all_to_all | solution.py:127
  55.4 3.9 all-to-all-start.4
  59.5 5.8 fusion.42
  69.3 17.6 %all-to-all-done.4 = bf16[1,256,16,128]{3,1,0,2:T(8,128)(2,1)S(1)} async-done(((bf16[1,256,16,128]{3,1,0,2:T(8,128)(2,1)}), bf16[1,256,16,128]{3,1,0,2:T(8,128)(2,1)S(1)}, u32[]{:S(2)}, u32[]{:S(2)}) %all-to-all-start.4) | async-done | bytes 1048608 | tf_op jit(solution)/shard_map/all_to_all | solution.py:137
  86.8 4.7 all-to-all-start.2
  93.9 2.9 copy.135
  96.8 21.0 %all-to-all-done.2 = bf16[1,256,16,128]{3,1,0,2:T(8,128)(2,1)} async-done(((bf16[1,256,16,128]{3,1,0,2:T(8,128)(2,1)}), bf16[1,256,16,128]{3,1,0,2:T(8,128)(2,1)}, u32[]{:S(2)}, u32[]{:S(2)}) %all-to-all-start.2) | async-done | bytes 1048608 | tf_op jit(solution)/shard_map/all_to_all | solution.py:126
  119.0 3.9 all-to-all-start
  122.9 26.7 %fusion.67 = (f32[4096]{0:T(1024)S(1)}, f32[1,1,1,4096,4096]{3,4,2,1,0:T(8,128)}) fusion(bf16[4096,128]{1,0:T(8,128)(2,1)} %bitcast.195, bf16[4096,128]{1,0:T(8,128)(2,1)} %bitcast.17), kind=kOutput, calls=%fused_computation.91 | convolution fusion | flops 4362072064 | bytes 69222400 | tf_op jit(solution)/shard_map/while/body/eval_jaxpr/bqkgd,bskd->bkgqs/dot_general | solution.py:52
  149.6 21.3 %fusion.2 = f32[4096]{0:T(1024)S(1)} fusion(f32[1,1,1,4096,4096]{3,4,2,1,0:T(8,128)} %get-tuple-element.90, f32[4096]{0:T(1024)S(1)} %get-tuple-element.89), kind=kLoop, calls=%fused_computation.9 | loop fusion | flops 33550336 | bytes 67141632 | tf_op jit(solution)/shard_map/while/body/eval_jaxpr/reduce_sum | solution.py:57
  170.8 25.4 %multiply_reduce_fusion = (f32[4096]{0:T(1024)S(1)}, bf16[128,4096]{1,0:T(8,128)(2,1)}) fusion(f32[4096,128]{0,1:T(8,128)} %copy.135, bf16[4096,128]{1,0:T(8,128)(2,1)S(1)} %bitcast.193, f32[4096]{0:T(1024)S(1)} %fusion.2, f32[1,1,1,4096,4096]{3,4,2,1,0:T(8,128)} %get-tuple-element.90, f32[4096]{0:T(1024)S(1)} %get-tuple-element.89), kind=kOutput, calls=%fused_computation.50 | convolution fusion | flops 4347392000 | bytes 71352320 | tf_op jit(solution)/shard_map/while/body/eval_jaxpr/bkgqs,bskd->bqkgd/dot_general | solution.py:59
  196.3 5.5 copy.117
  202.3 24.8 %reduce.19 = bf16[4096,128]{1,0:T(8,128)(2,1)} reduce(bf16[4096,1,1,128]{3,2,1,0:T(2,128)(2,1)} %bitcast.191, bf16[]{:T(256)} %broadcast.146), dimensions={1,2}, to_apply=%bitcast.154.reduce_sub_computation | reduce | bytes 2097154
  227.1 2.1 reshape.526
  229.3 7.2 all-to-all-start.3
  236.5 36.9 %fusion.1 = bf16[1,1,1,4096,4096]{3,4,2,1,0:T(8,128)(2,1)} fusion(f32[1,1,1,4096,4096]{3,4,2,1,0:T(8,128)} %get-tuple-element.90, bf16[4096,128]{1,0:T(8,128)(2,1)S(1)} %bitcast.194, bf16[4096,128]{1,0:T(8,128)(2,1)S(1)} %bitcast.185, f32[4096]{0:T(1024)S(1)} %get-tuple-element.91, f32[4096]{0:T(1024)S(1)} %log_add_fusion), kind=kOutput, calls=%fused_computation.3 | convolution fusion | flops 4378853376 | bytes 102793216 | tf_op jit(solution)/shard_map/while/body/eval_jaxpr/bqkgd,bskd->bkgqs/dot_general | solution.py:85
  273.5 15.4 %fusion.26 = bf16[1,4096,1,128]{1,3,2,0:T(8,128)(2,1)S(1)} fusion(bf16[4096,128]{1,0:T(8,128)(2,1)} %bitcast.196, bf16[1,1,1,4096,4096]{3,4,2,1,0:T(8,128)(2,1)} %fusion.1), kind=kOutput, calls=%fused_computation.24 | convolution fusion | flops 4295491584 | bytes 35651584 | tf_op jit(solution)/shard_map/while/body/eval_jaxpr/bkgqs,bskd->bqkgd/dot_general | solution.py:90
  288.9 3.9 copy.120
  292.7 23.6 %reduce.20 = bf16[4096,128]{1,0:T(8,128)(2,1)S(1)} reduce(bf16[4096,1,1,128]{3,2,1,0:T(2,128)(2,1)} %bitcast.192, bf16[]{:T(256)} %broadcast.146), dimensions={1,2}, to_apply=%bitcast.156.reduce_sub_computation | reduce | bytes 2097154
  317.5 7.3 all-to-all-start.5
  324.7 24.7 %fusion.17 = f32[1,4096,1,128]{1,3,2,0:T(8,128)} fusion(bf16[4096,128]{1,0:T(8,128)(2,1)S(1)} %bitcast.186, f32[1,1,1,4096,4096]{3,4,2,1,0:T(8,128)} %get-tuple-element.90, f32[4096]{0:T(1024)S(1)} %log_add_fusion), kind=kOutput, calls=%fused_computation.21 | convolution fusion | flops 4328521728 | bytes 70270976 | tf_op jit(solution)/shard_map/while/body/eval_jaxpr/bkgqs,bqkgd->bskd/dot_general | solution.py:87
  349.4 5.6 copy.127
  356.0 7.2 all-to-all-start.7
  363.2 16.1 %fusion.14 = f32[1,4096,1,128]{1,3,2,0:T(8,128)S(1)} fusion(bf16[4096,128]{1,0:T(8,128)(2,1)} %bitcast.17, bf16[1,1,1,4096,4096]{3,4,2,1,0:T(8,128)(2,1)} %fusion.1), kind=kOutput, calls=%fused_computation.20 | convolution fusion | flops 4294967296 | bytes 36700160 | tf_op jit(solution)/shard_map/while/body/eval_jaxpr/bkgqs,bqkgd->bskd/dot_general | solution.py:89
  379.4 3.7 copy.124
  383.1 29.0 %all-to-all-done.7 = f32[1,4096,1,128]{3,2,0,1:T(1,128)} async-done(((f32[1,4096,1,128]{3,2,0,1:T(1,128)}), f32[1,4096,1,128]{3,2,0,1:T(1,128)}, u32[]{:S(2)}, u32[]{:S(2)}) %all-to-all-start.7) | async-done | bytes 2097184 | tf_op jit(solution)/shard_map/all_to_all | solution.py:145
  412.0 5.4 all-to-all-start.6
  417.8 4.3 reshape.527
  424.9 3.4 reshape.529
  435.8 9.9 %fusion.46 = f32[2048,2048]{1,0:T(8,128)} fusion(bf16[256,2048]{0,1:T(8,128)(2,1)S(1)} %bitcast.187, bf16[1,256,2048]{2,1,0:T(8,128)(2,1)} %param.12), kind=kOutput, calls=%fused_computation.62 | convolution fusion | flops 2147483648 | bytes 18874368 | tf_op jit(solution)/shard_map/btd,bte->de/dot_general | solution.py:135
  445.7 8.7 fusion.60
  454.3 3.3 copy.128
  457.7 8.6 all-to-all-done.6
  470.2 2.2 bitcast_reduce_fusion
  472.4 2.0 fusion.56
  476.4 3.5 fusion.49
  480.0 7.1 fusion.68
  487.1 6.7 fusion.33
  496.1 2.4 convolution_add_fusion.1
  498.5 2.3 fusion.40
  500.8 43.8 %all-reduce = (f32[2048]{0:T(1024)}, f32[2048]{0:T(1024)}, f32[256]{0:T(256)}, f32[256]{0:T(256)}) all-reduce(f32[2048]{0:T(1024)S(1)} %get-tuple-element.53, f32[2048]{0:T(1024)S(1)} %bitcast.212, f32[256]{0:T(256)S(1)} %bitcast.213, f32[256]{0:T(256)S(1)} %bitcast.215), channel_id=1, replica_groups=mesh['dp'=4,'sp'=16] {'sp'}, use_global_device_ids=true, to_apply=%region_7.8 | all-reduce | flops 4608 | bytes 36864 | tf_op jit(solution)/shard_map/psum | solution.py:164
  544.6 3.2 fusion.39
  547.9 331.8 %all-reduce.4.cloned.1.call-done = (f32[2048,2048]{1,0:T(8,128)}, f32[2048,256]{1,0:T(8,128)}, f32[2048,256]{1,0:T(8,128)}, f32[2048,2048]{1,0:T(8,128)}) async-done(((f32[2048,2048]{1,0:T(8,128)}, f32[2048,256]{1,0:T(8,128)}, f32[2048,256]{1,0:T(8,128)}, f32[2048,2048]{1,0:T(8,128)}), (f32[2048,2048]{1,0:T(8,128)}, f32[2048,256]{1,0:T(8,128)}, f32[2048,256]{1,0:T(8,128)}, ...) | async-done | bytes 37748752 | tf_op jit(solution)/shard_map/psum | solution.py:164
  879.6 14.1 %copy.164 = f32[2048,2048]{1,0:T(8,128)} copy(f32[2048,2048]{1,0:T(8,128)} %get-tuple-element.97) | data formatting | bytes 33554432
  898.6 6.2 copy.167
  (113 shorter events, 42.6 us)
Async XLA Ops:
  7.2 84.4 %copy-start = (bf16[2048,256]{1,0:T(8,128)(2,1)S(1)}, bf16[2048,256]{1,0:T(8,128)(2,1)}, u32[]{:S(2)}) copy-start(bf16[2048,256]{1,0:T(8,128)(2,1)} %param.19) | copy-start | bytes 3145732
  10.2 81.4 %copy-start.23 = (f32[256]{0:T(256)}, f32[256]{0:T(256)S(1)}, u32[]{:S(2)}) copy-start(f32[256]{0:T(256)S(1)} %add_rsqrt_fusion) | copy-start | bytes 3076
  10.9 80.7 %copy-start.21 = (f32[2048]{0:T(1024)}, f32[2048]{0:T(1024)S(1)}, u32[]{:S(2)}) copy-start(f32[2048]{0:T(1024)S(1)} %convert_element_type.171) | copy-start | bytes 24580
  14.1 45.2 %copy-start.19 = (f32[256,64]{0,1:T(8,128)}, f32[256,64]{0,1:T(8,128)S(1)}, u32[]{:S(2)}) copy-start(f32[256,64]{0,1:T(8,128)S(1)} %get-tuple-element.88) | copy-start | bytes 196612
  14.1 12.5 %copy-start.7 = (bf16[1,256,2048]{2,1,0:T(8,128)(2,1)S(1)}, bf16[1,256,2048]{2,1,0:T(8,128)(2,1)}, u32[]{:S(2)}) copy-start(bf16[1,256,2048]{2,1,0:T(8,128)(2,1)} %param.12) | copy-start | bytes 3145732
  15.8 38.6 %all-to-all-start.1 = ((bf16[1,256,16,128]{3,1,0,2:T(8,128)(2,1)}), bf16[1,256,16,128]{3,1,0,2:T(8,128)(2,1)S(1)}, u32[]{:S(2)}, u32[]{:S(2)}) async-start(bf16[1,256,16,128]{3,1,0,2:T(8,128)(2,1)} %bitcast.202), calls=%async_computation.1 | async-start | bytes 2097152 | tf_op jit(solution)/shard_map/all_to_all | solution.py:127
  32.5 26.9 %copy-start.26 = (bf16[2048]{0:T(1024)(128)(2,1)S(1)}, bf16[2048]{0:T(1024)(128)(2,1)}, u32[]{:S(2)}) copy-start(bf16[2048]{0:T(1024)(128)(2,1)} %param.16) | copy-start | bytes 12292
  32.6 26.9 %copy-start.1 = (bf16[1,256,2048]{2,1,0:T(8,128)(2,1)S(1)}, bf16[1,256,2048]{2,1,0:T(8,128)(2,1)}, u32[]{:S(2)}) copy-start(bf16[1,256,2048]{2,1,0:T(8,128)(2,1)} %param.11) | copy-start | bytes 3145732
  54.4 1.0 copy-start.6
  55.4 31.4 %all-to-all-start.4 = ((bf16[1,256,16,128]{3,1,0,2:T(8,128)(2,1)}), bf16[1,256,16,128]{3,1,0,2:T(8,128)(2,1)S(1)}, u32[]{:S(2)}, u32[]{:S(2)}) async-start(bf16[1,256,16,128]{3,1,0,2:T(8,128)(2,1)} %copy.119), calls=%async_computation.4 | async-start | bytes 2097152 | tf_op jit(solution)/shard_map/all_to_all | solution.py:137
  59.3 7.0 copy-start.15
  67.7 23.8 %copy-start.27 = (bf16[256]{0:T(256)(128)(2,1)S(1)}, bf16[256]{0:T(256)(128)(2,1)}, u32[]{:S(2)}) copy-start(bf16[256]{0:T(256)(128)(2,1)} %param.20) | copy-start | bytes 1540
  86.8 31.0 %all-to-all-start.2 = ((bf16[1,256,16,128]{3,1,0,2:T(8,128)(2,1)}), bf16[1,256,16,128]{3,1,0,2:T(8,128)(2,1)}, u32[]{:S(2)}, u32[]{:S(2)}) async-start(bf16[1,256,16,128]{3,1,0,2:T(8,128)(2,1)} %maximum_bitcast_fusion), calls=%async_computation.2 | async-start | bytes 2097152 | tf_op jit(solution)/shard_map/all_to_all | solution.py:126
  119.0 51.9 %all-to-all-start = ((bf16[1,256,16,128]{3,1,0,2:T(8,128)(2,1)}), bf16[1,256,16,128]{3,1,0,2:T(8,128)(2,1)S(1)}, u32[]{:S(2)}, u32[]{:S(2)}) async-start(bf16[1,256,16,128]{3,1,0,2:T(8,128)(2,1)} %bitcast.201), calls=%async_computation | async-start | bytes 2097152 | tf_op jit(solution)/shard_map/all_to_all | solution.py:128
  229.3 88.2 %all-to-all-start.3 = ((bf16[16,2,16384]{2,1,0:T(2,128)(2,1)}), bf16[16,2,16384]{2,1,0:T(2,128)(2,1)}, u32[]{:S(2)}, u32[]{:S(2)}) async-start(bf16[16,2,16384]{2,1,0:T(2,128)(2,1)} %reshape.526), calls=%async_computation.3 | async-start | bytes 2097152 | tf_op jit(solution)/shard_map/all_to_all | solution.py:130
  317.5 37.6 %all-to-all-start.5 = ((bf16[16,2,16384]{2,1,0:T(2,128)(2,1)}), bf16[16,2,16384]{2,1,0:T(2,128)(2,1)S(1)}, u32[]{:S(2)}, u32[]{:S(2)}) async-start(bf16[16,2,16384]{2,1,0:T(2,128)(2,1)} %reshape.528), calls=%async_computation.5 | async-start | bytes 2097152 | tf_op jit(solution)/shard_map/all_to_all | solution.py:142
  355.0 1.0 copy-start.11
  356.0 56.0 %all-to-all-start.7 = ((f32[1,4096,1,128]{3,2,0,1:T(1,128)}), f32[1,4096,1,128]{3,2,0,1:T(1,128)}, u32[]{:S(2)}, u32[]{:S(2)}) async-start(f32[1,4096,1,128]{3,2,0,1:T(1,128)} %copy.127), calls=%async_computation.7 | async-start | bytes 4194304 | tf_op jit(solution)/shard_map/all_to_all | solution.py:145
  383.1 34.7 %copy-start.20 = (f32[256,64]{0,1:T(8,128)S(1)}, f32[256,64]{0,1:T(8,128)}, u32[]{:S(2)}) copy-start(f32[256,64]{0,1:T(8,128)} %get-tuple-element.86) | copy-start | bytes 196612
  412.0 54.2 %all-to-all-start.6 = ((f32[1,4096,1,128]{3,2,0,1:T(1,128)}), f32[1,4096,1,128]{3,2,0,1:T(1,128)}, u32[]{:S(2)}, u32[]{:S(2)}) async-start(f32[1,4096,1,128]{3,2,0,1:T(1,128)} %copy.124), calls=%async_computation.6 | async-start | bytes 4194304 | tf_op jit(solution)/shard_map/all_to_all | solution.py:144
  417.5 462.2 %all-reduce.4.cloned.1.call-start = ((), (), s32[]{:S(2)}) async-start(), calls=%async_computation.8 | async-start | bytes 75497472 | tf_op jit(solution)/shard_map/psum | solution.py:164
  423.3 1.6 copy-start.12
  430.0 0.9 copy-start.16
  431.9 1.4 copy-start.3
  431.9 2.0 copy-start.4
  435.7 9.9 %copy-start.2 = (bf16[1,256,2048]{2,1,0:T(8,128)(2,1)S(1)}, bf16[1,256,2048]{2,1,0:T(8,128)(2,1)}, u32[]{:S(2)}) copy-start(bf16[1,256,2048]{2,1,0:T(8,128)(2,1)} %param.11) | copy-start | bytes 3145732
  435.7 9.9 %copy-start.9 = (bf16[1,256,16,128]{1,3,2,0:T(8,128)(2,1)S(1)}, bf16[1,256,16,128]{1,3,2,0:T(8,128)(2,1)}, u32[]{:S(2)}) copy-start(bf16[1,256,16,128]{1,3,2,0:T(8,128)(2,1)} %copy.123) | copy-start | bytes 3145732
  435.8 9.9 %copy-start.22 = (f32[2048]{0:T(1024)S(1)}, f32[2048]{0:T(1024)}, u32[]{:S(2)}) copy-start(f32[2048]{0:T(1024)} %copy-done.21) | copy-start | bytes 24580
  435.8 9.9 %copy-start.24 = (f32[256]{0:T(256)S(1)}, f32[256]{0:T(256)}, u32[]{:S(2)}) copy-start(f32[256]{0:T(256)} %copy-done.23) | copy-start | bytes 3076
  470.1 4.3 copy-start.17
  476.4 3.5 copy-start.10
  493.8 2.3 copy-start.18
  498.5 2.3 copy-start.25
  498.5 46.1 %copy-start.8 = (bf16[1,256,2048]{2,1,0:T(8,128)(2,1)S(1)}, bf16[1,256,2048]{2,1,0:T(8,128)(2,1)}, u32[]{:S(2)}) copy-start(bf16[1,256,2048]{2,1,0:T(8,128)(2,1)} %param.12) | copy-start | bytes 3145732
  879.6 14.1 %copy-start.14 = (f32[2048,256]{1,0:T(8,128)S(1)}, f32[2048,256]{1,0:T(8,128)}, u32[]{:S(2)}) copy-start(f32[2048,256]{1,0:T(8,128)} %get-tuple-element.99) | copy-start | bytes 6291460
  879.6 19.0 %copy-start.5 = (f32[2048,2048]{1,0:T(8,128)S(1)}, f32[2048,2048]{1,0:T(8,128)}, u32[]{:S(2)}) copy-start(f32[2048,2048]{1,0:T(8,128)} %get-tuple-element.103) | copy-start | bytes 50331652
  893.8 3.1 copy-start.13
Sparse Core Ops, SparseCore 0:
  476.5 403.0 all-reduce.3
where the time goes:
time: 922 us; the launch traced here: 912 us
  waiting for transfers between devices  429 us (47%)
  matrix products  201 us (22%)
  other arithmetic  95 us (10%)
  local copies, waits for them, and re-layouts  78.4 us (9%)
  starting transfers between devices  50.6 us (5%)
  blocking collectives  43.8 us (5%)
  between operations  15 us (2%)
    psum x1, waiting for transfers between devices, device_step(): lax.psum((jnp.sum(gain_terms, axis=(0, 1)), d_w_query, jnp.sum(dq_pre, ax...  332 us
    unnamed x4, other arithmetic  51.7 us
    unnamed x70, local copies, waits for them, and re-layouts  46.8 us
    psum x1, blocking collectives, device_step(): lax.psum((jnp.sum(gain_terms, axis=(0, 1)), d_w_query, jnp.sum(dq_pre, ax...  43.8 us
    dot_general x1, matrix products, one_block(): jnp.einsum('bqkgd,bskd->bkgqs', do_block, values, preferred_element_type=...  36.9 us
    all_to_all x1, waiting for transfers between devices, device_step(): d_values = lax.all_to_all(dv_h.astype(wire_type), 'sp', 1, 2, tiled=True)  29 us
    dot_general x1, matrix products, one_block(): jnp.einsum('bqkgd,bskd->bkgqs', q_block, keys, preferred_element_type=jnp...  26.7 us
    dot_general x1, matrix products, one_block(): jnp.einsum('bkgqs,bskd->bqkgd', probs, values, preferred_element_type=jnp...  25.4 us
  transfers between devices with their start and end apart: 9, of which 6 were waited for; matrix products, arithmetic and copies ran while one was open for 29% of the time, Pallas kernels for 0%

commit v1 on v0

v1 whole, which is shorter than its diff:
```python
import functools, math
import jax
import jax.numpy as jnp
from jax import lax
from jax.experimental import pallas as pl
from jax.experimental.pallas import tpu as pltpu
from jax.sharding import PartitionSpec as P

HEAD_DIM = 128
ROPE_BASE = 1000000.0
NORM_EPS = 1e-6
MESH = pl.DeviceIdType.MESH
NSUB = 4
F32 = jnp.float32
BF16 = jnp.bfloat16
ANY = pl.BlockSpec(memory_space=pl.ANY)
VM = pl.BlockSpec(memory_space=pltpu.VMEM)


class Ring:
    def __init__(self, full, own, rows, nz, sems):
        self.full, self.own, self.rows, self.nz = full, own, rows, nz
        self.send, self.recv, self.dsend, self.drecv = sems
        self.sp = lax.axis_index('sp')
        self.dp = lax.axis_index('dp')
        self.z, self.c = self.sp // 2, self.sp % 2
        self.sub = rows // (2 * NSUB)
        self.nsend = 7 * NSUB

    def dev(self, z, c):
        return (self.dp, z * 2 + c)

    def where(self, d, j, z):
        s = j // (2 * NSUB)
        r = j % (2 * NSUB)
        half = (r // NSUB + d) % 2
        origin = (z + (self.nz - s if d == 0 else s)) % self.nz
        return pl.multiple_of((origin * 2 + self.c) * self.rows + half * (self.rows // 2) + (r % NSUB) * self.sub, self.sub)

    def ici(self, d, j, src=None):
        off = self.where(d, j, self.z)
        to = (self.z + (1 if d == 0 else self.nz - 1)) % self.nz
        return pltpu.make_async_remote_copy(
            src_ref=self.full.at[pl.ds(off, self.sub)] if src is None else src,
            dst_ref=self.full.at[pl.ds(off, self.sub)],
            send_sem=self.send.at[d, j], recv_sem=self.recv.at[d, j],
            device_id=self.dev(to, self.c), device_id_type=MESH)

    def d2d(self, d, j):
        frm = (self.z + (self.nz - 1 if d == 0 else 1)) % self.nz
        off = self.where(d, j, frm)
        return pltpu.make_async_remote_copy(
            src_ref=self.full.at[pl.ds(off, self.sub)], dst_ref=self.full.at[pl.ds(off, self.sub)],
            send_sem=self.dsend.at[d, j], recv_sem=self.drecv.at[d, j],
            device_id=self.dev(self.z, 1 - self.c), device_id_type=MESH)

    def d2d_own(self):
        off = pl.multiple_of(self.sp * self.rows, self.rows)
        return pltpu.make_async_remote_copy(
            src_ref=self.own, dst_ref=self.full.at[pl.ds(off, self.rows)],
            send_sem=self.dsend.at[2, 0], recv_sem=self.drecv.at[2, 0],
            device_id=self.dev(self.z, 1 - self.c), device_id_type=MESH)

    def start(self):
        @pl.loop(0, 2 * NSUB)
        def _(j):
            for d in range(2):
                half = (j // NSUB + d) % 2
                off = pl.multiple_of(half * (self.rows // 2) + (j % NSUB) * self.sub, self.sub)
                self.ici(d, j, self.own.at[pl.ds(off, self.sub)]).start()
        self.d2d_own().start()

    def tick(self, j):
        for d in range(2):
            self.ici(d, j).wait_recv()

            @pl.when(j + 2 * NSUB < self.nsend)
            def _():
                self.ici(d, j + 2 * NSUB).start()
            self.d2d(d, j).start()

    def finish_sends(self):
        @pl.loop(0, self.nsend)
        def _(j):
            for d in range(2):
                self.ici(d, j).wait_send()
                self.d2d(d, j).wait_send()
        self.d2d_own().wait_send()

    def wait_other(self, j):
        for d in range(2):
            self.d2d(d, j).wait_recv()


def ring_sems(nz):
    n = 7 * NSUB
    return [pltpu.SemaphoreType.DMA((2, n)), pltpu.SemaphoreType.DMA((2, n)),
            pltpu.SemaphoreType.DMA((3, n)), pltpu.SemaphoreType.DMA((3, n))]


def greet_all(n_sp):
    sp, dp = lax.axis_index('sp'), lax.axis_index('dp')
    bar = pltpu.get_barrier_semaphore()

    @pl.loop(1, n_sp)
    def _(o):
        pl.semaphore_signal(bar, inc=1, device_id=(dp, (sp + o) % n_sp), device_id_type=MESH)
    pl.semaphore_wait(bar, n_sp - 1)


def k1_kernel(n_sp, h_own, pos, wq, wk, wv, bq, bk, bv, hf, ht, qt, k_o, kt_o, v_o, vt_o, cs_o,
              pos_all, wq_v, wk_v, wv_v, hb, htb, qs, ks, kts, vs, vts, css, send, recv, dsend, drecv, psend, precv, lsem, osem):
    nz = n_sp // 2
    rows, dm = h_own.shape
    qw = wq_v.shape[1]
    sp, dp = lax.axis_index('sp'), lax.axis_index('dp')
    z, c = sp // 2, sp % 2
    heads = qw // HEAD_DIM
    half_dim = HEAD_DIM // 2
    ring = Ring(hf, h_own, rows, nz, (send, recv, dsend, drecv))
    wcopies = [pltpu.make_async_copy(wq.at[:, pl.ds(pl.multiple_of(c * qw, qw), qw)], wq_v, lsem.at[0]),
               pltpu.make_async_copy(wk.at[:, pl.ds(pl.multiple_of(c * HEAD_DIM, HEAD_DIM), HEAD_DIM)], wk_v, lsem.at[1]),
               pltpu.make_async_copy(wv.at[:, pl.ds(pl.multiple_of(c * HEAD_DIM, HEAD_DIM), HEAD_DIM)], wv_v, lsem.at[2])]
    pos_copy = pltpu.make_async_copy(pos, pos_all.at[sp], lsem.at[4])
    for w in wcopies:
        w.start()
    pos_copy.start()
    greet_all(n_sp)
    ring.start()
    own_in = pltpu.make_async_copy(h_own, hb, lsem.at[5])
    own_in.start()

    def pos_send(o):
        return pltpu.make_async_remote_copy(src_ref=pos, dst_ref=pos_all.at[sp], send_sem=psend.at[o], recv_sem=precv.at[o],
                                            device_id=(dp, (sp + o) % n_sp), device_id_type=MESH)

    @pl.loop(1, n_sp)
    def _(o):
        pos_send(o).start()
    own_in.wait()
    own_out = pltpu.make_async_copy(hb, hf.at[pl.ds(pl.multiple_of(sp * rows, rows), rows)], lsem.at[3])
    own_out.start()
    for w in wcopies:
        w.wait()
    pos_copy.wait()
    own_out.wait()

    @pl.loop(1, n_sp)
    def _(o):
        pos_send(o).wait()

    freq = jnp.exp(lax.broadcasted_iota(jnp.int32, (half_dim, 1), 0).astype(F32) * (-2.0 / HEAD_DIM * math.log(ROPE_BASE)))

    def outs(blk):
        cols = pl.ds(pl.multiple_of(blk * rows, rows), rows)
        return [pltpu.make_async_copy(htb, ht.at[:, cols], osem.at[0]),
                pltpu.make_async_copy(qs, qt.at[blk], osem.at[1]),
                pltpu.make_async_copy(ks, k_o.at[cols], osem.at[2]),
                pltpu.make_async_copy(kts, kt_o.at[:, cols], osem.at[3]),
                pltpu.make_async_copy(vs, v_o.at[cols], osem.at[4]),
                pltpu.make_async_copy(vts, vt_o.at[:, cols], osem.at[5]),
                pltpu.make_async_copy(css, cs_o.at[:, cols], osem.at[6])]

    def compute(n, blk):
        load = pltpu.make_async_copy(hf.at[pl.ds(pl.multiple_of(blk * rows, rows), rows)], hb, lsem.at[5])
        load.start()
        load.wait()
        @pl.when(n > 0)
        def _():
            for o in outs(blk):
                o.wait()
        ang = freq * pos_all[blk, 0:1, :].astype(F32)
        cos, sin = jnp.cos(ang), jnp.sin(ang)
        css[0:half_dim, :] = cos
        css[half_dim:, :] = sin
        h = hb[...]
        htb[...] = h.T

        def rope_t(t):
            a, b = t[:half_dim], t[half_dim:]
            return jnp.concatenate([a * cos - b * sin, b * cos + a * sin], axis=0)
        for g in range(heads // 2):
            cols = slice(g * 2 * HEAD_DIM, (g + 1) * 2 * HEAD_DIM)
            q = jnp.dot(h, wq_v[:, cols], preferred_element_type=F32) + bq_c(bq, c, qw, cols)
            t = q.T
            for e in range(2):
                hd = g * 2 + e
                qs[:, hd * rows:(hd + 1) * rows] = rope_t(t[e * HEAD_DIM:(e + 1) * HEAD_DIM]).astype(BF16)
        k = jnp.dot(h, wk_v[...], preferred_element_type=F32) + bk[pl.ds(c, 1), :]
        kt = rope_t(k.T)
        kts[...] = kt.astype(BF16)
        ks[...] = kt.T.astype(BF16)
        v = jnp.dot(h, wv_v[...], preferred_element_type=F32) + bv[pl.ds(c, 1), :]
        vs[...] = v.astype(BF16)
        vts[...] = v.T.astype(BF16)
        for o in outs(blk):
            o.start()

    def bq_c(bq, c, qw, cols):
        return bq[pl.ds(c, 1), cols]

    @pl.loop(0, n_sp)
    def _(n):
        m = n - 2
        s = m // 4
        b = jnp.where(s == 3, (m % 4) * 2, m % 4)
        other = jnp.where(n < 2, n, b // 2)
        left = b % 2 == 0
        dist = jnp.where(n < 2, 0, s + 1)

        @pl.when((n >= 2) & (m % 4 == 0))
        def _():
            @pl.loop(0, jnp.where(s == 3, NSUB, 2 * NSUB))
            def _(r):
                ring.tick(s * 2 * NSUB + r)

        @pl.when(n == 1)
        def _():
            ring.d2d_own().wait_recv()

        @pl.when((n >= 2) & (other == 1) & left)
        def _():
            @pl.loop(0, jnp.where(s == 3, NSUB, 2 * NSUB))
            def _(r):
                ring.wait_other(s * 2 * NSUB + r)
        zb = (z + jnp.where(left, nz - dist, dist)) % nz
        cb = jnp.where(other == 1, 1 - c, c)
        compute(n, zb * 2 + cb)
    for o in outs(0):
        o.wait()
    ring.finish_sends()


def k1(n_sp, h_own, pos8, wq, wk, wv, bq, bk, bv):
    rows, dm = h_own.shape
    seq = rows * n_sp
    nz = n_sp // 2
    qw = wq.shape[1] // 2
    heads = qw // HEAD_DIM
    sds = jax.ShapeDtypeStruct
    outs = [sds((seq, dm), BF16), sds((dm, seq), BF16), sds((n_sp, HEAD_DIM, heads * rows), BF16),
            sds((seq, HEAD_DIM), BF16), sds((HEAD_DIM, seq), BF16), sds((seq, HEAD_DIM), BF16), sds((HEAD_DIM, seq), BF16),
            sds((HEAD_DIM, seq), F32)]
    vm = pltpu.VMEM
    scratch = [vm((n_sp,) + pos8.shape, jnp.int32), vm((dm, qw), BF16), vm((dm, HEAD_DIM), BF16), vm((dm, HEAD_DIM), BF16),
               vm((rows, dm), BF16), vm((dm, rows), BF16), vm((HEAD_DIM, heads * rows), BF16),
               vm((rows, HEAD_DIM), BF16), vm((HEAD_DIM, rows), BF16), vm((rows, HEAD_DIM), BF16), vm((HEAD_DIM, rows), BF16),
               vm((HEAD_DIM, rows), F32)] + ring_sems(nz) + [
               pltpu.SemaphoreType.DMA((n_sp,)), pltpu.SemaphoreType.DMA((n_sp,)),
               pltpu.SemaphoreType.DMA((6,)), pltpu.SemaphoreType.DMA((7,))]
    return pl.pallas_call(
        functools.partial(k1_kernel, n_sp), out_shape=outs,
        in_specs=[ANY, ANY, ANY, ANY, ANY, VM, VM, VM], out_specs=[ANY] * len(outs), scratch_shapes=scratch,
        compiler_params=pltpu.CompilerParams(collective_id=0, has_side_effects=True, vmem_limit_bytes=60 * 2 ** 20),
        name='gather_project')(h_own, pos8, wq, wk, wv, bq, bk, bv)


LOG2E = math.log2(math.e)
NEG = -1e30

def split_scaled(q, scale):
    qs = q.astype(F32) * scale
    hi = qs.astype(BF16)
    lo = (qs - hi.astype(F32)).astype(BF16)
    return jnp.concatenate([hi, lo], axis=0)

def decode(n, nblk):
    one = int if isinstance(n, int) else (lambda x: x.astype(jnp.int32))
    j = sum(one(n >= i * (i + 1)) for i in range(1, nblk // 2))
    r = n - j * (j + 1)
    odd = one(r > j)
    return 2 * j + odd, r - odd * (j + 1)

def fwd_steps(nblk):
    return (nblk // 2) * (nblk // 2 + 1)

class Fwd:
    def __init__(self, nblk, rows, heads, qt, at, lse, kk, vt, qb, q2, acc, mx, cm, ls, al, rt, lsv, sb, pb, bias, ats, qsem, osem):
        self.__dict__.update(locals())
        self.bk = 2 * rows
        self.cols = [slice(g * rows, (g + 1) * rows) for g in range(heads)]
        self.halves = (range(0, heads // 2), range(heads // 2, heads))
        self.nstep = fwd_steps(nblk)

    def load_q(self, blk):
        return pltpu.make_async_copy(self.qt.at[blk], self.qb, self.qsem)

    def make_q2(self, blk):
        for g in range(self.heads):
            self.q2[blk % 2, :, self.cols[g]] = split_scaled(self.qb[:, self.cols[g]], LOG2E * HEAD_DIM ** -0.5)

    def prepare(self):
        for b in range(2):
            self.load_q(b).start()
            self.load_q(b).wait()
            self.make_q2(b)
        self.load_q(2).start()
        d = lax.broadcasted_iota(jnp.int32, (self.bk, self.rows), 0) - lax.broadcasted_iota(jnp.int32, (self.bk, self.rows), 1)
        self.bias[0] = jnp.zeros((self.bk, self.rows), F32)
        self.bias[1] = jnp.where(d <= 0, 0.0, NEG)
        self.bias[2] = jnp.where(d <= self.rows, 0.0, NEG)
        self.acc[...] = jnp.zeros_like(self.acc)
        self.pb[...] = jnp.zeros_like(self.pb)
        self.ls[...] = jnp.zeros_like(self.ls)
        self.al[...] = jnp.zeros_like(self.al)
        self.mx[...] = jnp.zeros_like(self.mx)
        self.scores(0, 0)

    def scores(self, n, part):
        blk, t = decode(n, self.nblk)
        kb = self.kk[pl.ds(pl.multiple_of(t * self.bk, self.bk), self.bk), :]
        kind = jnp.where(t == blk // 2, 1 + blk % 2, 0)
        for g in self.halves[part]:
            s = jnp.dot(kb, self.q2[blk % 2, :, self.cols[g]], preferred_element_type=F32) + self.bias[kind]
            self.sb[g] = s
            self.cm[:, self.cols[g]] = jnp.max(s.reshape(self.bk // 8, 8, self.rows), axis=0)

    def soft(self, n, part):
        blk, t = decode(n, self.nblk)
        for g in self.halves[part]:
            c = self.cols[g]
            m0 = jnp.where(t == 0, NEG, self.mx[0:1, c])
            m1 = jnp.maximum(m0, jnp.max(self.cm[:, c], axis=0, keepdims=True))
            p = jnp.exp2(self.sb[g] - m1)
            a = jnp.exp2(m0 - m1)
            self.mx[0:1, c] = m1
            self.al[0:1, c] = a
            self.ls[:, c] = self.ls[:, c] * a + jnp.sum(p.reshape(self.bk // 8, 8, self.rows), axis=0)
            self.pb[g] = p.astype(BF16)

    def values(self, n, part):
        blk, t = decode(n, self.nblk)
        vb = self.vt[:, pl.ds(pl.multiple_of(t * self.bk, self.bk), self.bk)]
        for g in self.halves[part]:
            c = self.cols[g]
            self.acc[:, c] = self.acc[:, c] * self.al[0:1, c] + jnp.dot(vb, self.pb[g], preferred_element_type=F32)

    def outs(self, blk, part):
        nh = self.heads // 2
        r = slice(part * nh * HEAD_DIM, (part + 1) * nh * HEAD_DIM)
        return pltpu.make_async_copy(self.ats.at[r], self.at.at[r, pl.ds(pl.multiple_of(blk * self.rows, self.rows), self.rows)], self.osem.at[part])

    def out_lse(self, blk):
        return pltpu.make_async_copy(self.lsv, self.lse.at[blk], self.osem.at[2])

    def finish(self, blk, part):
        @pl.when(blk > 0)
        def _():
            self.outs(blk, part).wait()
        for g in self.halves[part]:
            c = self.cols[g]
            self.ats[g * HEAD_DIM:(g + 1) * HEAD_DIM, :] = (self.acc[:, c] * self.rt[0:1, c]).astype(BF16)
        self.outs(blk, part).start()

    def end_block(self, blk):
        @pl.when(blk > 0)
        def _():
            self.out_lse(blk).wait()
        tot = jnp.sum(self.ls[...], axis=0, keepdims=True)
        self.rt[0:1, :] = 1.0 / tot
        self.lsv[0:1, :] = self.mx[0:1, :] + jnp.log2(tot)
        self.out_lse(blk).start()
        self.finish(blk, 0)

        @pl.when(blk + 2 < self.nblk)
        def _():
            self.load_q(blk + 2).wait()
            self.make_q2(blk + 2)

        @pl.when(blk + 3 < self.nblk)
        def _():
            self.load_q(blk + 3).start()

    def run(self, lo, hi, on_step=lambda n: None):
        @pl.loop(lo, hi)
        def _(n):
            on_step(n)
            self.step(n)
            blk, t = decode(n, self.nblk)

            @pl.when((t == 0) & (n > 0))
            def _():
                self.finish(blk - 1, 1)

            @pl.when(t == blk // 2)
            def _():
                self.end_block(blk)

    def drain(self):
        n, blk = self.nstep - 1, self.nblk - 1
        self.values(n, 1)
        self.finish(blk, 1)
        self.outs(blk, 0).wait()
        self.outs(blk, 1).wait()
        self.out_lse(blk).wait()

    def step(self, n):
        n1 = jnp.minimum(n + 1, self.nstep - 1)
        self.scores(n, 1)
        self.soft(n, 0)
        self.values(jnp.maximum(n - 1, 0), 1)
        self.scores(n1, 0)
        self.soft(n, 1)
        self.values(n, 0)


def fwd_scratch(nblk, rows, heads):
    vm = pltpu.VMEM
    w, seq, bk = heads * rows, nblk * rows, 2 * rows
    return [vm((seq, 2 * HEAD_DIM), BF16), vm((HEAD_DIM, seq), BF16), vm((HEAD_DIM, w), BF16), vm((2, 2 * HEAD_DIM, w), BF16), vm((HEAD_DIM, w), F32),
            vm((8, w), F32), vm((8, w), F32), vm((8, w), F32), vm((8, w), F32), vm((8, w), F32), vm((8, w), F32),
            vm((heads, bk, rows), F32), vm((heads, bk, rows), BF16), vm((3, bk, rows), F32), vm((heads * HEAD_DIM, rows), BF16),
            pltpu.SemaphoreType.DMA, pltpu.SemaphoreType.DMA((3,))]


NT = (((1,), (1,)), ((), ()))
SCALE = HEAD_DIM ** -0.5

def dot_nt(a, b):
    return lax.dot_general(a, b, NT, preferred_element_type=F32)

def decode_down(n, nq):
    one = int if isinstance(n, int) else (lambda x: x.astype(jnp.int32))
    k = sum(one(n >= nq * m - m * (m - 1) // 2) for m in range(1, nq))
    return nq - 1 - k, n - (nq * k - k * (k - 1) // 2)

def bwd_steps(nq):
    return nq * (nq + 1) // 2

class Bwd:
    def __init__(self, nq, rows, head, qt, at, lse, dqo, kk, kt, vv, dat, dlt, lsv, qb, q2, cs, dk, dv, dq, dbq, sb, dpb, pb, dsb, bias, dqs, psem, dqsem, on_chunk, on_tile):
        self.__dict__.update(locals())
        self.bk = 2 * rows
        self.nstep = bwd_steps(nq)
        self.cols = [slice(0, rows), slice(rows, 2 * rows)]

    def loads(self, i):
        slot = i % 2
        c = pl.ds(pl.multiple_of(self.head * self.rows, self.rows), self.rows)
        return [pltpu.make_async_copy(self.qt.at[2 * i + e, :, c], self.qb.at[slot, :, self.cols[e]], self.psem.at[slot, e]) for e in range(2)]

    def make_q2(self, i):
        for e in range(2):
            self.q2[i % 2, :, self.cols[e]] = split_scaled(self.qb[i % 2, :, self.cols[e]], LOG2E * SCALE)

    def prepare(self):
        nq = self.nq
        for i in (nq - 1, nq - 2):
            for cp in self.loads(i):
                cp.start()
            for cp in self.loads(i):
                cp.wait()
            self.make_q2(i)
        d = lax.broadcasted_iota(jnp.int32, (self.bk, self.rows), 0) - lax.broadcasted_iota(jnp.int32, (self.bk, self.rows), 1)
        self.bias[0] = jnp.zeros((self.bk, self.rows), F32)
        self.bias[1] = jnp.where(d <= 0, 0.0, NEG)
        self.bias[2] = jnp.where(d <= self.rows, 0.0, NEG)
        self.dk[...] = jnp.zeros_like(self.dk)
        self.dv[...] = jnp.zeros_like(self.dv)
        self.dq[...] = jnp.zeros_like(self.dq)
        self.dbq[...] = jnp.zeros_like(self.dbq)
        self.pb[...] = jnp.zeros_like(self.pb)
        self.dsb[...] = jnp.zeros_like(self.dsb)
        self.scores(0, 0)

    def keys(self, t):
        return pl.ds(pl.multiple_of(t * self.bk, self.bk), self.bk)

    def qcols(self, i, e):
        return pl.ds(pl.multiple_of(i * self.bk + e * self.rows, self.rows), self.rows)

    def scores(self, n, e):
        i, t = decode_down(n, self.nq)
        kind = jnp.where(t == i, 1 + e, 0)
        s = jnp.dot(self.kk[self.keys(t), :], self.q2[i % 2, :, self.cols[e]], preferred_element_type=F32)
        self.sb[e] = s + self.bias[kind]
        self.dpb[e] = jnp.dot(self.vv[self.keys(t), :], self.dat[:, self.qcols(i, e)], preferred_element_type=F32)

    def soft(self, n, e):
        i, t = decode_down(n, self.nq)
        c = self.qcols(i, e)
        p = jnp.exp2(self.sb[e] - self.lsv[0:1, c])
        self.pb[e] = p.astype(BF16)
        self.dsb[e] = (p * (self.dpb[e] - self.dlt[0:1, c])).astype(BF16)

    def grads(self, n, e):
        i, t = decode_down(n, self.nq)
        r = self.keys(t)
        self.dv[r, :] += dot_nt(self.pb[e], self.dat[:, self.qcols(i, e)])
        self.dk[r, :] += dot_nt(self.dsb[e], self.qb[i % 2, :, self.cols[e]])
        keep = jnp.where(t == 0, 0.0, 1.0)
        self.dq[:, self.cols[e]] = self.dq[:, self.cols[e]] * keep + jnp.dot(self.kt[:, self.keys(t)], self.dsb[e], preferred_element_type=F32)

    def step(self, n):
        n1 = jnp.minimum(n + 1, self.nstep - 1)
        self.scores(n, 1)
        self.soft(n, 0)
        self.grads(jnp.maximum(n - 1, 0), 1)
        self.scores(n1, 0)
        self.soft(n, 1)
        self.grads(n, 0)

    def finish(self, i, e):
        c = self.qcols(i, e)
        g = self.dq[:, self.cols[e]] * SCALE
        hd = HEAD_DIM // 2
        cos, sin = self.cs[0:hd, c], self.cs[hd:, c]
        a, b = g[:hd], g[hd:]
        a, b = a * cos + b * sin, b * cos - a * sin
        self.dbq[0:hd, :] += a
        self.dbq[hd:, :] += b
        blk = 2 * i + e
        self.dqs[blk, 0:hd, :] = a.astype(BF16)
        self.dqs[blk, hd:, :] = b.astype(BF16)
        self.on_chunk(blk)

    def run(self):
        @pl.loop(0, self.nstep)
        def _(n):
            self.step(n)
            i, t = decode_down(n, self.nq)

            @pl.when((t == 0) & (n > 0))
            def _():
                self.finish(i + 1, 1)
                self.on_tile(i + 1)

                @pl.when(i >= 1)
                def _():
                    for cp in self.loads(i - 1):
                        cp.start()
                    for cp in self.loads(i - 1):
                        cp.wait()
                    self.make_q2(i - 1)

            @pl.when(t == i)
            def _():
                self.finish(i, 0)
        self.grads(self.nstep - 1, 1)
        self.finish(0, 1)
        self.on_tile(0)


def bwd_scratch(nq, rows):
    vm = pltpu.VMEM
    bk, seq = 2 * rows, 2 * rows * nq
    return [vm((seq, 2 * HEAD_DIM), BF16), vm((HEAD_DIM, seq), BF16), vm((seq, HEAD_DIM), BF16), vm((HEAD_DIM, seq), BF16), vm((8, seq), F32), vm((8, seq), F32),
            vm((2, HEAD_DIM, bk), BF16), vm((2, 2 * HEAD_DIM, bk), BF16), vm((HEAD_DIM, seq), F32), vm((seq, HEAD_DIM), F32), vm((seq, HEAD_DIM), F32),
            vm((HEAD_DIM, bk), F32), vm((HEAD_DIM, rows), F32), vm((2, bk, rows), F32), vm((2, bk, rows), F32), vm((2, bk, rows), BF16), vm((2, bk, rows), BF16),
            vm((3, bk, rows), F32), vm((2 * nq, HEAD_DIM, rows), BF16), pltpu.SemaphoreType.DMA((2, 2)), pltpu.SemaphoreType.DMA((2 * nq,))]


def load_bwd(k_h, kt_h, v_h, cs_h, lse_h, head, rows, nblk, kk, kt, vv, cs, lsv, sem):
    cps = [pltpu.make_async_copy(k_h, kk.at[:, 0:HEAD_DIM], sem.at[0]), pltpu.make_async_copy(k_h, kk.at[:, HEAD_DIM:], sem.at[1]),
           pltpu.make_async_copy(kt_h, kt, sem.at[2]), pltpu.make_async_copy(v_h, vv, sem.at[3]), pltpu.make_async_copy(cs_h, cs, sem.at[4])]
    for c in cps:
        c.start()

    def lcopy(b):
        return pltpu.make_async_copy(lse_h.at[b, :, pl.ds(pl.multiple_of(head * rows, rows), rows)], lsv.at[:, pl.ds(pl.multiple_of(b * rows, rows), rows)], sem.at[5 + b])

    @pl.loop(0, nblk)
    def _(b):
        lcopy(b).start()
    for c in cps:
        c.wait()

    @pl.loop(0, nblk)
    def _(b):
        lcopy(b).wait()


def grad_att(dy_h, at_h, wo_h, head, seq, dat, dlt, wo_v, dyb, atb, sem):
    blk = dyb.shape[1]
    w = pltpu.make_async_copy(wo_h, wo_v, sem.at[2])
    w.start()

    def cp(b):
        s = b % 2
        r = pl.ds(pl.multiple_of(b * blk, blk), blk)
        return [pltpu.make_async_copy(dy_h.at[r], dyb.at[s], sem.at[s]),
                pltpu.make_async_copy(at_h.at[pl.ds(pl.multiple_of(head * HEAD_DIM, HEAD_DIM), HEAD_DIM), r], atb.at[s], sem.at[3 + s])]
    for c in cp(0):
        c.start()
    w.wait()
    nb = seq // blk

    @pl.loop(0, nb)
    def _(b):
        @pl.when(b + 1 < nb)
        def _():
            for c in cp(b + 1):
                c.start()
        for c in cp(b):
            c.wait()
        d = dot_nt(dyb[b % 2], wo_v[...]).T.astype(BF16)
        r = pl.ds(pl.multiple_of(b * blk, blk), blk)
        dat[:, r] = d
        dlt[0:1, r] = jnp.sum(d.astype(F32) * atb[b % 2].astype(F32), axis=0, keepdims=True)


def k2_kernel(n_sp, own_dy, qt, k_h, vt_h, dyf, at, lse, ao, *scr):
    *scr, send, recv, dsend, drecv, lsem, xsem = scr
    kk, vt, qb = scr[:3]
    rows = own_dy.shape[0]
    heads = qt.shape[2] // rows
    nz = n_sp // 2
    sp, dp = lax.axis_index('sp'), lax.axis_index('dp')
    ring = Ring(dyf, own_dy, rows, nz, (send, recv, dsend, drecv))
    loads = [pltpu.make_async_copy(k_h, kk.at[:, 0:HEAD_DIM], lsem.at[0]), pltpu.make_async_copy(k_h, kk.at[:, HEAD_DIM:], lsem.at[1]),
             pltpu.make_async_copy(vt_h, vt, lsem.at[2])]
    for c in loads:
        c.start()
    greet_all(n_sp)
    ring.start()
    mine = pltpu.make_async_copy(own_dy, dyf.at[pl.ds(pl.multiple_of(sp * rows, rows), rows)], lsem.at[3])
    mine.start()
    for c in loads:
        c.wait()
    f = Fwd(n_sp, rows, heads, qt, at, lse, *scr)
    f.prepare()

    def due(n):
        return jnp.clip((n - 2) * 5 // 11, 0, ring.nsend)

    def on_step(n):
        @pl.loop(due(n), due(n + 1))
        def _(j):
            ring.tick(j)
    f.run(0, f.nstep, on_step)
    f.drain()
    other = (sp // 2) * 2 + 1 - sp % 2
    give = pltpu.make_async_remote_copy(
        src_ref=at.at[:, pl.ds(pl.multiple_of(other * rows, rows), rows)], dst_ref=ao, send_sem=xsem.at[0], recv_sem=xsem.at[1],
        device_id=(dp, other), device_id_type=MESH)
    give.start()

    @pl.loop(due(f.nstep), ring.nsend)
    def _(j):
        ring.tick(j)

    @pl.loop(0, ring.nsend)
    def _(j):
        ring.wait_other(j)
    ring.d2d_own().wait_recv()
    give.wait()
    mine.wait()
    ring.finish_sends()


def k2(n_sp, own_dy, qt, k, vt):
    rows, dm = own_dy.shape
    seq = rows * n_sp
    heads = qt.shape[2] // rows
    sds = jax.ShapeDtypeStruct
    outs = [sds((seq, dm), BF16), sds((heads * HEAD_DIM, seq), BF16), sds((n_sp, 8, heads * rows), F32), sds((heads * HEAD_DIM, rows), BF16)]
    return pl.pallas_call(
        functools.partial(k2_kernel, n_sp), out_shape=outs, in_specs=[ANY] * 4, out_specs=[ANY] * 4,
        scratch_shapes=fwd_scratch(n_sp, rows, heads) + ring_sems(n_sp // 2) + [pltpu.SemaphoreType.DMA((4,)), pltpu.SemaphoreType.DMA((2,))],
        compiler_params=pltpu.CompilerParams(collective_id=1, has_side_effects=True, vmem_limit_bytes=62 * 2 ** 20),
        name='gather_attend')(own_dy, qt, k, vt)


def k3_kernel(nq, rows, qt, at, lse, k_h, kt_h, v_h, cs_h, dy_h, wo_h, dq_o, dk_o, dv_o, db_o, *scr):
    *scr, wo_v, dyb, atb, sem, sem2 = scr
    kk, kt, vv, dat, dlt, lsv, qb, q2, cs, dk, dv, dq, dbq, sb, dpb, pb, dsb, bias, dqs, psem, dqsem = scr
    sp = lax.axis_index('sp')
    head = sp // 2
    load_bwd(k_h, kt_h, v_h, cs_h, lse, head, rows, 2 * nq, kk, kt, vv, cs, lsv, sem)
    row0 = pl.multiple_of((sp % 2) * at.shape[0] + head * HEAD_DIM, HEAD_DIM)
    grad_att(dy_h, at, wo_h.at[pl.ds(row0, HEAD_DIM)], head, dy_h.shape[0], dat, dlt, wo_v, dyb, atb, sem2)

    def chunk(b):
        return pltpu.make_async_copy(dqs.at[b], dq_o.at[b], dqsem.at[b])
    b = Bwd(nq, rows, head, qt, at, lse, dq_o, *scr[:20], dqsem, lambda b: chunk(b).start(), lambda i: None)
    b.prepare()
    b.run()
    dk[...] = dk[...] * SCALE
    last = [pltpu.make_async_copy(dk, dk_o, sem.at[0]), pltpu.make_async_copy(dv, dv_o, sem.at[1]), pltpu.make_async_copy(dbq, db_o, sem.at[2])]
    for c in last:
        c.start()
    for c in last:
        c.wait()

    @pl.loop(0, 2 * nq)
    def _(b):
        chunk(b).wait()


def k3(qt, at, lse, k, kt, v, cs, dy, wo):
    nblk, seq = qt.shape[0], k.shape[0]
    rows = seq // nblk
    sds, vm = jax.ShapeDtypeStruct, pltpu.VMEM
    return pl.pallas_call(
        functools.partial(k3_kernel, nblk // 2, rows),
        out_shape=[sds((nblk, HEAD_DIM, rows), BF16), sds((seq, HEAD_DIM), F32), sds((seq, HEAD_DIM), F32), sds((HEAD_DIM, rows), F32)],
        in_specs=[ANY] * 9, out_specs=[ANY] * 4,
        scratch_shapes=bwd_scratch(nblk // 2, rows) + [vm((HEAD_DIM, dy.shape[1]), BF16), vm((2, 512, dy.shape[1]), BF16), vm((2, HEAD_DIM, 512), BF16),
                                                       pltpu.SemaphoreType.DMA((5 + nblk,)), pltpu.SemaphoreType.DMA((5,))],
        compiler_params=pltpu.CompilerParams(vmem_limit_bytes=62 * 2 ** 20), name='attend_back')(qt, at, lse, k, kt, v, cs, dy, wo)


def norm_forward(hidden, norm_gain):
    hidden_f = hidden.astype(F32)
    inv_rms = lax.rsqrt(jnp.mean(hidden_f * hidden_f, axis=-1, keepdims=True) + NORM_EPS)
    unit = hidden_f * inv_rms
    return (unit * norm_gain.astype(F32)).astype(BF16), unit, inv_rms


def norm_backward(d_normed, unit, inv_rms, norm_gain):
    d_unit = d_normed * norm_gain.astype(F32)
    d_input = inv_rms * (d_unit - unit * jnp.mean(d_unit * unit, axis=-1, keepdims=True))
    return d_input, d_normed * unit


def mm(spec, a, b):
    return jnp.einsum(spec, a, b, preferred_element_type=F32)


def solution(mesh):
    n_sp = mesh.shape['sp']
    planes = [[z * 2 + c for z in range(n_sp // 2)] for c in range(2)]

    def step(hidden, d_out, positions, norm_gain, w_query, b_query, w_key, b_key, w_value, b_value, w_out):
        x, dy = hidden[0], d_out[0]
        rows, dm = x.shape
        seq = rows * n_sp
        heads = w_query.shape[1] // HEAD_DIM
        nz = n_sp // 2
        sp = lax.axis_index('sp')
        h, unit, inv_rms = norm_forward(x, norm_gain)
        pos8 = jnp.broadcast_to(positions, (8, rows))
        two = lambda b: b.astype(F32).reshape(2, -1)
        hf, ht, qt, k, kt, v, vt, cs = k1(n_sp, h, pos8, w_query, w_key, w_value, two(b_query), two(b_key), two(b_value))
        dyf, at, lse, ao = k2(n_sp, dy, qt, k, vt)
        dq, dk, dv, dbq = k3(qt, at, lse, k, kt, v, cs, dyf, w_out)

        am = lax.dynamic_slice_in_dim(at, sp * rows, rows, axis=1)
        c = sp % 2
        a_all = jnp.where(c == 0, jnp.concatenate([am, ao]), jnp.concatenate([ao, am]))
        y = (x.astype(F32) + mm('ep,ed->pd', a_all, w_out)).astype(BF16)
        dw_o = mm('es,sd->ed', at, dyf)
        dw_out = lax.psum(lax.dynamic_update_slice(jnp.zeros((dm, dm), F32), jnp.where(sp // 2 == 0, dw_o, 0.0), (c * dw_o.shape[0], 0)), 'sp')

        dq_all = lax.all_gather(dq, 'sp', axis=0)
        hb = hf.reshape(n_sp, rows, dm)
        dw_q = mm('bpd,vbep->vde', hb, dq_all)
        dw_q = dw_q.reshape(nz, 2, dm, HEAD_DIM).transpose(2, 1, 0, 3).reshape(dm, heads * HEAD_DIM)
        kv = lax.psum(jnp.concatenate([dk, dv], axis=1), 'sp', axis_index_groups=planes)
        kv = lax.all_gather(kv, 'sp', axis=0, axis_index_groups=[[2 * z, 2 * z + 1] for z in range(nz)])
        dkr, dvr = kv[:, :, :HEAD_DIM], kv[:, :, HEAD_DIM:]
        hd = HEAD_DIM // 2
        cos, sin = cs[:hd].T, cs[hd:].T
        a, b = dkr[..., :hd], dkr[..., hd:]
        dkp = jnp.concatenate([a * cos + b * sin, b * cos - a * sin], axis=-1)
        dk_bf, dv_bf = dkp.astype(BF16), dvr.astype(BF16)
        dw_k = mm('sd,gse->dge', hf, dk_bf).reshape(dm, -1)
        dw_v = mm('sd,gse->dge', hf, dv_bf).reshape(dm, -1)
        dqm = lax.dynamic_index_in_dim(dq_all, sp, axis=1, keepdims=False).reshape(nz, 2, HEAD_DIM, rows).transpose(1, 0, 2, 3).reshape(-1, rows)
        own = lambda t: lax.dynamic_slice_in_dim(t, sp * rows, rows, axis=1)
        d_normed = mm('ep,de->pd', dqm, w_query) + mm('gpe,dge->pd', own(dk_bf), w_key.reshape(dm, 2, -1)) + mm('gpe,dge->pd', own(dv_bf), w_value.reshape(dm, 2, -1))
        d_input, gain_terms = norm_backward(d_normed, unit, inv_rms, norm_gain)
        dx = (dy.astype(F32) + d_input).astype(BF16)
        db_q = lax.all_gather(jnp.sum(dbq, axis=1), 'sp', axis=0).reshape(nz, 2, HEAD_DIM).transpose(1, 0, 2).reshape(-1)
        d_gain = lax.psum(jnp.sum(gain_terms, axis=0), 'sp')
        return (y[None], dx[None], d_gain, dw_q, db_q, dw_k, jnp.sum(dkp, axis=1).reshape(-1), dw_v, jnp.sum(dvr, axis=1).reshape(-1), dw_out)

    seq_spec = P('dp', 'sp', None)
    in_specs = (seq_spec, seq_spec, P('dp', 'sp')) + (P(),) * 8
    out_specs = (seq_spec, seq_spec, P('dp'), P('dp', None), P('dp'), P('dp', None), P('dp'), P('dp', None), P('dp'), P('dp', None))
    return jax.shard_map(step, mesh=mesh, in_specs=in_specs, out_specs=out_specs, check_vma=False)
```

time: 922 us -> 764 us (0.83)
  Pallas kernels: 0 us -> 300 us
  waiting for transfers between devices: 429 us -> 180 us
  matrix products: 201 us -> 114 us
  other arithmetic: 95 us -> 24.7 us
  starting transfers between devices: 50.6 us -> 0.71 us
    pallas_call x0 -> x3, Pallas kernels: none -> 300 us  [the longest x1 127 us: k2(): pl.pallas_call(functools.partial(k2_kernel, n_sp), out_shape=outs, in_spe...]
    psum x1 -> x2, waiting for transfers between devices: 332 us -> 180 us  [the longest x1 102 us: step(): lax.psum(jnp.concatenate([dk, dv], axis=1), 'sp', axis_index_groups=planes)]
    dot_general x18 -> x6, matrix products: 201 us -> 85.4 us  [mm(): return jnp.einsum(spec, a, b, preferred_element_type=F32)]
    all_to_all x8 -> x0, waiting for transfers between devices: 96.8 us -> none  [the longest x1 29 us: device_step(): d_values = lax.all_to_all(dv_h.astype(wire_type), 'sp', 1, 2, tiled=True)]
    unnamed x4 -> x0, other arithmetic: 51.7 us -> none
    all_to_all x8 -> x0, starting transfers between devices: 50.3 us -> none  [the longest x1 10.7 us: device_step(): keys_h = lax.all_to_all(keys, 'sp', 2, 1, tiled=True)]
    unnamed x0 -> x2, matrix products: none -> 29 us
    reduce_sum x6 -> x3, other arithmetic: 29.2 us -> 5.13 us  [the longest x1 3.3 us: step(): jnp.sum(dvr, axis=1).reshape(-1)]
  transfers between devices with their start and end apart: 9 -> 4, of which waited for: 6 -> 2; matrix products, arithmetic and copies ran while one was open for 29% -> 25% of each run, Pallas kernels for 0% -> 0%
where the time goes in v1:
time: 764 us; the launch traced here: 753 us
  Pallas kernels  300 us (39%)
  waiting for transfers between devices  180 us (24%)
  matrix products  114 us (15%)
  local copies, waits for them, and re-layouts  77.8 us (10%)
  blocking collectives  40.8 us (5%)
  other arithmetic  24.7 us (3%)
  between operations  14.5 us (2%)
    pallas_call x1, Pallas kernels, k2(): pl.pallas_call(functools.partial(k2_kernel, n_sp), out_shape=outs, in_spe...  127 us
    pallas_call x1, Pallas kernels, k1(): pl.pallas_call(functools.partial(k1_kernel, n_sp), out_shape=outs, in_spe...  117 us
    psum x1, waiting for transfers between devices, step(): lax.psum(jnp.concatenate([dk, dv], axis=1), 'sp', axis_index_groups=planes)  102 us
    dot_general x6, matrix products, mm(): return jnp.einsum(spec, a, b, preferred_element_type=F32)  85.4 us
    psum x1, waiting for transfers between devices, step(): lax.psum(lax.dynamic_update_slice(jnp.zeros((dm, dm), F32), jnp.where(sp...  78 us
    pallas_call x1, Pallas kernels, k3(): pl.pallas_call(functools.partial(k3_kernel, nblk // 2, rows), out_shape=[...  55.7 us
    unnamed x20, local copies, waits for them, and re-layouts  29.3 us
    unnamed x2, matrix products  29 us
  transfers between devices with their start and end apart: 4, of which 2 were waited for; matrix products, arithmetic and copies ran while one was open for 25% of the time, Pallas kernels for 0%

profile of v1, /device:TPU:21, one launch (start us, length us, event | category | flops | bytes accessed | tf_op | source)
XLA Modules:
  0.0 753.1 jit_solution(11190827923241553037)
XLA Ops:
  7.2 0.1 all-reduce.3.cloned.1.call-start
  7.3 1.5 fusion.15
  8.8 0.7 convert_element_type.34
  9.5 1.3 reshape.113.bq
  10.8 1.2 bitcast_convert_fusion
  12.0 2.5 fusion.8.h_own
  14.5 1.3 broadcast_in_dim.15.pos
  15.8 116.8 %gather_project.1 = (bf16[4096,2048]{1,0:T(8,128)(2,1)}, bf16[2048,4096]{1,0:T(8,128)(2,1)}, bf16[16,128,2048]{2,1,0:T(8,128)(2,1)}, bf16[4096,128]{1,0:T(8,128)...) custom-call(bf16[256,2048]{1,0:T(8,128)(2,1)} %fusion.8.h_own, ...), custom_call_target="tpu_custom_call" | custom-call | tf_op jit(solution)/shard_map/gather_project/pallas_call | solution.py:251
  132.6 127.4 %gather_attend.1 = (bf16[4096,2048]{1,0:T(8,128)(2,1)}, bf16[1024,4096]{1,0:T(8,128)(2,1)}, f32[16,8,2048]{2,1,0:T(8,128)}, bf16[1024,256]{1,0:T(8,128)(2,1)}) custom-call(bf16[256,2048]{1,0:T(8,128)(2,1)} %bitcast.108, bf16[16,128,2048]{2,1,0:T(8,128)(2,1)} %get-tuple-element.25.qt, bf16[4096,128]{1,0:T(8,128)(2,1)} %get-tuple-element.26.k_h, ...), custom_call_target="tpu_custom_call" | custom-call | tf_op jit(solution)/shard_map/gather_attend/pallas_call | solution.py:657
  260.0 55.7 %attend_back.1 = (bf16[16,128,256]{2,1,0:T(8,128)(2,1)}, f32[4096,128]{1,0:T(8,128)}, f32[4096,128]{1,0:T(8,128)}, f32[128,256]{1,0:T(8,128)}) custom-call(bf16[16,128,2048]{2,1,0:T(8,128)(2,1)} %get-tuple-element.25.qt, bf16[1024,4096]{1,0:T(8,128)(2,1)} %get-tuple-element.28.at, f32[16,8,2048]{2,1,0:T(8,128)} %get-tuple-element.30.lse, ...), custom_call_target="tpu_custom_call" | custom-call | tf_op jit(solution)/shard_map/attend_back/pallas_call | solution.py:694
  315.7 4.5 maximum_bitcast_fusion
  320.2 0.1 all-gather.6.cloned.1.call-start
  320.3 101.5 %all-reduce.3.cloned.1.call-done = f32[1,4096,256]{2,1,0:T(8,128)} async-done(((f32[1,4096,256]{2,1,0:T(8,128)}), f32[1,4096,256]{2,1,0:T(8,128)}) %all-reduce.3.cloned.1.call-update) | async-done | bytes 4194320 | tf_op jit(solution)/shard_map/psum | solution.py:749
  421.9 0.1 all-gather.8.cloned.1.call-start
  422.0 0.7 all-gather.8.cloned.1.call-update
  422.7 0.5 all-reduce.5.cloned.1.call-start
  423.3 7.8 %broadcast_in_dim.32 = f32[2048,2048]{1,0:T(8,128)} broadcast(f32[]{:T(128)} %constant.42.clone.1), dimensions={} | broadcast | bytes 16777220 | tf_op jit(solution)/shard_map/broadcast_in_dim | solution.py:743
  431.1 24.1 %select_dynamic-update-slice_fusion = f32[2048,2048]{1,0:T(8,128)} fusion(f32[2048,2048]{1,0:T(8,128)} %broadcast_in_dim.32, s32[]{:T(128)S(6)} %select_n.47, bf16[1024,4096]{1,0:T(8,128)(2,1)} %get-tuple-element.28.at, bf16[4096,2048]{1,0:T(8,128)(2,1)} %get-tuple-element.34.dy_h, pred[]{:T(512)S(6)} %eq.9), kind=kOutput, calls=%fused_computation.1 | convolution fusion | flops 17181966336 | bytes 33554436 | tf_op jit(solution)/shard_map/es,sd->ed/dot_general | solution.py:717
  455.3 1.5 copy-done.1
  456.8 1.5 slice_bitcast_fusion.1
  458.3 1.9 copy.62
  460.2 3.2 copy.63
  463.3 0.1 reduce_sum.57
  463.4 16.5 %all-gather.2 = f32[16,1,128]{2,1,0:T(1,128)S(1)} all-gather(f32[1,1,128]{2,1,0:T(1,128)S(1)} %bitcast.116), channel_id=3, replica_groups=mesh['dp'=4,'sp'=16] {'sp'}, dimensions={0}, use_global_device_ids=true | all-gather | bytes 8704 | tf_op jit(solution)/shard_map/all_gather | solution.py:764
  479.9 0.6 copy.89
  480.5 1.1 constant_dynamic-slice_fusion.1
  481.6 7.1 fusion.7
  488.7 4.7 multiply_add_fusion
  493.4 1.7 fusion.16
  495.1 0.9 fusion.17
  496.0 3.8 slice.34
  499.8 4.1 copy.69
  503.9 3.1 convolution_bitcast_fusion
  507.0 2.9 copy.68
  509.8 14.4 %fusion.36 = f32[2048,256]{1,0:T(8,128)} fusion(bf16[4096,256]{0,1:T(8,128)(2,1)} %bitcast.110, bf16[4096,2048]{1,0:T(8,128)(2,1)} %get-tuple-element.38), kind=kOutput, calls=%fused_computation.59 | convolution fusion | flops 4294967296 | bytes 20971520
  524.2 3.3 slice_reduce_fusion
  527.5 14.6 %fusion.37 = f32[2048,256]{1,0:T(8,128)} fusion(bf16[4096,256]{0,1:T(8,128)(2,1)} %bitcast.109, bf16[4096,2048]{1,0:T(8,128)(2,1)} %get-tuple-element.38), kind=kOutput, calls=%fused_computation.60 | convolution fusion | flops 4294967296 | bytes 20971520
  542.2 43.1 %fusion.35 = f32[16,128,2048,1]{2,1,3,0:T(8,128)} fusion(bf16[16,16,128,256]{3,2,1,0:T(8,128)(2,1)} %bitcast.112, bf16[16,256,2048,1]{2,1,0,3:T(8,128)(2,1)} %bitcast.120), kind=kOutput, calls=%fused_computation.58 | convolution fusion | flops 34359738368 | bytes 50331648 | tf_op jit(solution)/shard_map/bpd,vbep->vde/dot_general | solution.py:717
  585.2 17.8 %copy.66 = f32[2048,2,8,128]{3,2,1,0:T(8,128)} copy(f32[2048,2,8,128]{0,3,1,2:T(8,128)} %bitcast.106) | data formatting | bytes 33554432 | tf_op jit(solution)/shard_map/transpose | solution.py:748
  603.0 15.9 %copy.88 = f32[256,8,16,128]{3,1,2,0:T(8,128)} copy(f32[256,8,16,128]{3,2,1,0:T(8,128)} %bitcast.104) | data formatting | bytes 33554432
  618.9 1.3 constant_dynamic-slice_fusion
  620.3 0.1 copy.61
  620.4 5.9 fusion.34
  626.3 2.2 fusion.14
  628.5 24.3 %psum.22 = f32[2048]{0:T(1024)} all-reduce(f32[2048]{0:T(1024)S(1)} %get-tuple-element.90), channel_id=1, replica_groups=mesh['dp'=4,'sp'=16] {'sp'}, use_global_device_ids=true, to_apply=%region_4.5 | all-reduce | flops 2048 | bytes 16384 | tf_op jit(solution)/shard_map/psum | solution.py:765
  652.8 3.5 fusion.18
  656.3 78.0 %all-reduce.5.cloned.1.call-done = f32[2048,2048]{1,0:T(8,128)} async-done(((f32[2048,2048]{1,0:T(8,128)}), f32[2048,2048]{1,0:T(8,128)}) %all-reduce.5.cloned.1.call-update) | async-done | bytes 16777232 | tf_op jit(solution)/shard_map/psum | solution.py:743
  734.3 11.8 %copy.93 = f32[2048,2048]{1,0:T(8,128)} copy(f32[2048,2048]{1,0:T(8,128)} %all-reduce.5.cloned.1.call-done) | data formatting | bytes 33554432
  (24 shorter events, 0.2 us)
Async XLA Ops:
  7.2 414.7 %all-reduce.3.cloned.1.call-start = ((), (), s32[]{:S(2)}) async-start(), calls=%async_computation | async-start | bytes 8388608 | tf_op jit(solution)/shard_map/psum | solution.py:749
  8.8 123.8 %copy-start.7 = (f32[256]{0:T(256)}, f32[256]{0:T(256)S(1)}, u32[]{:S(2)}) copy-start(f32[256]{0:T(256)S(1)} %add_rsqrt_fusion) | copy-start | bytes 3076
  9.5 123.1 %copy-start.4 = (f32[2048]{0:T(1024)}, f32[2048]{0:T(1024)S(1)}, u32[]{:S(2)}) copy-start(f32[2048]{0:T(1024)S(1)} %convert_element_type.34) | copy-start | bytes 24580
  320.2 168.5 %all-gather.6.cloned.1.call-start = ((), (), s32[]{:S(2)}) async-start(), calls=%async_computation.1 | async-start | bytes 12582912 | tf_op jit(solution)/shard_map/all_gather | solution.py:750
  421.9 120.2 %all-gather.8.cloned.1.call-start = ((), (), s32[]{:S(2)}) async-start(), calls=%async_computation.3 | async-start | bytes 17825792 | tf_op jit(solution)/shard_map/all_gather | solution.py:745
  422.7 311.6 %all-reduce.5.cloned.1.call-start = ((), (), s32[]{:S(2)}) async-start(), calls=%async_computation.2 | async-start | bytes 33554432 | tf_op jit(solution)/shard_map/psum | solution.py:743
  455.2 1.6 copy-start.1
  458.2 5.1 copy-start.6
  458.2 23.4 %copy-start = (bf16[1,256,2048]{2,1,0:T(8,128)(2,1)S(1)}, bf16[1,256,2048]{2,1,0:T(8,128)(2,1)}, u32[]{:S(2)}) copy-start(bf16[1,256,2048]{2,1,0:T(8,128)(2,1)} %param.11) | copy-start | bytes 3145732
  620.3 6.0 copy-start.2
  620.3 6.0 copy-start.3
  620.4 6.0 copy-start.5
  620.4 6.0 copy-start.8
Sparse Core Ops, SparseCore 0:
  320.4 101.4 all-reduce.2
  423.4 22.4 all-gather.5
  448.1 93.1 all-gather.7
  543.6 190.6 all-reduce.4

commit v2 on v1

v2 whole, which is shorter than its diff:
```python
import functools, math
import jax
import jax.numpy as jnp
from jax import lax
from jax.experimental import pallas as pl
from jax.experimental.pallas import tpu as pltpu
from jax.sharding import PartitionSpec as P

HEAD_DIM = 128
ROPE_BASE = 1000000.0
NORM_EPS = 1e-6
MESH = pl.DeviceIdType.MESH
PAIR = 2
TOP = slice(0, 1)
KEYS = 0
YES = True
MIB = 1 << 20
NSUB = PAIR
F32 = jnp.float32
BF16 = jnp.bfloat16
ANY = pl.BlockSpec(memory_space=pl.ANY)
VM = pl.BlockSpec(memory_space=pltpu.VMEM)


def span(i, n):
    return slice(i * n, (i + 1) * n)


def turns(n):
    return pl.loop(0, n)


class Ring:
    def __init__(self, full, own, rows, nz, sems):
        self.full, self.own, self.rows, self.nz = full, own, rows, nz
        self.send, self.recv, self.drecv = sems
        self.sp = lax.axis_index('sp')
        self.dp = lax.axis_index('dp')
        self.z, self.c = self.sp // PAIR, self.sp % PAIR
        self.sub = rows // (PAIR * NSUB)
        self.nsend = 7 * NSUB

    def dev(self, z, c):
        return (self.dp, z * PAIR + c)

    def where(self, d, j, z):
        s = j // (PAIR * NSUB)
        r = j % (PAIR * NSUB)
        half = (r // NSUB + d) % PAIR
        origin = (z + (self.nz - s if d == 0 else s)) % self.nz
        return pl.multiple_of((origin * PAIR + self.c) * self.rows + half * (self.rows // PAIR) + (r % NSUB) * self.sub, self.sub)

    def ici(self, d, j, src=None):
        off = self.where(d, j, self.z)
        to = (self.z + (1 if d == 0 else self.nz - 1)) % self.nz
        return pltpu.make_async_remote_copy(
            src_ref=self.full.at[pl.ds(off, self.sub)] if src is None else src,
            dst_ref=self.full.at[pl.ds(off, self.sub)],
            send_sem=self.send.at[d], recv_sem=self.recv.at[d, j],
            device_id=self.dev(to, self.c), device_id_type=MESH)

    def d2d(self, d, j):
        frm = (self.z + (self.nz - 1 if d == 0 else 1)) % self.nz
        off = self.where(d, j, frm)
        return pltpu.make_async_remote_copy(
            src_ref=self.full.at[pl.ds(off, self.sub)], dst_ref=self.full.at[pl.ds(off, self.sub)],
            send_sem=self.send.at[PAIR], recv_sem=self.drecv.at[j // (PAIR * NSUB)],
            device_id=self.dev(self.z, 1 - self.c), device_id_type=MESH)

    def d2d_own(self):
        off = pl.multiple_of(self.sp * self.rows, self.rows)
        return pltpu.make_async_remote_copy(
            src_ref=self.own, dst_ref=self.full.at[pl.ds(off, self.rows)],
            send_sem=self.send.at[3], recv_sem=self.drecv.at[4],
            device_id=self.dev(self.z, 1 - self.c), device_id_type=MESH)

    def start(self):
        @turns(PAIR * NSUB)
        def _(j):
            for d in range(PAIR):
                half = (j // NSUB + d) % PAIR
                off = pl.multiple_of(half * (self.rows // PAIR) + (j % NSUB) * self.sub, self.sub)
                self.ici(d, j, self.own.at[pl.ds(off, self.sub)]).start()
        self.d2d_own().start()

    def tick(self, j):
        for d in range(PAIR):
            self.ici(d, j).wait_recv()

            @pl.when(j + PAIR * NSUB < self.nsend)
            def _():
                self.ici(d, j + PAIR * NSUB).start()
            self.d2d(d, j).start()

    def total(self, rows, sem):
        ref = self.full.at[pl.ds(0, rows)]
        pltpu.make_async_copy(ref, ref, sem).wait()

    def finish_sends(self):
        each = self.nsend * self.sub
        self.total(each, self.send.at[0])
        self.total(each, self.send.at[1])
        self.total(PAIR * each, self.send.at[PAIR])
        self.d2d_own().wait_send()

    def wait_other(self, s):
        self.total(self.rows if s == 3 else PAIR * self.rows, self.drecv.at[s])


def ring_sems(nz):
    return [pltpu.SemaphoreType.DMA((4,)), pltpu.SemaphoreType.DMA((PAIR, 7 * NSUB)), pltpu.SemaphoreType.DMA((5,))]


def greet_all(n_sp):
    sp, dp = lax.axis_index('sp'), lax.axis_index('dp')
    bar = pltpu.get_barrier_semaphore()

    @pl.loop(1, n_sp)
    def _(o):
        pl.semaphore_signal(bar, inc=1, device_id=(dp, (sp + o) % n_sp), device_id_type=MESH)
    pl.semaphore_wait(bar, n_sp - 1)


def k1_kernel(n_sp, x_h, pos, par, wq, wk, wv, hf, ht, qt, k_o, kt_o, v_o, vt_o, cs_o,
              pos_all, wq_v, wk_v, wv_v, hb, htb, qs, ks, kts, vs, vts, css, send, recv, drecv, psend, precv, lsem, wsem, osem):
    nz = n_sp // PAIR
    rows, dm = x_h.shape
    qw = wq_v.shape[1]
    sp, dp = lax.axis_index('sp'), lax.axis_index('dp')
    z, c = sp // PAIR, sp % PAIR
    far = 1 - c
    heads = qw // HEAD_DIM
    half_dim = HEAD_DIM // PAIR
    ng = dm // HEAD_DIM
    mine = pl.ds(pl.multiple_of(sp * rows, rows), rows)
    ring = Ring(hf, hf.at[mine], rows, nz, (send, recv, drecv))
    x_in = pltpu.make_async_copy(x_h, hb, lsem.at[0])
    x_in.start()
    pos_copy = pltpu.make_async_copy(pos, pos_all.at[sp], lsem.at[1])
    pos_copy.start()

    def head_of(g):
        return (z + g) % heads

    wcopies = [pltpu.make_async_copy(wq.at[:, pl.ds(pl.multiple_of(c * qw + head_of(g) * HEAD_DIM, HEAD_DIM), HEAD_DIM)],
                                     wq_v.at[:, span(g, HEAD_DIM)], wsem.at[g]) for g in range(heads)]
    cols = pl.ds(pl.multiple_of(c * HEAD_DIM, HEAD_DIM), HEAD_DIM)
    wcopies += [pltpu.make_async_copy(wk.at[:, cols], wk_v, lsem.at[PAIR]), pltpu.make_async_copy(wv.at[:, cols], wv_v, lsem.at[3])]
    for w in wcopies:
        w.start()
    x_in.wait()
    gain = jnp.concatenate([par[g:g + 1, :] for g in range(ng)], axis=1)
    nr = 16

    @turns(rows // nr)
    def _(i):
        rr = pl.ds(pl.multiple_of(i * nr, nr), nr)
        xf = hb[rr, :].astype(F32)
        inv = lax.rsqrt(jnp.mean(xf * xf, axis=-1, keepdims=YES) + NORM_EPS)
        hb[rr, :] = (xf * inv * gain).astype(BF16)
    own_out = pltpu.make_async_copy(hb, hf.at[mine], lsem.at[0])
    own_out.start()
    greet_all(n_sp)

    def pos_send(o):
        return pltpu.make_async_remote_copy(src_ref=pos, dst_ref=pos_all.at[sp], send_sem=psend.at[0], recv_sem=precv.at[0],
                                            device_id=(dp, (sp + o) % n_sp), device_id_type=MESH)

    @pl.loop(1, n_sp)
    def _(o):
        pos_send(o).start()
    own_out.wait()
    ring.start()
    for w in wcopies:
        w.wait()
    pos_copy.wait()
    others = pos_all.at[pl.ds(0, n_sp - 1)]
    pltpu.make_async_copy(others, others, psend.at[0]).wait()
    pltpu.make_async_copy(others, others, precv.at[0]).wait()

    freq = jnp.exp(lax.broadcasted_iota(jnp.int32, (half_dim, 1), 0).astype(F32) * (-2.0 / HEAD_DIM * math.log(ROPE_BASE)))

    def outs(blk):
        cols = pl.ds(pl.multiple_of(blk * rows, rows), rows)
        return [pltpu.make_async_copy(htb, ht.at[:, cols], osem.at[0]),
                pltpu.make_async_copy(qs, qt.at[blk], osem.at[1]),
                pltpu.make_async_copy(ks, k_o.at[cols], osem.at[PAIR]),
                pltpu.make_async_copy(kts, kt_o.at[:, cols], osem.at[3]),
                pltpu.make_async_copy(vs, v_o.at[cols], osem.at[4]),
                pltpu.make_async_copy(vts, vt_o.at[:, cols], osem.at[5]),
                pltpu.make_async_copy(css, cs_o.at[:, cols], osem.at[6])]

    def compute(n, blk):
        load = pltpu.make_async_copy(hf.at[pl.ds(pl.multiple_of(blk * rows, rows), rows)], hb, lsem.at[0])
        load.start()
        load.wait()
        @pl.when(n > 0)
        def _():
            for o in outs(blk):
                o.wait()
        ang = freq * pos_all[blk].astype(F32)
        cos, sin = jnp.cos(ang), jnp.sin(ang)
        css[0:half_dim, :] = cos
        css[half_dim:, :] = sin
        h = hb[...]
        htb[...] = h.T

        def rope_t(t):
            a, b = t[:half_dim], t[half_dim:]
            return jnp.concatenate([a * cos - b * sin, b * cos + a * sin], axis=KEYS)
        for g in range(heads // PAIR):
            cols = slice(g * PAIR * HEAD_DIM, (g + 1) * PAIR * HEAD_DIM)
            bias = jnp.concatenate([par[pl.ds(ng + c * heads + head_of(g * PAIR + e), 1), :] for e in range(PAIR)], axis=1)
            q = jnp.dot(h, wq_v[:, cols], preferred_element_type=F32) + bias
            t = q.T
            for e in range(PAIR):
                hd = g * PAIR + e
                qs[:, span(hd, rows)] = rope_t(t[span(e, HEAD_DIM)]).astype(BF16)
        k = jnp.dot(h, wk_v[...], preferred_element_type=F32) + par[pl.ds(PAIR * ng + c, 1), :]
        kt = rope_t(k.T)
        kts[...] = kt.astype(BF16)
        ks[...] = kt.T.astype(BF16)
        v = jnp.dot(h, wv_v[...], preferred_element_type=F32) + par[pl.ds(PAIR * ng + PAIR + c, 1), :]
        vs[...] = v.astype(BF16)
        vts[...] = v.T.astype(BF16)
        for o in outs(blk):
            o.start()

    @turns(n_sp)
    def _(n):
        m = n - PAIR
        s = m // 4
        b = jnp.where(s == 3, (m % 4) * PAIR, m % 4)
        other = jnp.where(n < PAIR, n, b // PAIR)
        left = b % PAIR == 0
        dist = jnp.where(n < PAIR, 0, s + 1)

        @pl.when((n >= PAIR) & (m % 4 == 0))
        def _():
            @turns(jnp.where(s == 3, NSUB, PAIR * NSUB))
            def _(r):
                ring.tick(s * PAIR * NSUB + r)

        @pl.when(n == 1)
        def _():
            ring.d2d_own().wait_recv()

        for h in range(4):
            @pl.when((n >= PAIR) & (other == 1) & left & (s == h))
            def _():
                ring.wait_other(h)
        zb = (z + jnp.where(left, nz - dist, dist)) % nz
        cb = jnp.where(other == 1, 1 - c, c)
        compute(n, zb * PAIR + cb)
    for o in outs(0):
        o.wait()
    ring.finish_sends()


def k1(n_sp, x, pos, par, wq, wk, wv):
    rows, dm = x.shape
    seq = rows * n_sp
    nz = n_sp // PAIR
    qw = wq.shape[1] // PAIR
    heads = qw // HEAD_DIM
    sds = jax.ShapeDtypeStruct
    outs = [sds((seq, dm), BF16), sds((dm, seq), BF16), sds((n_sp, HEAD_DIM, heads * rows), BF16),
            sds((seq, HEAD_DIM), BF16), sds((HEAD_DIM, seq), BF16), sds((seq, HEAD_DIM), BF16), sds((HEAD_DIM, seq), BF16),
            sds((HEAD_DIM, seq), F32)]
    vm, dma = pltpu.VMEM, pltpu.SemaphoreType.DMA
    scratch = [vm((n_sp,) + pos.shape, jnp.int32), vm((dm, qw), BF16), vm((dm, HEAD_DIM), BF16), vm((dm, HEAD_DIM), BF16),
               vm((rows, dm), BF16), vm((dm, rows), BF16), vm((HEAD_DIM, heads * rows), BF16),
               vm((rows, HEAD_DIM), BF16), vm((HEAD_DIM, rows), BF16), vm((rows, HEAD_DIM), BF16), vm((HEAD_DIM, rows), BF16),
               vm((HEAD_DIM, rows), F32)] + ring_sems(nz) + [dma((1,)), dma((1,)), dma((4,)), dma((heads,)), dma((7,))]
    return pl.pallas_call(
        functools.partial(k1_kernel, n_sp), out_shape=outs,
        in_specs=[ANY, ANY, VM, ANY, ANY, ANY], out_specs=[ANY] * len(outs), scratch_shapes=scratch,
        compiler_params=pltpu.CompilerParams(collective_id=0, has_side_effects=YES, vmem_limit_bytes=60 * MIB),
        name='gather_project')(x, pos, par, wq, wk, wv)


LOG2E = math.log2(math.e)
NEG = -1e30

def split_scaled(q, scale):
    qs = q.astype(F32) * scale
    hi = qs.astype(BF16)
    lo = (qs - hi.astype(F32)).astype(BF16)
    return jnp.concatenate([hi, lo], axis=KEYS)

def decode(n, nblk):
    one = int if isinstance(n, int) else (lambda x: x.astype(jnp.int32))
    j = sum(one(n >= i * (i + 1)) for i in range(1, nblk // PAIR))
    r = n - j * (j + 1)
    odd = one(r > j)
    return PAIR * j + odd, r - odd * (j + 1)

def fwd_steps(nblk):
    return (nblk // PAIR) * (nblk // PAIR + 1)

def decode_up(n, nq):
    one = int if isinstance(n, int) else (lambda x: x.astype(jnp.int32))
    i = sum(one(n >= m * (m + 1) // PAIR) for m in range(1, nq))
    return i, n - i * (i + 1) // PAIR


def causal_bias(bias, bk, rows):
    d = lax.broadcasted_iota(jnp.int32, (bk, rows), 0) - lax.broadcasted_iota(jnp.int32, (bk, rows), 1)
    bias[0] = jnp.zeros((bk, rows), F32)
    bias[1] = jnp.where(d <= 0, 0.0, NEG)
    bias[PAIR] = jnp.where(d <= rows, 0.0, NEG)


class Fwd:
    def __init__(self, nblk, rows, heads, first, wide, qt, sink, lse, kk, vt, qb, q2, acc, mx, cm, ls, al, rt, lsv, sb, pb, bias, qsem, osem):
        self.__dict__.update(locals())
        self.bk = PAIR * rows
        self.groups = heads * wide
        self.cols = [span(u, rows) for u in range(self.groups)]
        self.halves = (range(0, self.groups // PAIR), range(self.groups // PAIR, self.groups))
        self.nq = nblk // wide
        self.nstep = fwd_steps(nblk) if wide == 1 else self.nq * (self.nq + 1) // PAIR

    def where(self, n):
        if self.wide == 1:
            i, t = decode(n, self.nblk)
            return i, t, t == i // PAIR
        i, t = decode_up(n, self.nq)
        return i, t, t == i

    def load_q(self, i):
        w = self.heads * self.rows
        src = slice(self.first * self.rows, self.first * self.rows + w)
        return [pltpu.make_async_copy(self.qt.at[self.wide * i + e, :, src], self.qb.at[:, span(e, w)], self.qsem.at[e]) for e in range(self.wide)]

    def make_q2(self, i):
        for u in range(self.groups):
            self.q2[i % PAIR, :, self.cols[u]] = split_scaled(self.qb[:, self.cols[u]], LOG2E * HEAD_DIM ** -0.5)

    def prepare(self):
        causal_bias(self.bias, self.bk, self.rows)
        for i in range(PAIR):
            for cp in self.load_q(i):
                cp.start()
            for cp in self.load_q(i):
                cp.wait()
            self.make_q2(i)
        for cp in self.load_q(PAIR):
            cp.start()
        self.acc[...] = jnp.zeros_like(self.acc)
        self.pb[...] = jnp.zeros_like(self.pb)
        self.ls[...] = jnp.zeros_like(self.ls)
        self.al[...] = jnp.zeros_like(self.al)
        self.mx[...] = jnp.zeros_like(self.mx)
        self.scores(0, 0)

    def keys(self, t):
        return pl.ds(pl.multiple_of(t * self.bk, self.bk), self.bk)

    def scores(self, n, part):
        i, t, last = self.where(n)
        kb = self.kk[self.keys(t), :]
        for u in self.halves[part]:
            kind = jnp.where(last, 1 + (i % PAIR if self.wide == 1 else u // self.heads), 0)
            s = jnp.dot(kb, self.q2[i % PAIR, :, self.cols[u]], preferred_element_type=F32) + self.bias[kind]
            self.sb[u] = s
            self.cm[:, self.cols[u]] = jnp.max(s.reshape(self.bk // 8, 8, self.rows), axis=KEYS)

    def soft(self, n, part):
        i, t, last = self.where(n)
        for u in self.halves[part]:
            c = self.cols[u]
            m0 = jnp.where(t == 0, NEG, self.mx[TOP, c])
            m1 = jnp.maximum(m0, jnp.max(self.cm[:, c], axis=KEYS, keepdims=YES))
            p = jnp.exp2(self.sb[u] - m1)
            a = jnp.exp2(m0 - m1)
            self.mx[TOP, c] = m1
            self.al[TOP, c] = a
            self.ls[:, c] = self.ls[:, c] * a + jnp.sum(p.reshape(self.bk // 8, 8, self.rows), axis=KEYS)
            self.pb[u] = p.astype(BF16)

    def values(self, n, part):
        i, t, last = self.where(n)
        vb = self.vt[:, self.keys(t)]
        for u in self.halves[part]:
            c = self.cols[u]
            self.acc[:, c] = self.acc[:, c] * self.al[TOP, c] + jnp.dot(vb, self.pb[u], preferred_element_type=F32)

    def out_lse(self, i):
        return pltpu.make_async_copy(self.lsv, self.lse.at[i], self.osem)

    def finish(self, i, part):
        self.sink.before(i, part)
        for u in self.halves[part]:
            c = self.cols[u]
            self.sink.store(u % self.heads, self.wide * i + u // self.heads, (self.acc[:, c] * self.rt[TOP, c]).astype(BF16))
        self.sink.after(i, part)

    def end_block(self, i):
        tot = jnp.sum(self.ls[...], axis=KEYS, keepdims=YES)
        self.rt[TOP, :] = 1.0 / tot
        if self.lse is not None:
            @pl.when(i > 0)
            def _():
                self.out_lse(i).wait()
            self.lsv[TOP, :] = self.mx[TOP, :] + jnp.log2(tot)
            self.out_lse(i).start()
        self.finish(i, 0)

        @pl.when(i + PAIR < self.nq)
        def _():
            for cp in self.load_q(i + PAIR):
                cp.wait()
            self.make_q2(i + PAIR)

        @pl.when(i + 3 < self.nq)
        def _():
            for cp in self.load_q(i + 3):
                cp.start()

    def step(self, n):
        n1 = jnp.minimum(n + 1, self.nstep - 1)
        self.scores(n, 1)
        self.soft(n, 0)
        self.values(jnp.maximum(n - 1, 0), 1)
        self.scores(n1, 0)
        self.soft(n, 1)
        self.values(n, 0)

    def run(self, on_step):
        @turns(self.nstep)
        def _(n):
            on_step(n)
            self.step(n)
            i, t, last = self.where(n)

            @pl.when((t == 0) & (n > 0))
            def _():
                self.finish(i - 1, 1)

            @pl.when(last)
            def _():
                self.end_block(i)

    def drain(self):
        self.values(self.nstep - 1, 1)
        self.finish(self.nq - 1, 1)
        if self.lse is not None:
            self.out_lse(self.nq - 1).wait()


def fwd_scratch(nblk, rows, groups, wide):
    vm = pltpu.VMEM
    w, bk = groups * rows, PAIR * rows
    return [vm((HEAD_DIM, w), BF16), vm((PAIR, PAIR * HEAD_DIM, w), BF16), vm((HEAD_DIM, w), F32)] + [vm((8, w), F32)] * 6 + [
            vm((groups, bk, rows), F32), vm((groups, bk, rows), BF16), vm((3, bk, rows), F32),
            pltpu.SemaphoreType.DMA((wide,)), pltpu.SemaphoreType.DMA]


NT = (((1,), (1,)), ((), ()))
SCALE = HEAD_DIM ** -0.5

def dot_nt(a, b):
    return lax.dot_general(a, b, NT, preferred_element_type=F32)

def bwd_steps(nq):
    return nq * (nq + 1) // PAIR

class Bwd:
    def __init__(self, nq, rows, qt, kk, kt, vv, dat, dlt, lsv, qb, q2, cs, dk, dv, dq, dbq, sb, dpb, pb, dsb, bias, dqs, psem):
        self.__dict__.update(locals())
        self.bk = PAIR * rows
        self.nstep = bwd_steps(nq)
        self.cols = [slice(0, rows), slice(rows, PAIR * rows)]

    def loads(self, i):
        slot = i % PAIR
        return [pltpu.make_async_copy(self.qt.at[PAIR * i + e, :, 0:self.rows], self.qb.at[slot, :, self.cols[e]], self.psem.at[slot, e]) for e in range(PAIR)]

    def make_q2(self, i):
        for e in range(PAIR):
            self.q2[i % PAIR, :, self.cols[e]] = split_scaled(self.qb[i % PAIR, :, self.cols[e]], LOG2E * SCALE)

    def prepare(self):
        nq = self.nq
        for i in (0, 1):
            for cp in self.loads(i):
                cp.start()
            for cp in self.loads(i):
                cp.wait()
            self.make_q2(i)
        causal_bias(self.bias, self.bk, self.rows)
        self.dk[...] = jnp.zeros_like(self.dk)
        self.dv[...] = jnp.zeros_like(self.dv)
        self.dq[...] = jnp.zeros_like(self.dq)
        self.dbq[...] = jnp.zeros_like(self.dbq)
        self.pb[...] = jnp.zeros_like(self.pb)
        self.dsb[...] = jnp.zeros_like(self.dsb)
        self.scores(0, 0)

    def keys(self, t):
        return pl.ds(pl.multiple_of(t * self.bk, self.bk), self.bk)

    def qcols(self, i, e):
        return pl.ds(pl.multiple_of(i * self.bk + e * self.rows, self.rows), self.rows)

    def scores(self, n, e):
        i, t = decode_up(n, self.nq)
        kind = jnp.where(t == i, 1 + e, 0)
        s = jnp.dot(self.kk[self.keys(t), :], self.q2[i % PAIR, :, self.cols[e]], preferred_element_type=F32)
        self.sb[e] = s + self.bias[kind]
        self.dpb[e] = jnp.dot(self.vv[self.keys(t), :], self.dat[:, self.qcols(i, e)], preferred_element_type=F32)

    def soft(self, n, e):
        i, t = decode_up(n, self.nq)
        c = self.qcols(i, e)
        p = jnp.exp2(self.sb[e] - self.lsv[TOP, c])
        self.pb[e] = p.astype(BF16)
        self.dsb[e] = (p * (self.dpb[e] - self.dlt[TOP, c])).astype(BF16)

    def grads(self, n, e):
        i, t = decode_up(n, self.nq)
        r = self.keys(t)
        self.dv[r, :] += dot_nt(self.pb[e], self.dat[:, self.qcols(i, e)])
        self.dk[r, :] += dot_nt(self.dsb[e], self.qb[i % PAIR, :, self.cols[e]])
        keep = jnp.where(t == 0, 0.0, 1.0)
        self.dq[:, self.cols[e]] = self.dq[:, self.cols[e]] * keep + jnp.dot(self.kt[:, self.keys(t)], self.dsb[e], preferred_element_type=F32)

    def step(self, n):
        n1 = jnp.minimum(n + 1, self.nstep - 1)
        self.scores(n, 1)
        self.soft(n, 0)
        self.grads(jnp.maximum(n - 1, 0), 1)
        self.scores(n1, 0)
        self.soft(n, 1)
        self.grads(n, 0)

    def finish(self, i, e):
        c = self.qcols(i, e)
        g = self.dq[:, self.cols[e]] * SCALE
        hd = HEAD_DIM // PAIR
        cos, sin = self.cs[0:hd, c], self.cs[hd:, c]
        a, b = g[:hd], g[hd:]
        a, b = a * cos + b * sin, b * cos - a * sin
        self.dbq[0:hd, :] += a
        self.dbq[hd:, :] += b
        blk = PAIR * i + e
        self.dqs[blk, 0:hd, :] = a.astype(BF16)
        self.dqs[blk, hd:, :] = b.astype(BF16)

    def run(self, on_step=lambda n: None):
        @turns(self.nstep)
        def _(n):
            on_step(n)
            self.step(n)
            i, t = decode_up(n, self.nq)

            @pl.when((t == 0) & (n > 0))
            def _():
                self.finish(i - 1, 1)

                @pl.when(i + 1 < self.nq)
                def _():
                    for cp in self.loads(i + 1):
                        cp.start()
                    for cp in self.loads(i + 1):
                        cp.wait()
                    self.make_q2(i + 1)

            @pl.when(t == i)
            def _():
                self.finish(i, 0)
        self.grads(self.nstep - 1, 1)
        self.finish(self.nq - 1, 1)


def bwd_scratch(nq, rows):
    vm = pltpu.VMEM
    bk, seq = PAIR * rows, PAIR * rows * nq
    return [vm((seq, PAIR * HEAD_DIM), BF16), vm((HEAD_DIM, seq), BF16), vm((seq, HEAD_DIM), BF16), vm((HEAD_DIM, seq), BF16), vm((8, seq), F32), vm((8, seq), F32),
            vm((PAIR, HEAD_DIM, bk), BF16), vm((PAIR, PAIR * HEAD_DIM, bk), BF16), vm((HEAD_DIM, seq), F32), vm((seq, HEAD_DIM), F32), vm((seq, HEAD_DIM), F32),
            vm((HEAD_DIM, bk), F32), vm((HEAD_DIM, rows), F32), vm((PAIR, bk, rows), F32), vm((PAIR, bk, rows), F32), vm((PAIR, bk, rows), BF16), vm((PAIR, bk, rows), BF16),
            vm((3, bk, rows), F32), vm((PAIR * nq, HEAD_DIM, rows), BF16), pltpu.SemaphoreType.DMA((PAIR, PAIR)), pltpu.SemaphoreType.DMA((PAIR * nq,))]


def load_bwd(k_h, kt_h, v_h, cs_h, lse_h, rows, nblk, kk, kt, vv, cs, lsv, sem):
    cps = [pltpu.make_async_copy(k_h, kk.at[:, 0:HEAD_DIM], sem.at[0]), pltpu.make_async_copy(k_h, kk.at[:, HEAD_DIM:], sem.at[1]),
           pltpu.make_async_copy(kt_h, kt, sem.at[PAIR]), pltpu.make_async_copy(v_h, vv, sem.at[3]), pltpu.make_async_copy(cs_h, cs, sem.at[4])]
    for c in cps:
        c.start()

    cps += [pltpu.make_async_copy(lse_h.at[b, :, 0:rows], lsv.at[:, span(b, rows)], sem.at[5 + b]) for b in range(nblk)]
    for c in cps[5:]:
        c.start()
    return cps


class GradAtt:
    def __init__(self, dy_h, at_h, nb, dat, dlt, wo_v, dyb, atb, sem):
        self.__dict__.update(locals())
        self.blk = dyb.shape[1]

    def copies(self, b):
        s = b % PAIR
        r = pl.ds(pl.multiple_of(b * self.blk, self.blk), self.blk)
        return [pltpu.make_async_copy(self.dy_h.at[r], self.dyb.at[s], self.sem.at[s]),
                pltpu.make_async_copy(self.at_h.at[0:HEAD_DIM, r], self.atb.at[s], self.sem.at[PAIR + s])]

    def start(self, b):
        for c in self.copies(b):
            c.start()

    def block(self, b):
        for c in self.copies(b):
            c.wait()
        d = dot_nt(self.dyb[b % PAIR], self.wo_v[...]).T.astype(BF16)
        r = pl.ds(pl.multiple_of(b * self.blk, self.blk), self.blk)
        self.dat[:, r] = d
        self.dlt[TOP, r] = jnp.sum(d.astype(F32) * self.atb[b % PAIR].astype(F32), axis=KEYS, keepdims=YES)


class Rows:
    def __init__(self, at, ats, rows, sem):
        self.at, self.ats, self.rows, self.sem = at, ats, rows, sem

    def copy(self, i, part):
        n = self.ats.shape[0] // PAIR
        r = span(part, n)
        return pltpu.make_async_copy(self.ats.at[r], self.at.at[r, pl.ds(pl.multiple_of(i * self.rows, self.rows), self.rows)], self.sem.at[part])

    def before(self, i, part):
        @pl.when(i > 0)
        def _():
            self.copy(i, part).wait()

    def store(self, g, blk, value):
        self.ats[span(g, HEAD_DIM), :] = value

    def after(self, i, part):
        self.copy(i, part).start()


def k2_kernel(n_sp, own_dy, qt, k_h, vt_h, dyf, at, lse, ao, kk, vt, ats, *scr):
    *scr, asem, send, recv, drecv, lsem, xsem = scr
    rows = own_dy.shape[0]
    heads = at.shape[0] // HEAD_DIM
    nz = n_sp // PAIR
    sp, dp = lax.axis_index('sp'), lax.axis_index('dp')
    ring = Ring(dyf, own_dy, rows, nz, (send, recv, drecv))
    loads = [pltpu.make_async_copy(k_h, kk.at[:, 0:HEAD_DIM], lsem.at[0]), pltpu.make_async_copy(k_h, kk.at[:, HEAD_DIM:], lsem.at[1]),
             pltpu.make_async_copy(vt_h, vt, lsem.at[PAIR])]
    for c in loads:
        c.start()
    greet_all(n_sp)
    ring.start()
    mine = pltpu.make_async_copy(own_dy, dyf.at[pl.ds(pl.multiple_of(sp * rows, rows), rows)], lsem.at[3])
    mine.start()
    for c in loads:
        c.wait()
    sink = Rows(at, ats, rows, asem)
    f = Fwd(n_sp, rows, heads, 0, 1, qt, sink, lse, kk, vt, *scr)
    f.prepare()

    def due(n):
        return jnp.clip((n - 3) // 5, 0, ring.nsend)

    def on_step(n):
        @pl.loop(due(n), due(n + 1))
        def _(j):
            ring.tick(j)
    f.run(on_step)
    f.drain()
    for part in range(PAIR):
        sink.copy(0, part).wait()
    other = (sp // PAIR) * PAIR + 1 - sp % PAIR
    give = pltpu.make_async_remote_copy(
        src_ref=at.at[:, pl.ds(pl.multiple_of(other * rows, rows), rows)], dst_ref=ao, send_sem=xsem.at[0], recv_sem=xsem.at[1],
        device_id=(dp, other), device_id_type=MESH)
    give.start()

    @pl.loop(due(f.nstep), ring.nsend)
    def _(j):
        ring.tick(j)

    for s in range(4):
        ring.wait_other(s)
    ring.d2d_own().wait_recv()
    give.wait()
    mine.wait()
    ring.finish_sends()


def k2(n_sp, own_dy, qt, k, vt):
    rows, dm = own_dy.shape
    seq = rows * n_sp
    heads = qt.shape[PAIR] // rows * 3 // 4
    sds, vm, dma = jax.ShapeDtypeStruct, pltpu.VMEM, pltpu.SemaphoreType.DMA
    outs = [sds((seq, dm), BF16), sds((heads * HEAD_DIM, seq), BF16), sds((n_sp, 8, heads * rows), F32), sds((heads * HEAD_DIM, rows), BF16)]
    return pl.pallas_call(
        functools.partial(k2_kernel, n_sp), out_shape=outs, in_specs=[ANY] * 4, out_specs=[ANY] * 4,
        scratch_shapes=[vm((seq, PAIR * HEAD_DIM), BF16), vm((HEAD_DIM, seq), BF16), vm((heads * HEAD_DIM, rows), BF16)] + fwd_scratch(n_sp, rows, heads, 1)
        + [dma((PAIR,))] + ring_sems(n_sp // PAIR) + [dma((4,)), dma((PAIR,))],
        compiler_params=pltpu.CompilerParams(collective_id=1, has_side_effects=YES, vmem_limit_bytes=62 * MIB),
        name='gather_attend')(own_dy, qt, k, vt)


TICK0 = (5, 6, 7, 9, 13, 15, 18, 19, 21, 24, 31, 32, 34, 35)
TICK1 = (10, 20, 25, 26, 27, 33)


class Relay:
    def __init__(self, blk, nr, nz, send, recv):
        self.blk, self.nr, self.nz, self.send, self.recv = blk, nr, nz, send, recv
        sp = lax.axis_index('sp')
        self.dp, self.z, self.c = lax.axis_index('dp'), sp // PAIR, sp % PAIR

    def copy(self, d, s, r):
        origin = (self.z + (self.nz - s if d == 0 else s)) % self.nz
        to = (self.z + (1 if d == 0 else self.nz - 1)) % self.nz
        ref = self.blk(origin, r)
        i = s * self.nr + r
        return pltpu.make_async_remote_copy(src_ref=ref, dst_ref=ref, send_sem=self.send.at[d], recv_sem=self.recv.at[d, i],
                                            device_id=(self.dp, to * PAIR + self.c), device_id_type=MESH)

    def own(self, r):
        for d in range(PAIR):
            self.copy(d, 0, r).start()

    def tick(self, s, r):
        for d in range(PAIR):
            if s == 3:
                @pl.when(r % PAIR == d)
                def _():
                    self.copy(d, 3, r).wait_recv()
            else:
                self.copy(d, s, r).wait_recv()
                if s == PAIR:
                    @pl.when(r % PAIR == d)
                    def _():
                        self.copy(d, 3, r).start()
                else:
                    self.copy(d, s + 1, r).start()

    def ticks(self, s, lo, hi):
        @pl.loop(lo, hi)
        def _(r):
            self.tick(s, r)

    def finish(self, ref):
        for d in range(PAIR):
            pltpu.make_async_copy(ref, ref, self.send.at[d]).wait()


def k3_kernel(nq, rows, dims, x_h, dyo_h, par, qt, at, ao, lse, k_h, kt_h, v_h, vt_h, cs_h, ht_h, dy_h, wq_h, wk_h, wv_h, wo_h,
              y_o, dx_o, dwq_o, dwk_o, dwv_o, dwo_o, small_o,
              kk, vt, ao2, cs, dk, dv, dqa, dqo, rs, kva, kvo, sma, smo, qsend, qrecv, rsend, rrecv, ksend, krecv, xsend, xrecv, ssend, srecv, tsend, trecv, tl, lq):
    nz, n_sp, heads = dims
    nblk = PAIR * nq
    hd = HEAD_DIM // PAIR
    qw = heads * HEAD_DIM
    bk = PAIR * rows
    dm = x_h.shape[1]
    cw = PAIR * HEAD_DIM
    vm = pltpu.VMEM
    dma = pltpu.SemaphoreType.DMA
    sp, dp = lax.axis_index('sp'), lax.axis_index('dp')
    z, c = sp // PAIR, sp % PAIR
    far = 1 - c
    other = z * PAIR + 1 - c
    peer = dict(device_id=(dp, other), device_id_type=MESH)

    relay = Relay(lambda o, r: dqa.at[o, r], nblk, nz, qsend, qrecv)
    kvr = Relay(lambda o, r: kva.at[o, pl.ds(pl.multiple_of(r * HEAD_DIM, HEAD_DIM), HEAD_DIM)], PAIR, nz, ksend, krecv)
    greet_all(n_sp)
    sma[sp] = jnp.zeros(sma.shape[1:], F32)

    nstep = bwd_steps(nq)
    own_at = [(r // PAIR + 1) * (r // PAIR + PAIR) // PAIR + r % PAIR + PAIR for r in range(nblk)]

    def count(n, at_step):
        return sum((n >= a).astype(jnp.int32) for a in at_step)

    def back(*scr):
        *scr, wo_v, dyb, atb, sem, sem2 = scr
        kt, vv, dat, dlt, lsv, qb, q2, dq, dbq, sb, dpb, pb, dsb, bias, psem = scr
        row0 = pl.multiple_of(c * qw + z * HEAD_DIM, HEAD_DIM)
        w_in = pltpu.make_async_copy(wo_h.at[pl.ds(row0, HEAD_DIM)], wo_v, sem2.at[4])
        w_in.start()
        vt_in = pltpu.make_async_copy(vt_h, vt, lq.at[0])
        vt_in.start()
        ga = GradAtt(dy_h, at, nq, dat, dlt, wo_v, dyb, atb, sem2)
        ga.start(0)
        kin = load_bwd(k_h, kt_h, v_h, cs_h, lse, rows, nblk, kk, kt, vv, cs, lsv, sem)
        ga.start(1)
        w_in.wait()
        ga.block(0)
        for cp in kin:
            cp.wait()
        vt_in.wait()
        b = Bwd(nq, rows, qt, kk, kt, vv, dat, dlt, lsv, qb, q2, cs, dk, dv, dq, dbq, sb, dpb, pb, dsb, bias, dqa.at[z], psem)
        b.prepare()
        t0 = [min(t, nstep) + 1 for t in TICK0]
        t1 = [min(t, nstep) + 1 for t in TICK1]

        def on_step(n):
            @pl.loop(count(n, own_at), count(n + 1, own_at))
            def _(r):
                relay.own(r)
            relay.ticks(0, count(n, t0), count(n + 1, t0))
            relay.ticks(1, count(n, t1), count(n + 1, t1))
            i, t = decode_up(n, nq)

            @pl.when((t == 0) & (i + 1 < nq))
            def _():
                @pl.when(i + PAIR < nq)
                def _():
                    ga.start(i + PAIR)
                ga.block(i + 1)
        b.run(on_step)
        own_in = sum(1 for a in own_at if a <= nstep)

        @pl.loop(own_in, nblk)
        def _(r):
            relay.own(r)
        sma[sp, 16:17, :] = jnp.sum(dbq[...].T, axis=KEYS, keepdims=YES)
    scr = bwd_scratch(nq, rows)
    keep = scr[1:8] + scr[11:18] + [scr[19]]
    pl.run_scoped(back, *keep, vm((HEAD_DIM, dm), BF16), vm((PAIR, bk, dm), BF16), vm((PAIR, HEAD_DIM, bk), BF16), dma((5 + nblk,)), dma((5,)))
    h0, h1 = sum(1 for t in TICK0 if t + 1 <= nstep), sum(1 for t in TICK1 if t + 1 <= nstep)

    def rs_block(d, s):
        b = (z + (PAIR * nz - 1 - s if d == 0 else 1 + s)) % nz
        return (dk if d == 0 else dv).at[pl.ds(pl.multiple_of(b * bk, bk), bk)]

    def rs_copy(d, s):
        to = (z + (1 if d == 0 else nz - 1)) % nz
        return pltpu.make_async_remote_copy(src_ref=rs_block(d, 0) if s == 0 else rs.at[d, s - 1], dst_ref=rs.at[d, s],
                                            send_sem=rsend.at[d], recv_sem=rrecv.at[d, s], device_id=(dp, to * PAIR + c), device_id_type=MESH)
    for d in range(PAIR):
        rs_copy(d, 0).start()

    def rs_step(s):
        for d in range(PAIR):
            rs_copy(d, s - 1).wait_recv()
            rs[d, s - 1] = rs[d, s - 1] + rs_block(d, s)[...]
        for d in range(PAIR):
            rs_copy(d, s).start()

    kv_give = pltpu.make_async_remote_copy(src_ref=kva.at[z, :, pl.ds(pl.multiple_of(far * rows, rows), rows)], dst_ref=kvo,
                                           send_sem=xsend.at[0], recv_sem=xrecv.at[0], **peer)

    def keys_whole():
        for d in range(PAIR):
            rs_copy(d, nz - PAIR).wait_recv()
        own = pl.ds(pl.multiple_of(z * bk, bk), bk)
        g = ((rs[0, nz - PAIR] + dk[own, :]) * SCALE).T
        a, b = g[:hd], g[hd:]
        cos, sin = cs[0:hd, own], cs[hd:, own]
        g = jnp.concatenate([a * cos + b * sin, b * cos - a * sin], axis=KEYS)
        sma[sp, 17:18, :] = jnp.sum(g.T, axis=KEYS, keepdims=YES)
        kva[z, 0:HEAD_DIM, :] = g.astype(BF16)
        g = rs[1, nz - PAIR] + dv[own, :]
        sma[sp, 18:19, :] = jnp.sum(g, axis=KEYS, keepdims=YES)
        kva[z, HEAD_DIM:, :] = g.T.astype(BF16)
        for r in range(PAIR):
            kvr.own(r)
        kv_give.start()

    def late(tile, aT, hta, sem):
        nslot = tile.shape[0]
        ht_in = [pltpu.make_async_copy(ht_h.at[0:qw], hta, lq.at[1])]

        def put(dst, piece, e):
            slot = piece % nslot
            src = tile.at[slot, :, span(e, HEAD_DIM)]
            return (pltpu.make_async_copy(src, dst, tl.at[slot, e]),
                    pltpu.make_async_remote_copy(src_ref=src, dst_ref=dst, send_sem=tsend.at[slot, e], recv_sem=trecv.at[piece // (dm // cw + 4 * (dm // qw))], **peer))

        def give(dsts, piece):
            for e in range(PAIR):
                for cp in put(dsts[e], piece, e):
                    cp.start()

        def free(piece):
            for e in range(PAIR):
                a, b = put(dwk_o.at[0:qw, 0:HEAD_DIM], piece, e)
                a.wait()
                b.wait_send()

        def att_part(atv, aob, xo, hsem):
            have = at.shape[0] // HEAD_DIM

            def head_rows(g):
                return pl.ds(pl.multiple_of((z + g) % heads * HEAD_DIM, HEAD_DIM), HEAD_DIM)

            def spread(src, dst, base):
                return [pltpu.make_async_copy(src.at[span(g, HEAD_DIM)], dst.at[head_rows(g)], hsem.at[base + g]) for g in range(have)]
            ins = spread(at, atv, 0) + spread(ao, aob, heads) + [pltpu.make_async_copy(x_h, xo, lq.at[3])]
            for cp in ins:
                cp.start()
            turn_rs, turn0, turn1 = [7, 14, 21, 28, 35], [PAIR, PAIR], [4, 10, 17, 24, 31]

            class Here:
                def before(self, i, part):
                    pass

                def store(self, g, blk, value):
                    atv[head_rows(have + g), pl.ds(pl.multiple_of(blk * rows, rows), rows)] = value

                def after(self, i, part):
                    pass

            def rest(*fscr):
                f = Fwd(nblk, rows, heads - have, have, PAIR, qt, Here(), None, kk, vt, *fscr)
                f.prepare()

                def on_step(n):
                    relay.ticks(0, h0 + count(n, turn0), h0 + count(n + 1, turn0))
                    relay.ticks(1, h1 + count(n, turn1), h1 + count(n + 1, turn1))
                    for s in range(1, 6):
                        @pl.when(n + 1 == turn_rs[s - 1])
                        def _():
                            rs_step(s)
                f.run(on_step)
                f.drain()
            pl.run_scoped(rest, *fwd_scratch(nblk, rows, PAIR * (heads - have), PAIR))
            gives = [pltpu.make_async_remote_copy(src_ref=atv.at[head_rows(have + g), pl.ds(pl.multiple_of(other * rows, rows), rows)],
                                                  dst_ref=ao2.at[span(g, HEAD_DIM)], send_sem=xsend.at[PAIR + g], recv_sem=xrecv.at[PAIR + g], **peer)
                     for g in range(heads - have)]
            ht_in[0].start()
            for cp in ins:
                cp.wait()

            def products(dyt, wt):
                nw = wt.shape[0]

                def dy_tile(n):
                    return pltpu.make_async_copy(dy_h.at[:, pl.ds(pl.multiple_of(n * cw, cw), cw)], dyt.at[n % PAIR], sem.at[n % PAIR])

                def w_tile(n):
                    return pltpu.make_async_copy(wo_h.at[:, pl.ds(pl.multiple_of(n * cw, cw), cw)], wt.at[n % nw], sem.at[PAIR + n % nw])
                dy_tile(0).start()
                for i in range(nw - 1):
                    w_tile(i).start()
                for cp in gives:
                    cp.start()
                ntile = dm // cw
                w1 = [PAIR, 5, 6, 8, 8]
                k1 = h1 + len(turn1)

                @turns(ntile)
                def _(n):
                    @pl.when(n + 1 < ntile)
                    def _():
                        dy_tile(n + 1).start()
                    relay.ticks(1, k1 + count(n, w1), k1 + count(n + 1, w1))

                    @pl.when(n == 3)
                    def _():
                        rs_step(6)

                    @pl.when(n == 6)
                    def _():
                        keys_whole()
                    dy_tile(n).wait()

                    @pl.when(n >= nslot)
                    def _():
                        free(n - nslot)
                    tile[n % nslot] = jnp.dot(atv[...], dyt[n % PAIR], preferred_element_type=F32)
                    rws = pl.ds(pl.multiple_of(c * qw, qw), qw)
                    give([dwo_o.at[rws, pl.ds(pl.multiple_of(n * cw + e * HEAD_DIM, HEAD_DIM), HEAD_DIM)] for e in range(PAIR)], n)
                relay.ticks(PAIR, 0, nblk // PAIR)

                for cp in gives:
                    cp.wait()
                for g in range(heads - have):
                    aob[head_rows(have + g), :] = ao2[span(g, HEAD_DIM), :]
                aT[:, pl.ds(pl.multiple_of(c * qw, qw), qw)] = atv[:, pl.ds(pl.multiple_of(sp * rows, rows), rows)].T
                aT[:, pl.ds(pl.multiple_of(far * qw, qw), qw)] = aob[...].T

                @turns(ntile)
                def _(n):
                    @pl.when(n + nw - 1 < ntile)
                    def _():
                        w_tile(n + nw - 1).start()
                    w_tile(n).wait()
                    cl = pl.ds(pl.multiple_of(n * cw, cw), cw)
                    xo[:, cl] = (xo[:, cl].astype(F32) + jnp.dot(aT[...], wt[n % nw], preferred_element_type=F32)).astype(BF16)
                out = pltpu.make_async_copy(xo, y_o, lq.at[PAIR])
                out.start()
                out.wait()
            pl.run_scoped(products, vm((PAIR, dy_h.shape[0], cw), BF16), vm((3, dm, cw), BF16))
        pl.run_scoped(att_part, vm((qw, dy_h.shape[0]), BF16), vm((qw, rows), BF16), vm((rows, dm), BF16), dma((PAIR * heads,)))
        pl.run_scoped(functools.partial(later, tile, aT, hta, ht_in[0], sem, nslot, give, free), vm((dm - qw, nblk * rows), BF16))

    def later(tile, aT, hta, hta_in, sem, nslot, give, free, htb):
        htb_in = pltpu.make_async_copy(ht_h.at[qw:], htb, lq.at[0])
        htb_in.start()
        nm = dm // qw
        once = jnp.minimum(z + 1, 1)

        def product(rhs_of, cols_of, nr, m, piece):
            free(piece - nslot)

            @turns(once)
            def _(_):
                acc = None
                for r in range(nr):
                    part = dot_nt((hta, htb)[m][:, cols_of(r)], rhs_of(r))
                    acc = part if acc is None else acc + part
                tile[piece % nslot] = acc

        def pair(p, piece, between):
            ha = (z + nz - p) % nz
            hb = jnp.where(p < nz // PAIR, (z + p) % nz, z)
            for m in range(nm):
                product(lambda r: jnp.concatenate([dqa[ha, r], dqa[hb, r]], axis=KEYS), lambda r: span(r, rows), nblk, m, piece + m)
                give([dwq_o.at[span(m, qw), pl.ds(pl.multiple_of(c * qw + h * HEAD_DIM, HEAD_DIM), HEAD_DIM)] for h in (ha, hb)], piece + m)
                if m == 0:
                    between()
        hta_in.wait()
        base = dm // cw
        def in_rows(wr, xo, dyo, wkv, dkp, dn):
            ins = [pltpu.make_async_copy(x_h, xo, lq.at[PAIR]), pltpu.make_async_copy(dyo_h, dyo, lq.at[3]),
                   pltpu.make_async_copy(wk_h, wkv.at[0], lq.at[5]), pltpu.make_async_copy(wv_h, wkv.at[1], lq.at[6])]
            for cp in ins:
                cp.start()

            nw = wr.shape[0]

            def w_tile(n):
                return pltpu.make_async_copy(wq_h.at[pl.ds(pl.multiple_of(n * cw, cw), cw)], wr.at[n % nw], sem.at[n % nw])
            for i in range(nw - 1):
                w_tile(i).start()
            dq_give = pltpu.make_async_remote_copy(src_ref=dqa.at[:, other], dst_ref=dqo, send_sem=xsend.at[1], recv_sem=xrecv.at[1], **peer)
            kvr.ticks(0, 0, PAIR)
            relay.ticks(PAIR, nblk // PAIR, nblk)
            @turns(nz // PAIR)
            def _(q):
                @pl.when(q == 1)
                def _():
                    kvr.ticks(1, 0, PAIR)

                @pl.when(q == PAIR)
                def _():
                    kvr.ticks(PAIR, 0, PAIR)

                @pl.when(q == 3)
                def _():
                    relay.ticks(3, 0, nblk)
                    dq_give.start()

                def between():
                    @pl.when(q == 0)
                    def _():
                        htb_in.wait()
                pair(q + 1, base + q * nm, between)
            kv_give.wait()
            dq_give.wait()
            for cp in ins:
                cp.wait()
            for h in range(nz):
                aT[:, pl.ds(pl.multiple_of(c * qw + h * HEAD_DIM, HEAD_DIM), HEAD_DIM)] = dqa[h, sp].T
                aT[:, pl.ds(pl.multiple_of(far * qw + h * HEAD_DIM, HEAD_DIM), HEAD_DIM)] = dqo[h].T
            for e in range(PAIR):
                er = span(e, HEAD_DIM)
                dkp[e, :, pl.ds(pl.multiple_of(c * HEAD_DIM, HEAD_DIM), HEAD_DIM)] = kva[z, er, pl.ds(pl.multiple_of(c * rows, rows), rows)].T
                dkp[e, :, pl.ds(pl.multiple_of(far * HEAD_DIM, HEAD_DIM), HEAD_DIM)] = kvo[er, :].T

            @turns(dm // cw)
            def _(n):
                @pl.when(n + nw - 1 < dm // cw)
                def _():
                    w_tile(n + nw - 1).start()
                w_tile(n).wait()
                rr = pl.ds(pl.multiple_of(n * cw, cw), cw)
                dn[:, rr] = dot_nt(aT[...], wr[n % nw]) + dot_nt(dkp[0], wkv[0, rr, :]) + dot_nt(dkp[1], wkv[1, rr, :])
            nr = 16
            gain = jnp.concatenate([par[g:g + 1, :] for g in range(dm // HEAD_DIM)], axis=1)

            @turns(rows // nr)
            def _(i):
                rr = pl.ds(pl.multiple_of(i * nr, nr), nr)
                xf = xo[rr, :].astype(F32)
                inv = lax.rsqrt(jnp.mean(xf * xf, axis=-1, keepdims=YES) + NORM_EPS)
                unit = xf * inv
                g = dn[rr, :]
                du = g * gain
                di = inv * (du - unit * jnp.mean(du * unit, axis=-1, keepdims=YES))
                xo[rr, :] = (dyo[rr, :].astype(F32) + di).astype(BF16)
                dn[rr, :] = g * unit
            tot = jnp.sum(dn[...], axis=KEYS, keepdims=YES)
            for j in range(dm // HEAD_DIM):
                sma[sp, j:j + 1, :] = tot[:, span(j, HEAD_DIM)]
            dx_out = pltpu.make_async_copy(xo, dx_o, lq.at[PAIR])
            dx_out.start()
            dx_out.wait()
        pl.run_scoped(in_rows, vm((4, cw, dm), BF16), vm((rows, dm), BF16), vm((rows, dm), BF16), vm((PAIR, dm, cw), BF16),
                      vm((PAIR, rows, cw), BF16), vm((rows, dm), F32))

        def small(o):
            return pltpu.make_async_remote_copy(src_ref=sma.at[sp], dst_ref=sma.at[sp], send_sem=ssend.at[0], recv_sem=srecv.at[0],
                                                device_id=(dp, (sp + o) % n_sp), device_id_type=MESH)

        @pl.loop(1, n_sp)
        def _(o):
            small(o).start()
        kvr.ticks(3, 0, PAIR)

        for m in range(nm):
            piece = base + 4 * nm + m
            product(lambda o: kva[o], lambda o: span(o, bk), nz, m, piece)
            give([w.at[span(m, qw), pl.ds(pl.multiple_of(c * HEAD_DIM, HEAD_DIM), HEAD_DIM)] for w in (dwk_o, dwv_o)], piece)
        npiece = base + 5 * nm
        for i in range(nslot):
            free(npiece - nslot + i)

        for i, got in enumerate((dwo_o, dwo_o.at[0:npiece * qw * cw // dm - dm, :])):
            pltpu.make_async_copy(got, got, trecv.at[i]).wait()
        ref = sma.at[pl.ds(0, n_sp - 1)]
        pltpu.make_async_copy(ref, ref, ssend.at[0]).wait()
        pltpu.make_async_copy(ref, ref, srecv.at[0]).wait()
        ng = dm // HEAD_DIM
        tot = sma[0, 0:ng, :]
        for o in range(1, n_sp):
            tot = tot + sma[o, 0:ng, :]
        smo[0:ng, :] = tot
        for cc in range(PAIR):
            for zz in range(nz):
                smo[ng + cc * nz + zz:ng + cc * nz + zz + 1, :] = sma[zz * PAIR + cc, 16:17, :]
            for e in range(PAIR):
                tot = sma[cc, 17 + e:18 + e, :]
                for zz in range(1, nz):
                    tot = tot + sma[zz * PAIR + cc, 17 + e:18 + e, :]
                smo[PAIR * ng + PAIR * e + cc:PAIR * ng + PAIR * e + cc + 1, :] = tot
        out = pltpu.make_async_copy(smo, small_o, lq.at[PAIR])
        out.start()
        out.wait()
    pl.run_scoped(late, vm((3, qw, cw), F32), vm((rows, dm), BF16), vm((qw, nblk * rows), BF16), dma((6,)))
    relay.finish(ht_h.at[0:7 * HEAD_DIM // PAIR, :])
    kvr.finish(dy_h.at[0:7 * HEAD_DIM * bk // dm, :])
    for d in range(PAIR):
        pltpu.make_async_copy(rs.at[d], rs.at[d], rsend.at[d]).wait()


def k3(n_sp, x, dy_own, par, qt, at, ao, lse, k, kt, v, vt, cs, ht, dyf, wq, wk, wv, wo):
    rows, dm = x.shape
    nblk, seq, nz = qt.shape[0], k.shape[0], n_sp // PAIR
    heads = qt.shape[PAIR] // rows
    npiece = dm // (PAIR * HEAD_DIM) + 5 * (dm // (heads * HEAD_DIM))
    sds, vm, dma = jax.ShapeDtypeStruct, pltpu.VMEM, pltpu.SemaphoreType.DMA
    ns = PAIR * (dm // HEAD_DIM) + 8
    scratch = [vm((seq, PAIR * HEAD_DIM), BF16), vm((HEAD_DIM, seq), BF16), vm((heads * HEAD_DIM - at.shape[0], rows), BF16), vm((HEAD_DIM, seq), F32), vm((seq, HEAD_DIM), F32), vm((seq, HEAD_DIM), F32), vm((nz, nblk, HEAD_DIM, rows), BF16), vm((nz, HEAD_DIM, rows), BF16),
               vm((PAIR, nz - 1, PAIR * rows, HEAD_DIM), F32), vm((nz, PAIR * HEAD_DIM, PAIR * rows), BF16), vm((PAIR * HEAD_DIM, rows), BF16), vm((n_sp, 24, HEAD_DIM), F32), vm((ns, HEAD_DIM), F32),
               dma((PAIR,)), dma((PAIR, 4 * nblk)), dma((PAIR,)), dma((PAIR, nz - 1)), dma((PAIR,)), dma((PAIR, 8)), dma((4,)), dma((4,)),
               dma((1,)), dma((1,)), dma((4, PAIR)), dma((PAIR,)), dma((4, PAIR)), dma((8,))]
    outs = [sds((rows, dm), BF16), sds((rows, dm), BF16), sds(wq.shape, F32), sds(wk.shape, F32), sds(wv.shape, F32), sds(wo.shape, F32), sds((ns, HEAD_DIM), F32)]
    return pl.pallas_call(
        functools.partial(k3_kernel, nblk // PAIR, rows, (nz, n_sp, heads)), out_shape=outs, in_specs=[ANY, ANY, VM] + [ANY] * 15, out_specs=[ANY] * len(outs),
        scratch_shapes=scratch, compiler_params=pltpu.CompilerParams(collective_id=PAIR, has_side_effects=YES, vmem_limit_bytes=63 * MIB),
        name='attend_back')(x, dy_own, par, qt, at, ao, lse, k, kt, v, vt, cs, ht, dyf, wq, wk, wv, wo)


def solution(mesh):
    n_sp = mesh.shape['sp']

    def step(hidden, d_out, positions, norm_gain, w_query, b_query, w_key, b_key, w_value, b_value, w_out):
        x, dy = hidden[0], d_out[0]
        rows, dm = x.shape
        par = jnp.concatenate([b.astype(F32).reshape(-1, HEAD_DIM) for b in (norm_gain, b_query, b_key, b_value)])
        hf, ht, qt, k, kt, v, vt, cs = k1(n_sp, x, positions, par, w_query, w_key, w_value)
        dyf, at, lse, ao = k2(n_sp, dy, qt, k, vt)
        y, dx, dwq, dwk, dwv, dwo, small = k3(n_sp, x, dy, par, qt, at, ao, lse, k, kt, v, vt, cs, ht, dyf, w_query, w_key, w_value, w_out)
        ng = dm // HEAD_DIM
        return (y[None], dx[None], small[:ng].reshape(-1), dwq, small[ng:PAIR * ng].reshape(-1), dwk, small[PAIR * ng:PAIR * ng + PAIR].reshape(-1),
                dwv, small[PAIR * ng + PAIR:PAIR * ng + 4].reshape(-1), dwo)

    seq_spec = P('dp', 'sp', None)
    in_specs = (seq_spec, seq_spec, P('dp', 'sp')) + (P(),) * 8
    out_specs = (seq_spec, seq_spec, P('dp'), P('dp', None), P('dp'), P('dp', None), P('dp'), P('dp', None), P('dp'), P('dp', None))
    return jax.shard_map(step, mesh=mesh, in_specs=in_specs, out_specs=out_specs, check_vma=False)
```

time: 764 us -> 431 us (0.56); the launches traced: 753 us -> 430 us
  waiting for transfers between devices: 180 us -> 0 us
  matrix products: 114 us -> 0 us
  Pallas kernels: 300 us -> 396 us
  local copies, waits for them, and re-layouts: 77.8 us -> 31.6 us
  blocking collectives: 40.8 us -> 0 us
  other arithmetic: 24.7 us -> 1.35 us
  between operations: 14.5 us -> 0.69 us
    psum x2 -> x0, waiting for transfers between devices: 180 us -> none  [the longest x1 102 us: step(): lax.psum(jnp.concatenate([dk, dv], axis=1), 'sp', axis_index_groups=planes)]
    pallas_call x1, Pallas kernels: 55.7 us -> 190 us  [k3(): pl.pallas_call(functools.partial(k3_kernel, nblk // PAIR, rows, (nz, n_sp...]
    dot_general x6 -> x0, matrix products: 85.4 us -> none  [mm(): return jnp.einsum(spec, a, b, preferred_element_type=F32)]
    unnamed x2 -> x0, matrix products: 29 us -> none
    pallas_call x1, Pallas kernels: 127 us -> 102 us  [k2(): pl.pallas_call(functools.partial(k2_kernel, n_sp), out_shape=outs, in_spe...]
    transpose x6 -> x0, local copies, waits for them, and re-layouts: 25 us -> none  [the longest x1 17.8 us: step(): dw_q.reshape(nz, 2, dm, HEAD_DIM).transpose(2, 1, 0, 3)]
    psum x1 -> x0, blocking collectives: 24.3 us -> none  [step(): d_gain = lax.psum(jnp.sum(gain_terms, axis=0), 'sp')]
    all_gather x1 -> x0, blocking collectives: 16.5 us -> none  [step(): lax.all_gather(jnp.sum(dbq, axis=1), 'sp', axis=0).reshape(nz, 2, HEAD_DIM)]
  transfers between devices with their start and end apart: 4 -> 0, of which waited for: 2 -> 0; matrix products, arithmetic and copies ran while one was open for 25% -> 0% of each run, Pallas kernels for 0% -> 0%
where the time goes in v2:
time: 431 us; the launch traced here: 430 us
  Pallas kernels  396 us (92%)
  local copies, waits for them, and re-layouts  31.6 us (7%)
    pallas_call x1, Pallas kernels, k3(): pl.pallas_call(functools.partial(k3_kernel, nblk // PAIR, rows, (nz, n_sp...  190 us
    pallas_call x1, Pallas kernels, k1(): pl.pallas_call(functools.partial(k1_kernel, n_sp), out_shape=outs, in_spe...  104 us
    pallas_call x1, Pallas kernels, k2(): pl.pallas_call(functools.partial(k2_kernel, n_sp), out_shape=outs, in_spe...  102 us
    unnamed x18, local copies, waits for them, and re-layouts  29 us

profile of v2, /device:TPU:21, one launch (start us, length us, event | category | flops | bytes accessed | tf_op | source)
XLA Modules:
  0.0 429.7 jit_solution(16681200288959316984)
XLA Ops:
  0.6 1.4 maximum_convert_fusion.par
  2.0 104.4 %gather_project.1 = (bf16[4096,2048]{1,0:T(8,128)(2,1)}, bf16[2048,4096]{1,0:T(8,128)(2,1)}, bf16[16,128,2048]{2,1,0:T(8,128)(2,1)}, bf16[4096,128]{1,0:T(8,128)...) custom-call(bf16[256,2048]{1,0:T(8,128)(2,1)} %bitcast.18, ...), custom_call_target="tpu_custom_call" | custom-call | tf_op jit(solution)/shard_map/gather_project/pallas_call | solution.py:275
  106.4 101.9 %gather_attend.1 = (bf16[4096,2048]{1,0:T(8,128)(2,1)}, bf16[768,4096]{1,0:T(8,128)(2,1)}, f32[16,8,1536]{2,1,0:T(8,128)}, bf16[768,256]{1,0:T(8,128)(2,1)}) custom-call(bf16[256,2048]{1,0:T(8,128)(2,1)} %bitcast.20, bf16[16,128,2048]{2,1,0:T(8,128)(2,1)} %get-tuple-element.28.qt, bf16[4096,128]{1,0:T(8,128)(2,1)} %get-tuple-element.29.k_h, ...), custom_call_target="tpu_custom_call" | custom-call | tf_op jit(solution)/shard_map/gather_attend/pallas_call | solution.py:699
  208.2 189.8 %attend_back.1 = (bf16[256,2048]{1,0:T(8,128)(2,1)}, bf16[256,2048]{1,0:T(8,128)(2,1)}, f32[2048,2048]{1,0:T(8,128)}, f32[2048,256]{1,0:T(8,128)}, f32[2048,256]...) custom-call(bf16[256,2048]{1,0:T(8,128)(2,1)} %bitcast.19, bf16[256,2048]{1,0:T(8,128)(2,1)} %bitcast.21, ...), custom_call_target="tpu_custom_call" | custom-call | tf_op jit(solution)/shard_map/attend_back/pallas_call | solution.py:1159
  398.1 1.3 slice_bitcast_fusion.2
  399.4 1.3 slice_bitcast_fusion
  400.7 2.3 copy.27
  403.0 0.0 slice-start
  403.0 2.5 copy.28
  405.5 0.0 copy-start.1
  405.5 0.0 copy-start
  405.5 0.0 slice-start.1
  405.5 0.0 slice-start.2
  405.5 0.0 slice-start.3
  405.5 13.6 %copy.29 = f32[2048,2048]{1,0:T(8,128)} copy(f32[2048,2048]{1,0:T(8,128)} %get-tuple-element.63) | data formatting | bytes 33554432
  419.1 0.0 copy-done.1
  419.1 1.3 copy.30
  420.4 0.0 copy-done
  420.4 1.3 copy.31
  421.7 0.0 slice-done
  421.7 0.0 slice-done.1
  421.7 0.1 slice-done.2
  421.8 1.7 slice-done.3
  423.5 6.2 %copy.32 = f32[2048,2048]{1,0:T(8,128)} copy(f32[2048,2048]{1,0:T(8,128)S(1)} %bitcast.17) | data formatting | bytes 33554432
  (1 shorter events, 0.0 us)
Async XLA Ops:
  403.0 18.7 %slice-start = ((s8[16777216]{0:T(1024)(128)(4,1)}), s8[4194304]{0:T(1024)(128)(4,1)S(1)}, s32[]{:S(2)}) async-start(s8[16777216]{0:T(1024)(128)(4,1)} %bitcast.16), calls=%async_computation | async-start | bytes 8388608
  405.5 13.6 %copy-start.1 = (f32[2048,256]{1,0:T(8,128)S(1)}, f32[2048,256]{1,0:T(8,128)}, u32[]{:S(2)}) copy-start(f32[2048,256]{1,0:T(8,128)} %get-tuple-element.65) | copy-start | bytes 6291460
  405.5 14.9 %copy-start = (f32[2048,256]{1,0:T(8,128)S(1)}, f32[2048,256]{1,0:T(8,128)}, u32[]{:S(2)}) copy-start(f32[2048,256]{1,0:T(8,128)} %get-tuple-element.67) | copy-start | bytes 6291460
  405.5 16.3 %slice-start.1 = ((s8[16777216]{0:T(1024)(128)(4,1)}), s8[4194304]{0:T(1024)(128)(4,1)S(1)}, s32[]{:S(2)}) async-start(s8[16777216]{0:T(1024)(128)(4,1)} %bitcast.16), calls=%async_computation.1 | async-start | bytes 8388608
  405.5 16.3 %slice-start.2 = ((s8[16777216]{0:T(1024)(128)(4,1)}), s8[4194304]{0:T(1024)(128)(4,1)S(1)}, s32[]{:S(2)}) async-start(s8[16777216]{0:T(1024)(128)(4,1)} %bitcast.16), calls=%async_computation.2 | async-start | bytes 8388608
  405.5 18.0 %slice-start.3 = ((s8[16777216]{0:T(1024)(128)(4,1)}), s8[4194304]{0:T(1024)(128)(4,1)S(1)}, s32[]{:S(2)}) async-start(s8[16777216]{0:T(1024)(128)(4,1)} %bitcast.16), calls=%async_computation.3 | async-start | bytes 8388608

commit v3 on v2

--- a/solution.py
+++ b/solution.py
@@ -10,7 +10,7 @@
 ROPE_BASE = 1000000.0
 NORM_EPS = 1e-6
 MESH = pl.DeviceIdType.MESH
-PAIR = 2
+PAIR, TRIO, QUAD = 2, 3, 4
 TOP = slice(0, 1)
 KEYS = 0
 YES = True
@@ -71,7 +71,7 @@
         off = pl.multiple_of(self.sp * self.rows, self.rows)
         return pltpu.make_async_remote_copy(
             src_ref=self.own, dst_ref=self.full.at[pl.ds(off, self.rows)],
-            send_sem=self.send.at[3], recv_sem=self.drecv.at[4],
+            send_sem=self.send.at[TRIO], recv_sem=self.drecv.at[QUAD],
             device_id=self.dev(self.z, 1 - self.c), device_id_type=MESH)
 
     def start(self):
@@ -104,11 +104,11 @@
         self.d2d_own().wait_send()
 
     def wait_other(self, s):
-        self.total(self.rows if s == 3 else PAIR * self.rows, self.drecv.at[s])
+        self.total(self.rows if s == TRIO else PAIR * self.rows, self.drecv.at[s])
 
 
 def ring_sems(nz):
-    return [pltpu.SemaphoreType.DMA((4,)), pltpu.SemaphoreType.DMA((PAIR, 7 * NSUB)), pltpu.SemaphoreType.DMA((5,))]
+    return [pltpu.SemaphoreType.DMA((QUAD,)), pltpu.SemaphoreType.DMA((PAIR, 7 * NSUB)), pltpu.SemaphoreType.DMA((5,))]
 
 
 def greet_all(n_sp):
@@ -118,7 +118,10 @@
     @pl.loop(1, n_sp)
     def _(o):
         pl.semaphore_signal(bar, inc=1, device_id=(dp, (sp + o) % n_sp), device_id_type=MESH)
-    pl.semaphore_wait(bar, n_sp - 1)
+
+    def all_here():
+        pl.semaphore_wait(bar, n_sp - 1)
+    return all_here
 
 
 def k1_kernel(n_sp, x_h, pos, par, wq, wk, wv, hf, ht, qt, k_o, kt_o, v_o, vt_o, cs_o,
@@ -136,6 +139,7 @@
     ring = Ring(hf, hf.at[mine], rows, nz, (send, recv, drecv))
     x_in = pltpu.make_async_copy(x_h, hb, lsem.at[0])
     x_in.start()
+    all_here = greet_all(n_sp)
     pos_copy = pltpu.make_async_copy(pos, pos_all.at[sp], lsem.at[1])
     pos_copy.start()
 
@@ -145,7 +149,7 @@
     wcopies = [pltpu.make_async_copy(wq.at[:, pl.ds(pl.multiple_of(c * qw + head_of(g) * HEAD_DIM, HEAD_DIM), HEAD_DIM)],
                                      wq_v.at[:, span(g, HEAD_DIM)], wsem.at[g]) for g in range(heads)]
     cols = pl.ds(pl.multiple_of(c * HEAD_DIM, HEAD_DIM), HEAD_DIM)
-    wcopies += [pltpu.make_async_copy(wk.at[:, cols], wk_v, lsem.at[PAIR]), pltpu.make_async_copy(wv.at[:, cols], wv_v, lsem.at[3])]
+    wcopies += [pltpu.make_async_copy(wk.at[:, cols], wk_v, lsem.at[PAIR]), pltpu.make_async_copy(wv.at[:, cols], wv_v, lsem.at[TRIO])]
     for w in wcopies:
         w.start()
     x_in.wait()
@@ -160,7 +164,7 @@
         hb[rr, :] = (xf * inv * gain).astype(BF16)
     own_out = pltpu.make_async_copy(hb, hf.at[mine], lsem.at[0])
     own_out.start()
-    greet_all(n_sp)
+    all_here()
 
     def pos_send(o):
         return pltpu.make_async_remote_copy(src_ref=pos, dst_ref=pos_all.at[sp], send_sem=psend.at[0], recv_sem=precv.at[0],
@@ -185,8 +189,8 @@
         return [pltpu.make_async_copy(htb, ht.at[:, cols], osem.at[0]),
                 pltpu.make_async_copy(qs, qt.at[blk], osem.at[1]),
                 pltpu.make_async_copy(ks, k_o.at[cols], osem.at[PAIR]),
-                pltpu.make_async_copy(kts, kt_o.at[:, cols], osem.at[3]),
-                pltpu.make_async_copy(vs, v_o.at[cols], osem.at[4]),
+                pltpu.make_async_copy(kts, kt_o.at[:, cols], osem.at[TRIO]),
+                pltpu.make_async_copy(vs, v_o.at[cols], osem.at[QUAD]),
                 pltpu.make_async_copy(vts, vt_o.at[:, cols], osem.at[5]),
                 pltpu.make_async_copy(css, cs_o.at[:, cols], osem.at[6])]
 
@@ -229,15 +233,15 @@
     @turns(n_sp)
     def _(n):
         m = n - PAIR
-        s = m // 4
-        b = jnp.where(s == 3, (m % 4) * PAIR, m % 4)
+        s = m // QUAD
+        b = jnp.where(s == TRIO, (m % QUAD) * PAIR, m % QUAD)
         other = jnp.where(n < PAIR, n, b // PAIR)
         left = b % PAIR == 0
         dist = jnp.where(n < PAIR, 0, s + 1)
 
-        @pl.when((n >= PAIR) & (m % 4 == 0))
+        @pl.when((n >= PAIR) & (m % QUAD == 0))
         def _():
-            @turns(jnp.where(s == 3, NSUB, PAIR * NSUB))
+            @turns(jnp.where(s == TRIO, NSUB, PAIR * NSUB))
             def _(r):
                 ring.tick(s * PAIR * NSUB + r)
 
@@ -245,7 +249,7 @@
         def _():
             ring.d2d_own().wait_recv()
 
-        for h in range(4):
+        for h in range(QUAD):
             @pl.when((n >= PAIR) & (other == 1) & left & (s == h))
             def _():
                 ring.wait_other(h)
@@ -271,7 +275,7 @@
     scratch = [vm((n_sp,) + pos.shape, jnp.int32), vm((dm, qw), BF16), vm((dm, HEAD_DIM), BF16), vm((dm, HEAD_DIM), BF16),
                vm((rows, dm), BF16), vm((dm, rows), BF16), vm((HEAD_DIM, heads * rows), BF16),
                vm((rows, HEAD_DIM), BF16), vm((HEAD_DIM, rows), BF16), vm((rows, HEAD_DIM), BF16), vm((HEAD_DIM, rows), BF16),
-               vm((HEAD_DIM, rows), F32)] + ring_sems(nz) + [dma((1,)), dma((1,)), dma((4,)), dma((heads,)), dma((7,))]
+               vm((HEAD_DIM, rows), F32)] + ring_sems(nz) + [dma((1,)), dma((1,)), dma((QUAD,)), dma((heads,)), dma((7,))]
     return pl.pallas_call(
         functools.partial(k1_kernel, n_sp), out_shape=outs,
         in_specs=[ANY, ANY, VM, ANY, ANY, ANY], out_specs=[ANY] * len(outs), scratch_shapes=scratch,
@@ -352,17 +356,19 @@
         self.ls[...] = jnp.zeros_like(self.ls)
         self.al[...] = jnp.zeros_like(self.al)
         self.mx[...] = jnp.zeros_like(self.mx)
-        self.scores(0, 0)
+        self.scores(0, 0, YES)
 
     def keys(self, t):
         return pl.ds(pl.multiple_of(t * self.bk, self.bk), self.bk)
 
-    def scores(self, n, part):
+    def scores(self, n, part, masked):
         i, t, last = self.where(n)
         kb = self.kk[self.keys(t), :]
         for u in self.halves[part]:
             kind = jnp.where(last, 1 + (i % PAIR if self.wide == 1 else u // self.heads), 0)
-            s = jnp.dot(kb, self.q2[i % PAIR, :, self.cols[u]], preferred_element_type=F32) + self.bias[kind]
+            s = jnp.dot(kb, self.q2[i % PAIR, :, self.cols[u]], preferred_element_type=F32)
+            if masked:
+                s = s + self.bias[kind]
             self.sb[u] = s
             self.cm[:, self.cols[u]] = jnp.max(s.reshape(self.bk // 8, 8, self.rows), axis=KEYS)
 
@@ -413,17 +419,17 @@
                 cp.wait()
             self.make_q2(i + PAIR)
 
-        @pl.when(i + 3 < self.nq)
+        @pl.when(i + TRIO < self.nq)
         def _():
-            for cp in self.load_q(i + 3):
+            for cp in self.load_q(i + TRIO):
                 cp.start()
 
-    def step(self, n):
+    def step(self, n, masked):
         n1 = jnp.minimum(n + 1, self.nstep - 1)
-        self.scores(n, 1)
+        self.scores(n, 1, masked)
         self.soft(n, 0)
         self.values(jnp.maximum(n - 1, 0), 1)
-        self.scores(n1, 0)
+        self.scores(n1, 0, masked)
         self.soft(n, 1)
         self.values(n, 0)
 
@@ -431,8 +437,19 @@
         @turns(self.nstep)
         def _(n):
             on_step(n)
-            self.step(n)
             i, t, last = self.where(n)
+            if self.wide == 1:
+                self.step(n, YES)
+            else:
+                masked = last | self.where(n + 1)[PAIR]
+
+                @pl.when(masked)
+                def _():
+                    self.step(n, YES)
+
+                @pl.when(jnp.logical_not(masked))
+                def _():
+                    self.step(n, False)
 
             @pl.when((t == 0) & (n > 0))
             def _():
@@ -453,7 +470,7 @@
     vm = pltpu.VMEM
     w, bk = groups * rows, PAIR * rows
     return [vm((HEAD_DIM, w), BF16), vm((PAIR, PAIR * HEAD_DIM, w), BF16), vm((HEAD_DIM, w), F32)] + [vm((8, w), F32)] * 6 + [
-            vm((groups, bk, rows), F32), vm((groups, bk, rows), BF16), vm((3, bk, rows), F32),
+            vm((groups, bk, rows), F32), vm((groups, bk, rows), BF16), vm((TRIO, bk, rows), F32),
             pltpu.SemaphoreType.DMA((wide,)), pltpu.SemaphoreType.DMA]
 
 
@@ -552,8 +569,14 @@
         @turns(self.nstep)
         def _(n):
             on_step(n)
+            i, t = decode_up(n, self.nq)
+
+            @pl.when((t == i) & (i > 0) & (i + 1 < self.nq))
+            def _():
+                for cp in self.loads(i + 1):
+                    cp.wait()
+                self.make_q2(i + 1)
             self.step(n)
-            i, t = decode_up(n, self.nq)
 
             @pl.when((t == 0) & (n > 0))
             def _():
@@ -563,9 +586,6 @@
                 def _():
                     for cp in self.loads(i + 1):
                         cp.start()
-                    for cp in self.loads(i + 1):
-                        cp.wait()
-                    self.make_q2(i + 1)
 
             @pl.when(t == i)
             def _():
@@ -580,12 +600,12 @@
     return [vm((seq, PAIR * HEAD_DIM), BF16), vm((HEAD_DIM, seq), BF16), vm((seq, HEAD_DIM), BF16), vm((HEAD_DIM, seq), BF16), vm((8, seq), F32), vm((8, seq), F32),
             vm((PAIR, HEAD_DIM, bk), BF16), vm((PAIR, PAIR * HEAD_DIM, bk), BF16), vm((HEAD_DIM, seq), F32), vm((seq, HEAD_DIM), F32), vm((seq, HEAD_DIM), F32),
             vm((HEAD_DIM, bk), F32), vm((HEAD_DIM, rows), F32), vm((PAIR, bk, rows), F32), vm((PAIR, bk, rows), F32), vm((PAIR, bk, rows), BF16), vm((PAIR, bk, rows), BF16),
-            vm((3, bk, rows), F32), vm((PAIR * nq, HEAD_DIM, rows), BF16), pltpu.SemaphoreType.DMA((PAIR, PAIR)), pltpu.SemaphoreType.DMA((PAIR * nq,))]
+            vm((TRIO, bk, rows), F32), vm((PAIR * nq, HEAD_DIM, rows), BF16), pltpu.SemaphoreType.DMA((PAIR, PAIR)), pltpu.SemaphoreType.DMA((PAIR * nq,))]
 
 
 def load_bwd(k_h, kt_h, v_h, cs_h, lse_h, rows, nblk, kk, kt, vv, cs, lsv, sem):
     cps = [pltpu.make_async_copy(k_h, kk.at[:, 0:HEAD_DIM], sem.at[0]), pltpu.make_async_copy(k_h, kk.at[:, HEAD_DIM:], sem.at[1]),
-           pltpu.make_async_copy(kt_h, kt, sem.at[PAIR]), pltpu.make_async_copy(v_h, vv, sem.at[3]), pltpu.make_async_copy(cs_h, cs, sem.at[4])]
+           pltpu.make_async_copy(kt_h, kt, sem.at[PAIR]), pltpu.make_async_copy(v_h, vv, sem.at[TRIO]), pltpu.make_async_copy(cs_h, cs, sem.at[QUAD])]
     for c in cps:
         c.start()
 
@@ -624,8 +644,8 @@
         self.at, self.ats, self.rows, self.sem = at, ats, rows, sem
 
     def copy(self, i, part):
-        n = self.ats.shape[0] // PAIR
-        r = span(part, n)
+        cut = self.ats.shape[0] // HEAD_DIM // PAIR * HEAD_DIM
+        r = slice(cut, None) if part else slice(0, cut)
         return pltpu.make_async_copy(self.ats.at[r], self.at.at[r, pl.ds(pl.multiple_of(i * self.rows, self.rows), self.rows)], self.sem.at[part])
 
     def before(self, i, part):
@@ -651,9 +671,9 @@
              pltpu.make_async_copy(vt_h, vt, lsem.at[PAIR])]
     for c in loads:
         c.start()
-    greet_all(n_sp)
+    greet_all(n_sp)()
     ring.start()
-    mine = pltpu.make_async_copy(own_dy, dyf.at[pl.ds(pl.multiple_of(sp * rows, rows), rows)], lsem.at[3])
+    mine = pltpu.make_async_copy(own_dy, dyf.at[pl.ds(pl.multiple_of(sp * rows, rows), rows)], lsem.at[TRIO])
     mine.start()
     for c in loads:
         c.wait()
@@ -662,7 +682,7 @@
     f.prepare()
 
     def due(n):
-        return jnp.clip((n - 3) // 5, 0, ring.nsend)
+        return jnp.clip((n - TRIO) // 6, 0, ring.nsend)
 
     def on_step(n):
         @pl.loop(due(n), due(n + 1))
@@ -682,7 +702,7 @@
     def _(j):
         ring.tick(j)
 
-    for s in range(4):
+    for s in range(QUAD):
         ring.wait_other(s)
     ring.d2d_own().wait_recv()
     give.wait()
@@ -693,13 +713,13 @@
 def k2(n_sp, own_dy, qt, k, vt):
     rows, dm = own_dy.shape
     seq = rows * n_sp
-    heads = qt.shape[PAIR] // rows * 3 // 4
+    heads = qt.shape[PAIR] // rows * 5 // 8
     sds, vm, dma = jax.ShapeDtypeStruct, pltpu.VMEM, pltpu.SemaphoreType.DMA
     outs = [sds((seq, dm), BF16), sds((heads * HEAD_DIM, seq), BF16), sds((n_sp, 8, heads * rows), F32), sds((heads * HEAD_DIM, rows), BF16)]
     return pl.pallas_call(
-        functools.partial(k2_kernel, n_sp), out_shape=outs, in_specs=[ANY] * 4, out_specs=[ANY] * 4,
+        functools.partial(k2_kernel, n_sp), out_shape=outs, in_specs=[ANY] * QUAD, out_specs=[ANY] * QUAD,
         scratch_shapes=[vm((seq, PAIR * HEAD_DIM), BF16), vm((HEAD_DIM, seq), BF16), vm((heads * HEAD_DIM, rows), BF16)] + fwd_scratch(n_sp, rows, heads, 1)
-        + [dma((PAIR,))] + ring_sems(n_sp // PAIR) + [dma((4,)), dma((PAIR,))],
+        + [dma((PAIR,))] + ring_sems(n_sp // PAIR) + [dma((QUAD,)), dma((PAIR,))],
         compiler_params=pltpu.CompilerParams(collective_id=1, has_side_effects=YES, vmem_limit_bytes=62 * MIB),
         name='gather_attend')(own_dy, qt, k, vt)
 
@@ -728,16 +748,16 @@
 
     def tick(self, s, r):
         for d in range(PAIR):
-            if s == 3:
+            if s == TRIO:
                 @pl.when(r % PAIR == d)
                 def _():
-                    self.copy(d, 3, r).wait_recv()
+                    self.copy(d, TRIO, r).wait_recv()
             else:
                 self.copy(d, s, r).wait_recv()
                 if s == PAIR:
                     @pl.when(r % PAIR == d)
                     def _():
-                        self.copy(d, 3, r).start()
+                        self.copy(d, TRIO, r).start()
                 else:
                     self.copy(d, s + 1, r).start()
 
@@ -752,7 +772,7 @@
 
 
 def k3_kernel(nq, rows, dims, x_h, dyo_h, par, qt, at, ao, lse, k_h, kt_h, v_h, vt_h, cs_h, ht_h, dy_h, wq_h, wk_h, wv_h, wo_h,
-              y_o, dx_o, dwq_o, dwk_o, dwv_o, dwo_o, small_o,
+              y_o, dx_o, dwq_o, dwo_o, small_o, kv_o, kvf_o,
               kk, vt, ao2, cs, dk, dv, dqa, dqo, rs, kva, kvo, sma, smo, qsend, qrecv, rsend, rrecv, ksend, krecv, xsend, xrecv, ssend, srecv, tsend, trecv, tl, lq):
     nz, n_sp, heads = dims
     nblk = PAIR * nq
@@ -771,7 +791,7 @@
 
     relay = Relay(lambda o, r: dqa.at[o, r], nblk, nz, qsend, qrecv)
     kvr = Relay(lambda o, r: kva.at[o, pl.ds(pl.multiple_of(r * HEAD_DIM, HEAD_DIM), HEAD_DIM)], PAIR, nz, ksend, krecv)
-    greet_all(n_sp)
+    all_here = greet_all(n_sp)
     sma[sp] = jnp.zeros(sma.shape[1:], F32)
 
     nstep = bwd_steps(nq)
@@ -784,7 +804,7 @@
         *scr, wo_v, dyb, atb, sem, sem2 = scr
         kt, vv, dat, dlt, lsv, qb, q2, dq, dbq, sb, dpb, pb, dsb, bias, psem = scr
         row0 = pl.multiple_of(c * qw + z * HEAD_DIM, HEAD_DIM)
-        w_in = pltpu.make_async_copy(wo_h.at[pl.ds(row0, HEAD_DIM)], wo_v, sem2.at[4])
+        w_in = pltpu.make_async_copy(wo_h.at[pl.ds(row0, HEAD_DIM)], wo_v, sem2.at[QUAD])
         w_in.start()
         vt_in = pltpu.make_async_copy(vt_h, vt, lq.at[0])
         vt_in.start()
@@ -797,6 +817,7 @@
         for cp in kin:
             cp.wait()
         vt_in.wait()
+        all_here()
         b = Bwd(nq, rows, qt, kk, kt, vv, dat, dlt, lsv, qb, q2, cs, dk, dv, dq, dbq, sb, dpb, pb, dsb, bias, dqa.at[z], psem)
         b.prepare()
         t0 = [min(t, nstep) + 1 for t in TICK0]
@@ -865,6 +886,15 @@
         for r in range(PAIR):
             kvr.own(r)
         kv_give.start()
+        kv_far(z).start()
+
+    def kv_far(o):
+        return pltpu.make_async_remote_copy(src_ref=kva.at[o], dst_ref=kvf_o.at[o], send_sem=tsend.at[0, PAIR], recv_sem=trecv.at[1], **peer)
+
+    def kv_tick(s):
+        kvr.ticks(s, 0, PAIR)
+        for o in (((z + nz - 1 - s) % nz, (z + 1 + s) % nz) if s < TRIO else ((z + nz // PAIR) % nz,)):
+            kv_far(o).start()
 
     def late(tile, aT, hta, sem):
         nslot = tile.shape[0]
@@ -874,7 +904,7 @@
             slot = piece % nslot
             src = tile.at[slot, :, span(e, HEAD_DIM)]
             return (pltpu.make_async_copy(src, dst, tl.at[slot, e]),
-                    pltpu.make_async_remote_copy(src_ref=src, dst_ref=dst, send_sem=tsend.at[slot, e], recv_sem=trecv.at[piece // (dm // cw + 4 * (dm // qw))], **peer))
+                    pltpu.make_async_remote_copy(src_ref=src, dst_ref=dst, send_sem=tsend.at[slot, e], recv_sem=trecv.at[0], **peer))
 
         def give(dsts, piece):
             for e in range(PAIR):
@@ -883,7 +913,7 @@
 
         def free(piece):
             for e in range(PAIR):
-                a, b = put(dwk_o.at[0:qw, 0:HEAD_DIM], piece, e)
+                a, b = put(dwo_o.at[0:qw, 0:HEAD_DIM], piece, e)
                 a.wait()
                 b.wait_send()
 
@@ -895,10 +925,10 @@
 
             def spread(src, dst, base):
                 return [pltpu.make_async_copy(src.at[span(g, HEAD_DIM)], dst.at[head_rows(g)], hsem.at[base + g]) for g in range(have)]
-            ins = spread(at, atv, 0) + spread(ao, aob, heads) + [pltpu.make_async_copy(x_h, xo, lq.at[3])]
+            ins = spread(at, atv, 0) + spread(ao, aob, heads) + [pltpu.make_async_copy(x_h, xo, lq.at[TRIO])]
             for cp in ins:
                 cp.start()
-            turn_rs, turn0, turn1 = [7, 14, 21, 28, 35], [PAIR, PAIR], [4, 10, 17, 24, 31]
+            turn_rs, turn0, turn1 = [6, 12, 18, 24, 30, 36], [PAIR, PAIR], [QUAD, 15, 27]
 
             class Here:
                 def before(self, i, part):
@@ -917,7 +947,7 @@
                 def on_step(n):
                     relay.ticks(0, h0 + count(n, turn0), h0 + count(n + 1, turn0))
                     relay.ticks(1, h1 + count(n, turn1), h1 + count(n + 1, turn1))
-                    for s in range(1, 6):
+                    for s in range(1, nz - 1):
                         @pl.when(n + 1 == turn_rs[s - 1])
                         def _():
                             rs_step(s)
@@ -927,7 +957,6 @@
             gives = [pltpu.make_async_remote_copy(src_ref=atv.at[head_rows(have + g), pl.ds(pl.multiple_of(other * rows, rows), rows)],
                                                   dst_ref=ao2.at[span(g, HEAD_DIM)], send_sem=xsend.at[PAIR + g], recv_sem=xrecv.at[PAIR + g], **peer)
                      for g in range(heads - have)]
-            ht_in[0].start()
             for cp in ins:
                 cp.wait()
 
@@ -940,12 +969,10 @@
                 def w_tile(n):
                     return pltpu.make_async_copy(wo_h.at[:, pl.ds(pl.multiple_of(n * cw, cw), cw)], wt.at[n % nw], sem.at[PAIR + n % nw])
                 dy_tile(0).start()
-                for i in range(nw - 1):
-                    w_tile(i).start()
                 for cp in gives:
                     cp.start()
                 ntile = dm // cw
-                w1 = [PAIR, 5, 6, 8, 8]
+                w1 = [1, PAIR, TRIO, QUAD, 5, 6, 7]
                 k1 = h1 + len(turn1)
 
                 @turns(ntile)
@@ -953,15 +980,24 @@
                     @pl.when(n + 1 < ntile)
                     def _():
                         dy_tile(n + 1).start()
+
+                    @pl.when(n == 1)
+                    def _():
+                        ht_in[0].start()
+
+                    @pl.when(n == QUAD)
+                    def _():
+                        for i in range(nw - 1):
+                            w_tile(i).start()
                     relay.ticks(1, k1 + count(n, w1), k1 + count(n + 1, w1))
 
-                    @pl.when(n == 3)
-                    def _():
-                        rs_step(6)
-
-                    @pl.when(n == 6)
+                    @pl.when(n == TRIO)
                     def _():
                         keys_whole()
+
+                    @pl.when(n == ntile - 1)
+                    def _():
+                        kv_tick(0)
                     dy_tile(n).wait()
 
                     @pl.when(n >= nslot)
@@ -990,7 +1026,7 @@
                 out = pltpu.make_async_copy(xo, y_o, lq.at[PAIR])
                 out.start()
                 out.wait()
-            pl.run_scoped(products, vm((PAIR, dy_h.shape[0], cw), BF16), vm((3, dm, cw), BF16))
+            pl.run_scoped(products, vm((PAIR, dy_h.shape[0], cw), BF16), vm((TRIO, dm, cw), BF16))
         pl.run_scoped(att_part, vm((qw, dy_h.shape[0]), BF16), vm((qw, rows), BF16), vm((rows, dm), BF16), dma((PAIR * heads,)))
         pl.run_scoped(functools.partial(later, tile, aT, hta, ht_in[0], sem, nslot, give, free), vm((dm - qw, nblk * rows), BF16))
 
@@ -1002,6 +1038,7 @@
 
         def product(rhs_of, cols_of, nr, m, piece):
             free(piece - nslot)
+
 
             @turns(once)
             def _(_):
@@ -1021,8 +1058,12 @@
                     between()
         hta_in.wait()
         base = dm // cw
+        def small(o):
+            return pltpu.make_async_remote_copy(src_ref=sma.at[sp], dst_ref=sma.at[sp], send_sem=ssend.at[0], recv_sem=srecv.at[0],
+                                                device_id=(dp, (sp + o) % n_sp), device_id_type=MESH)
+
         def in_rows(wr, xo, dyo, wkv, dkp, dn):
-            ins = [pltpu.make_async_copy(x_h, xo, lq.at[PAIR]), pltpu.make_async_copy(dyo_h, dyo, lq.at[3]),
+            ins = [pltpu.make_async_copy(x_h, xo, lq.at[PAIR]), pltpu.make_async_copy(dyo_h, dyo, lq.at[TRIO]),
                    pltpu.make_async_copy(wk_h, wkv.at[0], lq.at[5]), pltpu.make_async_copy(wv_h, wkv.at[1], lq.at[6])]
             for cp in ins:
                 cp.start()
@@ -1034,90 +1075,84 @@
             for i in range(nw - 1):
                 w_tile(i).start()
             dq_give = pltpu.make_async_remote_copy(src_ref=dqa.at[:, other], dst_ref=dqo, send_sem=xsend.at[1], recv_sem=xrecv.at[1], **peer)
-            kvr.ticks(0, 0, PAIR)
+            kv_tick(1)
             relay.ticks(PAIR, nblk // PAIR, nblk)
+            def own_rows():
+                kv_give.wait()
+                dq_give.wait()
+                for cp in ins:
+                    cp.wait()
+                for h in range(nz):
+                    aT[:, pl.ds(pl.multiple_of(c * qw + h * HEAD_DIM, HEAD_DIM), HEAD_DIM)] = dqa[h, sp].T
+                    aT[:, pl.ds(pl.multiple_of(far * qw + h * HEAD_DIM, HEAD_DIM), HEAD_DIM)] = dqo[h].T
+                for e in range(PAIR):
+                    er = span(e, HEAD_DIM)
+                    dkp[e, :, pl.ds(pl.multiple_of(c * HEAD_DIM, HEAD_DIM), HEAD_DIM)] = kva[z, er, pl.ds(pl.multiple_of(c * rows, rows), rows)].T
+                    dkp[e, :, pl.ds(pl.multiple_of(far * HEAD_DIM, HEAD_DIM), HEAD_DIM)] = kvo[er, :].T
+
+                @turns(dm // cw)
+                def _(n):
+                    @pl.when(n + nw - 1 < dm // cw)
+                    def _():
+                        w_tile(n + nw - 1).start()
+                    w_tile(n).wait()
+                    rr = pl.ds(pl.multiple_of(n * cw, cw), cw)
+                    dn[:, rr] = dot_nt(aT[...], wr[n % nw]) + dot_nt(dkp[0], wkv[0, rr, :]) + dot_nt(dkp[1], wkv[1, rr, :])
+                nr = 16
+                gain = jnp.concatenate([par[g:g + 1, :] for g in range(dm // HEAD_DIM)], axis=1)
+
+                @turns(rows // nr)
+                def _(i):
+                    rr = pl.ds(pl.multiple_of(i * nr, nr), nr)
+                    xf = xo[rr, :].astype(F32)
+                    inv = lax.rsqrt(jnp.mean(xf * xf, axis=-1, keepdims=YES) + NORM_EPS)
+                    unit = xf * inv
+                    g = dn[rr, :]
+                    du = g * gain
+                    di = inv * (du - unit * jnp.mean(du * unit, axis=-1, keepdims=YES))
+                    xo[rr, :] = (dyo[rr, :].astype(F32) + di).astype(BF16)
+                    dn[rr, :] = g * unit
+                tot = jnp.sum(dn[...], axis=KEYS, keepdims=YES)
+                for j in range(dm // HEAD_DIM):
+                    sma[sp, j:j + 1, :] = tot[:, span(j, HEAD_DIM)]
+                pltpu.make_async_copy(xo, dx_o, lq.at[PAIR]).start()
+
+                @pl.loop(1, n_sp)
+                def _(o):
+                    small(o).start()
+
             @turns(nz // PAIR)
             def _(q):
-                @pl.when(q == 1)
-                def _():
-                    kvr.ticks(1, 0, PAIR)
-
                 @pl.when(q == PAIR)
                 def _():
-                    kvr.ticks(PAIR, 0, PAIR)
-
-                @pl.when(q == 3)
+                    kv_tick(PAIR)
+
+                @pl.when(q == TRIO)
                 def _():
-                    relay.ticks(3, 0, nblk)
+                    relay.ticks(TRIO, 0, nblk)
                     dq_give.start()
+                    own_rows()
 
                 def between():
                     @pl.when(q == 0)
                     def _():
                         htb_in.wait()
                 pair(q + 1, base + q * nm, between)
-            kv_give.wait()
-            dq_give.wait()
-            for cp in ins:
-                cp.wait()
-            for h in range(nz):
-                aT[:, pl.ds(pl.multiple_of(c * qw + h * HEAD_DIM, HEAD_DIM), HEAD_DIM)] = dqa[h, sp].T
-                aT[:, pl.ds(pl.multiple_of(far * qw + h * HEAD_DIM, HEAD_DIM), HEAD_DIM)] = dqo[h].T
-            for e in range(PAIR):
-                er = span(e, HEAD_DIM)
-                dkp[e, :, pl.ds(pl.multiple_of(c * HEAD_DIM, HEAD_DIM), HEAD_DIM)] = kva[z, er, pl.ds(pl.multiple_of(c * rows, rows), rows)].T
-                dkp[e, :, pl.ds(pl.multiple_of(far * HEAD_DIM, HEAD_DIM), HEAD_DIM)] = kvo[er, :].T
-
-            @turns(dm // cw)
-            def _(n):
-                @pl.when(n + nw - 1 < dm // cw)
-                def _():
-                    w_tile(n + nw - 1).start()
-                w_tile(n).wait()
-                rr = pl.ds(pl.multiple_of(n * cw, cw), cw)
-                dn[:, rr] = dot_nt(aT[...], wr[n % nw]) + dot_nt(dkp[0], wkv[0, rr, :]) + dot_nt(dkp[1], wkv[1, rr, :])
-            nr = 16
-            gain = jnp.concatenate([par[g:g + 1, :] for g in range(dm // HEAD_DIM)], axis=1)
-
-            @turns(rows // nr)
-            def _(i):
-                rr = pl.ds(pl.multiple_of(i * nr, nr), nr)
-                xf = xo[rr, :].astype(F32)
-                inv = lax.rsqrt(jnp.mean(xf * xf, axis=-1, keepdims=YES) + NORM_EPS)
-                unit = xf * inv
-                g = dn[rr, :]
-                du = g * gain
-                di = inv * (du - unit * jnp.mean(du * unit, axis=-1, keepdims=YES))
-                xo[rr, :] = (dyo[rr, :].astype(F32) + di).astype(BF16)
-                dn[rr, :] = g * unit
-            tot = jnp.sum(dn[...], axis=KEYS, keepdims=YES)
-            for j in range(dm // HEAD_DIM):
-                sma[sp, j:j + 1, :] = tot[:, span(j, HEAD_DIM)]
-            dx_out = pltpu.make_async_copy(xo, dx_o, lq.at[PAIR])
-            dx_out.start()
-            dx_out.wait()
-        pl.run_scoped(in_rows, vm((4, cw, dm), BF16), vm((rows, dm), BF16), vm((rows, dm), BF16), vm((PAIR, dm, cw), BF16),
+            pltpu.make_async_copy(xo, dx_o, lq.at[PAIR]).wait()
+        pl.run_scoped(in_rows, vm((QUAD, cw, dm), BF16), vm((rows, dm), BF16), vm((rows, dm), BF16), vm((PAIR, dm, cw), BF16),
                       vm((PAIR, rows, cw), BF16), vm((rows, dm), F32))
 
-        def small(o):
-            return pltpu.make_async_remote_copy(src_ref=sma.at[sp], dst_ref=sma.at[sp], send_sem=ssend.at[0], recv_sem=srecv.at[0],
-                                                device_id=(dp, (sp + o) % n_sp), device_id_type=MESH)
-
-        @pl.loop(1, n_sp)
-        def _(o):
-            small(o).start()
-        kvr.ticks(3, 0, PAIR)
-
-        for m in range(nm):
-            piece = base + 4 * nm + m
-            product(lambda o: kva[o], lambda o: span(o, bk), nz, m, piece)
-            give([w.at[span(m, qw), pl.ds(pl.multiple_of(c * HEAD_DIM, HEAD_DIM), HEAD_DIM)] for w in (dwk_o, dwv_o)], piece)
-        npiece = base + 5 * nm
+        kv_tick(TRIO)
+        kv_out = pltpu.make_async_copy(kva, kv_o, lq.at[0])
+        kv_out.start()
+        npiece = base + QUAD * nm
         for i in range(nslot):
             free(npiece - nslot + i)
 
-        for i, got in enumerate((dwo_o, dwo_o.at[0:npiece * qw * cw // dm - dm, :])):
-            pltpu.make_async_copy(got, got, trecv.at[i]).wait()
+        pltpu.make_async_copy(dwo_o, dwo_o, trecv.at[0]).wait()
+        pltpu.make_async_copy(kvf_o, kvf_o, trecv.at[1]).wait()
+        pltpu.make_async_copy(kvf_o, kvf_o, tsend.at[0, PAIR]).wait()
+        kv_out.wait()
         ref = sma.at[pl.ds(0, n_sp - 1)]
         pltpu.make_async_copy(ref, ref, ssend.at[0]).wait()
         pltpu.make_async_copy(ref, ref, srecv.at[0]).wait()
@@ -1137,7 +1172,7 @@
         out = pltpu.make_async_copy(smo, small_o, lq.at[PAIR])
         out.start()
         out.wait()
-    pl.run_scoped(late, vm((3, qw, cw), F32), vm((rows, dm), BF16), vm((qw, nblk * rows), BF16), dma((6,)))
+    pl.run_scoped(late, vm((TRIO, qw, cw), F32), vm((rows, dm), BF16), vm((qw, nblk * rows), BF16), dma((6,)))
     relay.finish(ht_h.at[0:7 * HEAD_DIM // PAIR, :])
     kvr.finish(dy_h.at[0:7 * HEAD_DIM * bk // dm, :])
     for d in range(PAIR):
@@ -1153,13 +1188,102 @@
     ns = PAIR * (dm // HEAD_DIM) + 8
     scratch = [vm((seq, PAIR * HEAD_DIM), BF16), vm((HEAD_DIM, seq), BF16), vm((heads * HEAD_DIM - at.shape[0], rows), BF16), vm((HEAD_DIM, seq), F32), vm((seq, HEAD_DIM), F32), vm((seq, HEAD_DIM), F32), vm((nz, nblk, HEAD_DIM, rows), BF16), vm((nz, HEAD_DIM, rows), BF16),
                vm((PAIR, nz - 1, PAIR * rows, HEAD_DIM), F32), vm((nz, PAIR * HEAD_DIM, PAIR * rows), BF16), vm((PAIR * HEAD_DIM, rows), BF16), vm((n_sp, 24, HEAD_DIM), F32), vm((ns, HEAD_DIM), F32),
-               dma((PAIR,)), dma((PAIR, 4 * nblk)), dma((PAIR,)), dma((PAIR, nz - 1)), dma((PAIR,)), dma((PAIR, 8)), dma((4,)), dma((4,)),
-               dma((1,)), dma((1,)), dma((4, PAIR)), dma((PAIR,)), dma((4, PAIR)), dma((8,))]
-    outs = [sds((rows, dm), BF16), sds((rows, dm), BF16), sds(wq.shape, F32), sds(wk.shape, F32), sds(wv.shape, F32), sds(wo.shape, F32), sds((ns, HEAD_DIM), F32)]
+               dma((PAIR,)), dma((PAIR, QUAD * nblk)), dma((PAIR,)), dma((PAIR, nz - 1)), dma((PAIR,)), dma((PAIR, 8)), dma((5,)), dma((5,)),
+               dma((1,)), dma((1,)), dma((QUAD, TRIO)), dma((PAIR,)), dma((QUAD, PAIR)), dma((8,))]
+    outs = [sds((rows, dm), BF16), sds((rows, dm), BF16), sds(wq.shape, F32), sds(wo.shape, F32), sds((ns, HEAD_DIM), F32)] + [sds((nz, PAIR * HEAD_DIM, PAIR * rows), BF16)] * PAIR
     return pl.pallas_call(
         functools.partial(k3_kernel, nblk // PAIR, rows, (nz, n_sp, heads)), out_shape=outs, in_specs=[ANY, ANY, VM] + [ANY] * 15, out_specs=[ANY] * len(outs),
         scratch_shapes=scratch, compiler_params=pltpu.CompilerParams(collective_id=PAIR, has_side_effects=YES, vmem_limit_bytes=63 * MIB),
         name='attend_back')(x, dy_own, par, qt, at, ao, lse, k, kt, v, vt, cs, ht, dyf, wq, wk, wv, wo)
+
+
+def k4_kernel(y_h, dx_h, dwq_h, dwo_h, small, kv_h, kvf_h, ht_h, y_o, dx_o, dwq_o, dwk_o, dwv_o, dwo_o, g_o, bq_o, bk_o, bv_o,
+              buf, hbuf, kv, hts, wt, isem, osem, hsem, wsem, ksem):
+    nslot, half = buf.shape[0], buf.shape[0]
+    dm, rc = dwq_h.shape[0], buf.shape[1]
+    c = lax.axis_index('sp') % PAIR
+    for i, (src, dst) in enumerate(((y_h, y_o), (dx_h, dx_o))):
+        pltpu.make_async_copy(src, hbuf.at[i], hsem.at[i]).start()
+    kin = [pltpu.make_async_copy(kv_h, kv.at[c], ksem.at[0]), pltpu.make_async_copy(kvf_h, kv.at[1 - c], ksem.at[1])]
+    for cp in kin:
+        cp.start()
+    ng = dm // HEAD_DIM
+    g_o[...] = small[0:ng, :]
+    bq_o[...] = small[ng:PAIR * ng, :]
+    bk_o[...] = small[PAIR * ng:PAIR * ng + PAIR, :]
+    bv_o[...] = small[PAIR * ng + PAIR:PAIR * ng + QUAD, :]
+    n = dm // rc
+    work = [(src, dst, i) for i in range(n) for src, dst in ((dwq_h, dwq_o), (dwo_h, dwo_o))]
+
+    def into(i):
+        return pltpu.make_async_copy(work[i][0].at[pl.ds(work[i][PAIR] * rc, rc)], buf.at[i % nslot], isem.at[i % nslot])
+
+    def out(i):
+        return pltpu.make_async_copy(buf.at[i % nslot], work[i][1].at[pl.ds(work[i][PAIR] * rc, rc)], osem.at[i % nslot])
+    mr = hts.shape[1]
+
+    def ht_in(m):
+        return pltpu.make_async_copy(ht_h.at[pl.ds(pl.multiple_of(m * mr, mr), mr)], hts.at[m % PAIR], wsem.at[m % PAIR])
+
+    def w_out(m):
+        return [pltpu.make_async_copy(wt.at[m % PAIR, e], d.at[pl.ds(pl.multiple_of(m * mr, mr), mr)], wsem.at[PAIR + PAIR * e + m % PAIR]) for e, d in enumerate((dwk_o, dwv_o))]
+    for i in range(half):
+        into(i).start()
+    ht_in(0).start()
+    for cp in kin:
+        cp.wait()
+    steps = dm // mr
+    per = len(work) // steps
+    for m in range(steps):
+        if m + 1 < steps:
+            ht_in(m + 1).start()
+        for i in range(m * per, (m + 1) * per):
+            into(i).wait()
+            out(i).start()
+            if i >= half:
+                out(i - half).wait()
+            if i + half < len(work):
+                into(i + half).start()
+        ht_in(m).wait()
+        if m >= PAIR:
+            for cp in w_out(m - PAIR):
+                cp.wait()
+
+        @turns(PAIR)
+        def _(p):
+            acc = None
+            w = kv.shape[TRIO]
+            for o in range(kv.shape[1]):
+                part = dot_nt(hts[m % PAIR, :, span(o, w)], kv[p, o])
+                acc = part if acc is None else acc + part
+            cols = pl.ds(pl.multiple_of(p * HEAD_DIM, HEAD_DIM), HEAD_DIM)
+            for e in range(PAIR):
+                wt[m % PAIR, e, :, cols] = acc[:, span(e, HEAD_DIM)]
+        for cp in w_out(m):
+            cp.start()
+    for i, (src, dst) in enumerate(((y_h, y_o), (dx_h, dx_o))):
+        pltpu.make_async_copy(src, hbuf.at[i], hsem.at[i]).wait()
+        pltpu.make_async_copy(hbuf.at[i], dst, hsem.at[PAIR + i]).start()
+    for i in range(len(work) - half, len(work)):
+        out(i).wait()
+    for m in (steps - PAIR, steps - 1):
+        for cp in w_out(m):
+            cp.wait()
+    for i, (src, dst) in enumerate(((y_h, y_o), (dx_h, dx_o))):
+        pltpu.make_async_copy(hbuf.at[i], dst, hsem.at[PAIR + i]).wait()
+
+
+def k4(y, dx, dwq, dwo, small, kv, kvf, ht):
+    dm, ng = dwq.shape[0], dwq.shape[0] // HEAD_DIM
+    sds, vm, dma = jax.ShapeDtypeStruct, pltpu.VMEM, pltpu.SemaphoreType.DMA
+    wide = PAIR * HEAD_DIM
+    outs = [sds(y.shape, BF16), sds(dx.shape, BF16), sds(dwq.shape, F32), sds((dm, wide), F32), sds((dm, wide), F32), sds(dwo.shape, F32),
+            sds((ng, HEAD_DIM), F32), sds((ng, HEAD_DIM), F32), sds((PAIR, HEAD_DIM), F32), sds((PAIR, HEAD_DIM), F32)]
+    return pl.pallas_call(
+        k4_kernel, out_shape=outs, in_specs=[ANY] * QUAD + [VM] + [ANY] * TRIO, out_specs=[ANY] * 6 + [VM] * QUAD,
+        scratch_shapes=[vm((16, 256, dwq.shape[1]), F32), vm((PAIR,) + y.shape, BF16), vm((PAIR,) + kv.shape, BF16), vm((PAIR, dm // QUAD, ht.shape[1]), BF16),
+                        vm((PAIR, PAIR, dm // QUAD, wide), F32), dma((16,)), dma((16,)), dma((QUAD,)), dma((6,)), dma((PAIR,))],
+        compiler_params=pltpu.CompilerParams(vmem_limit_bytes=60 * MIB), name='place')(y, dx, dwq, dwo, small, kv, kvf, ht)
 
 
 def solution(mesh):
@@ -1171,10 +1295,9 @@
         par = jnp.concatenate([b.astype(F32).reshape(-1, HEAD_DIM) for b in (norm_gain, b_query, b_key, b_value)])
         hf, ht, qt, k, kt, v, vt, cs = k1(n_sp, x, positions, par, w_query, w_key, w_value)
         dyf, at, lse, ao = k2(n_sp, dy, qt, k, vt)
-        y, dx, dwq, dwk, dwv, dwo, small = k3(n_sp, x, dy, par, qt, at, ao, lse, k, kt, v, vt, cs, ht, dyf, w_query, w_key, w_value, w_out)
-        ng = dm // HEAD_DIM
-        return (y[None], dx[None], small[:ng].reshape(-1), dwq, small[ng:PAIR * ng].reshape(-1), dwk, small[PAIR * ng:PAIR * ng + PAIR].reshape(-1),
-                dwv, small[PAIR * ng + PAIR:PAIR * ng + 4].reshape(-1), dwo)
+        y, dx, dwq, dwo, small, kv, kvf = k3(n_sp, x, dy, par, qt, at, ao, lse, k, kt, v, vt, cs, ht, dyf, w_query, w_key, w_value, w_out)
+        y, dx, dwq, dwk, dwv, dwo, dg, dbq, dbk, dbv = k4(y, dx, dwq, dwo, small, kv, kvf, ht)
+        return y[None], dx[None], dg.reshape(-1), dwq, dbq.reshape(-1), dwk, dbk.reshape(-1), dwv, dbv.reshape(-1), dwo
 
     seq_spec = P('dp', 'sp', None)
     in_specs = (seq_spec, seq_spec, P('dp', 'sp')) + (P(),) * 8

time: 431 us -> 413 us (0.958)
  local copies, waits for them, and re-layouts: 31.6 us -> 0 us
  Pallas kernels: 396 us -> 409 us
    pallas_call x0 -> x1, Pallas kernels: none -> 33.1 us  [k4(): pl.pallas_call(k4_kernel, out_shape=outs, in_specs=[ANY] * QUAD + [VM] +...]
    unnamed x18 -> x0, local copies, waits for them, and re-layouts: 29 us -> none
    pallas_call x1, Pallas kernels: 190 us -> 181 us  [k3(): pl.pallas_call(functools.partial(k3_kernel, nblk // PAIR, rows, (nz, n_sp...]
    pallas_call x1, Pallas kernels: 102 us -> 93.2 us  [k2(): pl.pallas_call(functools.partial(k2_kernel, n_sp), out_shape=outs, in_spe...]
where the time goes in v3:
time: 413 us; the launch traced here: 412 us
  Pallas kernels  409 us (99%)
    pallas_call x1, Pallas kernels, k3(): pl.pallas_call(functools.partial(k3_kernel, nblk // PAIR, rows, (nz, n_sp...  181 us
    pallas_call x1, Pallas kernels, k1(): pl.pallas_call(functools.partial(k1_kernel, n_sp), out_shape=outs, in_spe...  102 us
    pallas_call x1, Pallas kernels, k2(): pl.pallas_call(functools.partial(k2_kernel, n_sp), out_shape=outs, in_spe...  93.2 us
    pallas_call x1, Pallas kernels, k4(): pl.pallas_call(k4_kernel, out_shape=outs, in_specs=[ANY] * QUAD + [VM] +...  33.1 us

profile of v3, /device:TPU:21, one launch (start us, length us, event | category | flops | bytes accessed | tf_op | source)
XLA Modules:
  0.0 411.7 jit_solution(4278238482199891088)
XLA Ops:
  0.6 1.3 maximum_convert_fusion.par
  2.0 102.2 %gather_project.1 = (bf16[4096,2048]{1,0:T(8,128)(2,1)}, bf16[2048,4096]{1,0:T(8,128)(2,1)}, bf16[16,128,2048]{2,1,0:T(8,128)(2,1)}, bf16[4096,128]{1,0:T(8,128)...) custom-call(bf16[256,2048]{1,0:T(8,128)(2,1)} %bitcast.12, ...), custom_call_target="tpu_custom_call" | custom-call | tf_op jit(solution)/shard_map/gather_project/pallas_call | solution.py:279
  104.2 93.2 %gather_attend.1 = (bf16[4096,2048]{1,0:T(8,128)(2,1)}, bf16[640,4096]{1,0:T(8,128)(2,1)}, f32[16,8,1280]{2,1,0:T(8,128)}, bf16[640,256]{1,0:T(8,128)(2,1)}) custom-call(bf16[256,2048]{1,0:T(8,128)(2,1)} %bitcast.14, bf16[16,128,2048]{2,1,0:T(8,128)(2,1)} %get-tuple-element.38.qt, bf16[4096,128]{1,0:T(8,128)(2,1)} %get-tuple-element.39.k_h, ...), custom_call_target="tpu_custom_call" | custom-call | tf_op jit(solution)/shard_map/gather_attend/pallas_call | solution.py:719
  197.4 181.0 %attend_back.1 = (bf16[256,2048]{1,0:T(8,128)(2,1)}, bf16[256,2048]{1,0:T(8,128)(2,1)}, f32[2048,2048]{1,0:T(8,128)}, f32[2048,2048]{1,0:T(8,128)}, f32[40,128]{...) custom-call(bf16[256,2048]{1,0:T(8,128)(2,1)} %bitcast.13, bf16[256,2048]{1,0:T(8,128)(2,1)} %bitcast.15, ...), custom_call_target="tpu_custom_call" | custom-call | tf_op jit(solution)/shard_map/attend_back/pallas_call | solution.py:1194
  378.4 33.1 %place.1 = (bf16[256,2048]{1,0:T(8,128)(2,1)}, bf16[256,2048]{1,0:T(8,128)(2,1)}, f32[2048,2048]{1,0:T(8,128)}, f32[2048,256]{1,0:T(8,128)}, f32[2048,256]{1,0:T...) custom-call(bf16[256,2048]{1,0:T(8,128)(2,1)} %get-tuple-element.49., ...), custom_call_target="tpu_custom_call" | custom-call | tf_op jit(solution)/shard_map/place/pallas_call | solution.py:1282

commit v4 on v3

--- a/solution.py
+++ b/solution.py
@@ -10,12 +10,13 @@
 ROPE_BASE = 1000000.0
 NORM_EPS = 1e-6
 MESH = pl.DeviceIdType.MESH
-PAIR, TRIO, QUAD = 2, 3, 4
+PAIR, TRIO, QUAD, OCTET = 2, 3, 4, 8
 TOP = slice(0, 1)
 KEYS = 0
 YES = True
 MIB = 1 << 20
 NSUB = PAIR
+SCALE = HEAD_DIM ** -0.5
 F32 = jnp.float32
 BF16 = jnp.bfloat16
 ANY = pl.BlockSpec(memory_space=pl.ANY)
@@ -124,8 +125,15 @@
     return all_here
 
 
-def k1_kernel(n_sp, x_h, pos, par, wq, wk, wv, hf, ht, qt, k_o, kt_o, v_o, vt_o, cs_o,
-              pos_all, wq_v, wk_v, wv_v, hb, htb, qs, ks, kts, vs, vts, css, send, recv, drecv, psend, precv, lsem, wsem, osem):
+def greet(peers):
+    bar = pltpu.get_barrier_semaphore()
+    for p in peers:
+        pl.semaphore_signal(bar, inc=1, device_id=p, device_id_type=MESH)
+    pl.semaphore_wait(bar, len(peers))
+
+
+def k1_kernel(n_sp, x_h, pos, par, wq, wk, wv, hf, ht, qt, k_o, kt_o, v_o, vt_o, cs_o, q2_o,
+              pos_all, wq_v, wk_v, wv_v, hb, htb, qs, ks, kts, vs, vts, cst, q2s, send, recv, drecv, psend, precv, lsem, wsem, osem):
     nz = n_sp // PAIR
     rows, dm = x_h.shape
     qw = wq_v.shape[1]
@@ -192,7 +200,13 @@
                 pltpu.make_async_copy(kts, kt_o.at[:, cols], osem.at[TRIO]),
                 pltpu.make_async_copy(vs, v_o.at[cols], osem.at[QUAD]),
                 pltpu.make_async_copy(vts, vt_o.at[:, cols], osem.at[5]),
-                pltpu.make_async_copy(css, cs_o.at[:, cols], osem.at[6])]
+                pltpu.make_async_copy(q2s, q2_o.at[blk], osem.at[6])]
+
+    def table(blk):
+        cols = pl.ds(pl.multiple_of(blk * rows, rows), rows)
+        ang = freq * pos_all[blk].astype(F32)
+        cst[0:half_dim, cols] = jnp.cos(ang)
+        cst[half_dim:, cols] = jnp.sin(ang)
 
     def compute(n, blk):
         load = pltpu.make_async_copy(hf.at[pl.ds(pl.multiple_of(blk * rows, rows), rows)], hb, lsem.at[0])
@@ -202,10 +216,8 @@
         def _():
             for o in outs(blk):
                 o.wait()
-        ang = freq * pos_all[blk].astype(F32)
-        cos, sin = jnp.cos(ang), jnp.sin(ang)
-        css[0:half_dim, :] = cos
-        css[half_dim:, :] = sin
+        cols = pl.ds(pl.multiple_of(blk * rows, rows), rows)
+        cos, sin = cst[0:half_dim, cols], cst[half_dim:, cols]
         h = hb[...]
         htb[...] = h.T
 
@@ -219,7 +231,9 @@
             t = q.T
             for e in range(PAIR):
                 hd = g * PAIR + e
-                qs[:, span(hd, rows)] = rope_t(t[span(e, HEAD_DIM)]).astype(BF16)
+                r = rope_t(t[span(e, HEAD_DIM)]).astype(BF16)
+                qs[:, span(hd, rows)] = r
+                q2s[:, span(hd, rows)] = split_scaled(r, LOG2E * SCALE)
         k = jnp.dot(h, wk_v[...], preferred_element_type=F32) + par[pl.ds(PAIR * ng + c, 1), :]
         kt = rope_t(k.T)
         kts[...] = kt.astype(BF16)
@@ -230,6 +244,10 @@
         for o in outs(blk):
             o.start()
 
+    table_out = pltpu.make_async_copy(cst, cs_o, osem.at[7])
+    table(sp)
+    table(z * PAIR + 1 - c)
+
     @turns(n_sp)
     def _(n):
         m = n - PAIR
@@ -256,8 +274,14 @@
         zb = (z + jnp.where(left, nz - dist, dist)) % nz
         cb = jnp.where(other == 1, 1 - c, c)
         compute(n, zb * PAIR + cb)
+
+        @pl.when(n == 1)
+        def _():
+            pl.loop(0, n_sp)(table)
+            table_out.start()
     for o in outs(0):
         o.wait()
+    table_out.wait()
     ring.finish_sends()
 
 
@@ -270,12 +294,12 @@
     sds = jax.ShapeDtypeStruct
     outs = [sds((seq, dm), BF16), sds((dm, seq), BF16), sds((n_sp, HEAD_DIM, heads * rows), BF16),
             sds((seq, HEAD_DIM), BF16), sds((HEAD_DIM, seq), BF16), sds((seq, HEAD_DIM), BF16), sds((HEAD_DIM, seq), BF16),
-            sds((HEAD_DIM, seq), F32)]
+            sds((HEAD_DIM, seq), F32), sds((n_sp, PAIR * HEAD_DIM, heads * rows), BF16)]
     vm, dma = pltpu.VMEM, pltpu.SemaphoreType.DMA
     scratch = [vm((n_sp,) + pos.shape, jnp.int32), vm((dm, qw), BF16), vm((dm, HEAD_DIM), BF16), vm((dm, HEAD_DIM), BF16),
                vm((rows, dm), BF16), vm((dm, rows), BF16), vm((HEAD_DIM, heads * rows), BF16),
                vm((rows, HEAD_DIM), BF16), vm((HEAD_DIM, rows), BF16), vm((rows, HEAD_DIM), BF16), vm((HEAD_DIM, rows), BF16),
-               vm((HEAD_DIM, rows), F32)] + ring_sems(nz) + [dma((1,)), dma((1,)), dma((QUAD,)), dma((heads,)), dma((7,))]
+               vm((HEAD_DIM, seq), F32), vm((PAIR * HEAD_DIM, heads * rows), BF16)] + ring_sems(nz) + [dma((1,)), dma((1,)), dma((QUAD,)), dma((heads,)), dma((OCTET,))]
     return pl.pallas_call(
         functools.partial(k1_kernel, n_sp), out_shape=outs,
         in_specs=[ANY, ANY, VM, ANY, ANY, ANY], out_specs=[ANY] * len(outs), scratch_shapes=scratch,
@@ -316,7 +340,7 @@
 
 
 class Fwd:
-    def __init__(self, nblk, rows, heads, first, wide, qt, sink, lse, kk, vt, qb, q2, acc, mx, cm, ls, al, rt, lsv, sb, pb, bias, qsem, osem):
+    def __init__(self, nblk, rows, heads, first, wide, q2h, sink, lse, kk, vt, q2, acc, mx, cm, ls, al, rt, lsv, sb, pb, bias, qsem, osem):
         self.__dict__.update(locals())
         self.bk = PAIR * rows
         self.groups = heads * wide
@@ -335,27 +359,20 @@
     def load_q(self, i):
         w = self.heads * self.rows
         src = slice(self.first * self.rows, self.first * self.rows + w)
-        return [pltpu.make_async_copy(self.qt.at[self.wide * i + e, :, src], self.qb.at[:, span(e, w)], self.qsem.at[e]) for e in range(self.wide)]
-
-    def make_q2(self, i):
-        for u in range(self.groups):
-            self.q2[i % PAIR, :, self.cols[u]] = split_scaled(self.qb[:, self.cols[u]], LOG2E * HEAD_DIM ** -0.5)
+        return [pltpu.make_async_copy(self.q2h.at[self.wide * i + e, :, src], self.q2.at[i % PAIR, :, span(e, w)], self.qsem.at[i % PAIR, e])
+                for e in range(self.wide)]
 
     def prepare(self):
+        for cp in self.load_q(0) + self.load_q(1):
+            cp.start()
         causal_bias(self.bias, self.bk, self.rows)
-        for i in range(PAIR):
-            for cp in self.load_q(i):
-                cp.start()
-            for cp in self.load_q(i):
-                cp.wait()
-            self.make_q2(i)
-        for cp in self.load_q(PAIR):
-            cp.start()
         self.acc[...] = jnp.zeros_like(self.acc)
         self.pb[...] = jnp.zeros_like(self.pb)
         self.ls[...] = jnp.zeros_like(self.ls)
         self.al[...] = jnp.zeros_like(self.al)
         self.mx[...] = jnp.zeros_like(self.mx)
+        for cp in self.load_q(0) + self.load_q(1):
+            cp.wait()
         self.scores(0, 0, YES)
 
     def keys(self, t):
@@ -370,7 +387,7 @@
             if masked:
                 s = s + self.bias[kind]
             self.sb[u] = s
-            self.cm[:, self.cols[u]] = jnp.max(s.reshape(self.bk // 8, 8, self.rows), axis=KEYS)
+            self.cm[:, self.cols[u]] = jnp.max(s.reshape(self.bk // OCTET, OCTET, self.rows), axis=KEYS)
 
     def soft(self, n, part):
         i, t, last = self.where(n)
@@ -382,7 +399,7 @@
             a = jnp.exp2(m0 - m1)
             self.mx[TOP, c] = m1
             self.al[TOP, c] = a
-            self.ls[:, c] = self.ls[:, c] * a + jnp.sum(p.reshape(self.bk // 8, 8, self.rows), axis=KEYS)
+            self.ls[:, c] = self.ls[:, c] * a + jnp.sum(p.reshape(self.bk // OCTET, OCTET, self.rows), axis=KEYS)
             self.pb[u] = p.astype(BF16)
 
     def values(self, n, part):
@@ -416,12 +433,6 @@
         @pl.when(i + PAIR < self.nq)
         def _():
             for cp in self.load_q(i + PAIR):
-                cp.wait()
-            self.make_q2(i + PAIR)
-
-        @pl.when(i + TRIO < self.nq)
-        def _():
-            for cp in self.load_q(i + TRIO):
                 cp.start()
 
     def step(self, n, masked):
@@ -438,6 +449,11 @@
         def _(n):
             on_step(n)
             i, t, last = self.where(n)
+
+            @pl.when(last & (i > 0) & (i + 1 < self.nq))
+            def _():
+                for cp in self.load_q(i + 1):
+                    cp.wait()
             if self.wide == 1:
                 self.step(n, YES)
             else:
@@ -469,13 +485,12 @@
 def fwd_scratch(nblk, rows, groups, wide):
     vm = pltpu.VMEM
     w, bk = groups * rows, PAIR * rows
-    return [vm((HEAD_DIM, w), BF16), vm((PAIR, PAIR * HEAD_DIM, w), BF16), vm((HEAD_DIM, w), F32)] + [vm((8, w), F32)] * 6 + [
+    return [vm((PAIR, PAIR * HEAD_DIM, w), BF16), vm((HEAD_DIM, w), F32)] + [vm((OCTET, w), F32)] * 6 + [
             vm((groups, bk, rows), F32), vm((groups, bk, rows), BF16), vm((TRIO, bk, rows), F32),
-            pltpu.SemaphoreType.DMA((wide,)), pltpu.SemaphoreType.DMA]
+            pltpu.SemaphoreType.DMA((PAIR, wide)), pltpu.SemaphoreType.DMA]
 
 
 NT = (((1,), (1,)), ((), ()))
-SCALE = HEAD_DIM ** -0.5
 
 def dot_nt(a, b):
     return lax.dot_general(a, b, NT, preferred_element_type=F32)
@@ -484,7 +499,7 @@
     return nq * (nq + 1) // PAIR
 
 class Bwd:
-    def __init__(self, nq, rows, qt, kk, kt, vv, dat, dlt, lsv, qb, q2, cs, dk, dv, dq, dbq, sb, dpb, pb, dsb, bias, dqs, psem):
+    def __init__(self, nq, rows, qt, q2h, kk, kt, vv, dat, dlt, lsv, qb, q2, cs, dk, dv, dq, dbq, sb, dpb, pb, dsb, bias, dqs, psem):
         self.__dict__.update(locals())
         self.bk = PAIR * rows
         self.nstep = bwd_steps(nq)
@@ -492,20 +507,12 @@
 
     def loads(self, i):
         slot = i % PAIR
-        return [pltpu.make_async_copy(self.qt.at[PAIR * i + e, :, 0:self.rows], self.qb.at[slot, :, self.cols[e]], self.psem.at[slot, e]) for e in range(PAIR)]
-
-    def make_q2(self, i):
-        for e in range(PAIR):
-            self.q2[i % PAIR, :, self.cols[e]] = split_scaled(self.qb[i % PAIR, :, self.cols[e]], LOG2E * SCALE)
-
-    def prepare(self):
-        nq = self.nq
-        for i in (0, 1):
-            for cp in self.loads(i):
-                cp.start()
-            for cp in self.loads(i):
-                cp.wait()
-            self.make_q2(i)
+        return [pltpu.make_async_copy(self.qt.at[PAIR * i + e, :, 0:self.rows], self.qb.at[slot, :, self.cols[e]], self.psem.at[slot, e]) for e in range(PAIR)] + [
+            pltpu.make_async_copy(self.q2h.at[PAIR * i + e, :, 0:self.rows], self.q2.at[slot, :, self.cols[e]], self.psem.at[slot, PAIR + e]) for e in range(PAIR)]
+
+    def clear(self):
+        for cp in self.loads(0) + self.loads(1):
+            cp.start()
         causal_bias(self.bias, self.bk, self.rows)
         self.dk[...] = jnp.zeros_like(self.dk)
         self.dv[...] = jnp.zeros_like(self.dv)
@@ -513,6 +520,10 @@
         self.dbq[...] = jnp.zeros_like(self.dbq)
         self.pb[...] = jnp.zeros_like(self.pb)
         self.dsb[...] = jnp.zeros_like(self.dsb)
+
+    def prepare(self):
+        for cp in self.loads(0) + self.loads(1):
+            cp.wait()
         self.scores(0, 0)
 
     def keys(self, t):
@@ -575,7 +586,6 @@
             def _():
                 for cp in self.loads(i + 1):
                     cp.wait()
-                self.make_q2(i + 1)
             self.step(n)
 
             @pl.when((t == 0) & (n > 0))
@@ -597,10 +607,10 @@
 def bwd_scratch(nq, rows):
     vm = pltpu.VMEM
     bk, seq = PAIR * rows, PAIR * rows * nq
-    return [vm((seq, PAIR * HEAD_DIM), BF16), vm((HEAD_DIM, seq), BF16), vm((seq, HEAD_DIM), BF16), vm((HEAD_DIM, seq), BF16), vm((8, seq), F32), vm((8, seq), F32),
+    return [vm((seq, PAIR * HEAD_DIM), BF16), vm((HEAD_DIM, seq), BF16), vm((seq, HEAD_DIM), BF16), vm((HEAD_DIM, seq), BF16), vm((OCTET, seq), F32), vm((OCTET, seq), F32),
             vm((PAIR, HEAD_DIM, bk), BF16), vm((PAIR, PAIR * HEAD_DIM, bk), BF16), vm((HEAD_DIM, seq), F32), vm((seq, HEAD_DIM), F32), vm((seq, HEAD_DIM), F32),
             vm((HEAD_DIM, bk), F32), vm((HEAD_DIM, rows), F32), vm((PAIR, bk, rows), F32), vm((PAIR, bk, rows), F32), vm((PAIR, bk, rows), BF16), vm((PAIR, bk, rows), BF16),
-            vm((TRIO, bk, rows), F32), vm((PAIR * nq, HEAD_DIM, rows), BF16), pltpu.SemaphoreType.DMA((PAIR, PAIR)), pltpu.SemaphoreType.DMA((PAIR * nq,))]
+            vm((TRIO, bk, rows), F32), vm((PAIR * nq, HEAD_DIM, rows), BF16), pltpu.SemaphoreType.DMA((PAIR, QUAD)), pltpu.SemaphoreType.DMA((PAIR * nq,))]
 
 
 def load_bwd(k_h, kt_h, v_h, cs_h, lse_h, rows, nblk, kk, kt, vv, cs, lsv, sem):
@@ -660,7 +670,7 @@
         self.copy(i, part).start()
 
 
-def k2_kernel(n_sp, own_dy, qt, k_h, vt_h, dyf, at, lse, ao, kk, vt, ats, *scr):
+def k2_kernel(n_sp, own_dy, q2h, k_h, vt_h, dyf, at, lse, ao, kk, vt, ats, *scr):
     *scr, asem, send, recv, drecv, lsem, xsem = scr
     rows = own_dy.shape[0]
     heads = at.shape[0] // HEAD_DIM
@@ -671,14 +681,14 @@
              pltpu.make_async_copy(vt_h, vt, lsem.at[PAIR])]
     for c in loads:
         c.start()
-    greet_all(n_sp)()
+    greet(((ring.dp, (ring.z + 1) % nz * PAIR + ring.c), (ring.dp, (ring.z + nz - 1) % nz * PAIR + ring.c), (ring.dp, ring.z * PAIR + 1 - ring.c)))
     ring.start()
     mine = pltpu.make_async_copy(own_dy, dyf.at[pl.ds(pl.multiple_of(sp * rows, rows), rows)], lsem.at[TRIO])
     mine.start()
     for c in loads:
         c.wait()
     sink = Rows(at, ats, rows, asem)
-    f = Fwd(n_sp, rows, heads, 0, 1, qt, sink, lse, kk, vt, *scr)
+    f = Fwd(n_sp, rows, heads, 0, 1, q2h, sink, lse, kk, vt, *scr)
     f.prepare()
 
     def due(n):
@@ -710,18 +720,18 @@
     ring.finish_sends()
 
 
-def k2(n_sp, own_dy, qt, k, vt):
+def k2(n_sp, own_dy, q2, k, vt):
     rows, dm = own_dy.shape
     seq = rows * n_sp
-    heads = qt.shape[PAIR] // rows * 5 // 8
+    heads = q2.shape[PAIR] // rows * 5 // OCTET
     sds, vm, dma = jax.ShapeDtypeStruct, pltpu.VMEM, pltpu.SemaphoreType.DMA
-    outs = [sds((seq, dm), BF16), sds((heads * HEAD_DIM, seq), BF16), sds((n_sp, 8, heads * rows), F32), sds((heads * HEAD_DIM, rows), BF16)]
+    outs = [sds((seq, dm), BF16), sds((heads * HEAD_DIM, seq), BF16), sds((n_sp, OCTET, heads * rows), F32), sds((heads * HEAD_DIM, rows), BF16)]
     return pl.pallas_call(
         functools.partial(k2_kernel, n_sp), out_shape=outs, in_specs=[ANY] * QUAD, out_specs=[ANY] * QUAD,
         scratch_shapes=[vm((seq, PAIR * HEAD_DIM), BF16), vm((HEAD_DIM, seq), BF16), vm((heads * HEAD_DIM, rows), BF16)] + fwd_scratch(n_sp, rows, heads, 1)
         + [dma((PAIR,))] + ring_sems(n_sp // PAIR) + [dma((QUAD,)), dma((PAIR,))],
         compiler_params=pltpu.CompilerParams(collective_id=1, has_side_effects=YES, vmem_limit_bytes=62 * MIB),
-        name='gather_attend')(own_dy, qt, k, vt)
+        name='gather_attend')(own_dy, q2, k, vt)
 
 
 TICK0 = (5, 6, 7, 9, 13, 15, 18, 19, 21, 24, 31, 32, 34, 35)
@@ -771,7 +781,7 @@
             pltpu.make_async_copy(ref, ref, self.send.at[d]).wait()
 
 
-def k3_kernel(nq, rows, dims, x_h, dyo_h, par, qt, at, ao, lse, k_h, kt_h, v_h, vt_h, cs_h, ht_h, dy_h, wq_h, wk_h, wv_h, wo_h,
+def k3_kernel(nq, rows, dims, x_h, dyo_h, par, qt, q2h, at, ao, lse, k_h, kt_h, v_h, vt_h, cs_h, ht_h, dy_h, wq_h, wk_h, wv_h, wo_h,
               y_o, dx_o, dwq_o, dwo_o, small_o, kv_o, kvf_o,
               kk, vt, ao2, cs, dk, dv, dqa, dqo, rs, kva, kvo, sma, smo, qsend, qrecv, rsend, rrecv, ksend, krecv, xsend, xrecv, ssend, srecv, tsend, trecv, tl, lq):
     nz, n_sp, heads = dims
@@ -812,13 +822,14 @@
         ga.start(0)
         kin = load_bwd(k_h, kt_h, v_h, cs_h, lse, rows, nblk, kk, kt, vv, cs, lsv, sem)
         ga.start(1)
+        b = Bwd(nq, rows, qt, q2h, kk, kt, vv, dat, dlt, lsv, qb, q2, cs, dk, dv, dq, dbq, sb, dpb, pb, dsb, bias, dqa.at[z], psem)
+        b.clear()
         w_in.wait()
         ga.block(0)
         for cp in kin:
             cp.wait()
         vt_in.wait()
         all_here()
-        b = Bwd(nq, rows, qt, kk, kt, vv, dat, dlt, lsv, qb, q2, cs, dk, dv, dq, dbq, sb, dpb, pb, dsb, bias, dqa.at[z], psem)
         b.prepare()
         t0 = [min(t, nstep) + 1 for t in TICK0]
         t1 = [min(t, nstep) + 1 for t in TICK1]
@@ -845,7 +856,7 @@
             relay.own(r)
         sma[sp, 16:17, :] = jnp.sum(dbq[...].T, axis=KEYS, keepdims=YES)
     scr = bwd_scratch(nq, rows)
-    keep = scr[1:8] + scr[11:18] + [scr[19]]
+    keep = scr[1:OCTET] + scr[11:18] + [scr[19]]
     pl.run_scoped(back, *keep, vm((HEAD_DIM, dm), BF16), vm((PAIR, bk, dm), BF16), vm((PAIR, HEAD_DIM, bk), BF16), dma((5 + nblk,)), dma((5,)))
     h0, h1 = sum(1 for t in TICK0 if t + 1 <= nstep), sum(1 for t in TICK1 if t + 1 <= nstep)
 
@@ -941,7 +952,7 @@
                     pass
 
             def rest(*fscr):
-                f = Fwd(nblk, rows, heads - have, have, PAIR, qt, Here(), None, kk, vt, *fscr)
+                f = Fwd(nblk, rows, heads - have, have, PAIR, q2h, Here(), None, kk, vt, *fscr)
                 f.prepare()
 
                 def on_step(n):
@@ -1179,22 +1190,22 @@
         pltpu.make_async_copy(rs.at[d], rs.at[d], rsend.at[d]).wait()
 
 
-def k3(n_sp, x, dy_own, par, qt, at, ao, lse, k, kt, v, vt, cs, ht, dyf, wq, wk, wv, wo):
+def k3(n_sp, x, dy_own, par, qt, q2, at, ao, lse, k, kt, v, vt, cs, ht, dyf, wq, wk, wv, wo):
     rows, dm = x.shape
     nblk, seq, nz = qt.shape[0], k.shape[0], n_sp // PAIR
     heads = qt.shape[PAIR] // rows
     npiece = dm // (PAIR * HEAD_DIM) + 5 * (dm // (heads * HEAD_DIM))
     sds, vm, dma = jax.ShapeDtypeStruct, pltpu.VMEM, pltpu.SemaphoreType.DMA
-    ns = PAIR * (dm // HEAD_DIM) + 8
+    ns = PAIR * (dm // HEAD_DIM) + OCTET
     scratch = [vm((seq, PAIR * HEAD_DIM), BF16), vm((HEAD_DIM, seq), BF16), vm((heads * HEAD_DIM - at.shape[0], rows), BF16), vm((HEAD_DIM, seq), F32), vm((seq, HEAD_DIM), F32), vm((seq, HEAD_DIM), F32), vm((nz, nblk, HEAD_DIM, rows), BF16), vm((nz, HEAD_DIM, rows), BF16),
                vm((PAIR, nz - 1, PAIR * rows, HEAD_DIM), F32), vm((nz, PAIR * HEAD_DIM, PAIR * rows), BF16), vm((PAIR * HEAD_DIM, rows), BF16), vm((n_sp, 24, HEAD_DIM), F32), vm((ns, HEAD_DIM), F32),
-               dma((PAIR,)), dma((PAIR, QUAD * nblk)), dma((PAIR,)), dma((PAIR, nz - 1)), dma((PAIR,)), dma((PAIR, 8)), dma((5,)), dma((5,)),
-               dma((1,)), dma((1,)), dma((QUAD, TRIO)), dma((PAIR,)), dma((QUAD, PAIR)), dma((8,))]
+               dma((PAIR,)), dma((PAIR, QUAD * nblk)), dma((PAIR,)), dma((PAIR, nz - 1)), dma((PAIR,)), dma((PAIR, OCTET)), dma((5,)), dma((5,)),
+               dma((1,)), dma((1,)), dma((QUAD, TRIO)), dma((PAIR,)), dma((QUAD, PAIR)), dma((OCTET,))]
     outs = [sds((rows, dm), BF16), sds((rows, dm), BF16), sds(wq.shape, F32), sds(wo.shape, F32), sds((ns, HEAD_DIM), F32)] + [sds((nz, PAIR * HEAD_DIM, PAIR * rows), BF16)] * PAIR
     return pl.pallas_call(
-        functools.partial(k3_kernel, nblk // PAIR, rows, (nz, n_sp, heads)), out_shape=outs, in_specs=[ANY, ANY, VM] + [ANY] * 15, out_specs=[ANY] * len(outs),
+        functools.partial(k3_kernel, nblk // PAIR, rows, (nz, n_sp, heads)), out_shape=outs, in_specs=[ANY, ANY, VM] + [ANY] * 16, out_specs=[ANY] * len(outs),
         scratch_shapes=scratch, compiler_params=pltpu.CompilerParams(collective_id=PAIR, has_side_effects=YES, vmem_limit_bytes=63 * MIB),
-        name='attend_back')(x, dy_own, par, qt, at, ao, lse, k, kt, v, vt, cs, ht, dyf, wq, wk, wv, wo)
+        name='attend_back')(x, dy_own, par, qt, q2, at, ao, lse, k, kt, v, vt, cs, ht, dyf, wq, wk, wv, wo)
 
 
 def k4_kernel(y_h, dx_h, dwq_h, dwo_h, small, kv_h, kvf_h, ht_h, y_o, dx_o, dwq_o, dwk_o, dwv_o, dwo_o, g_o, bq_o, bk_o, bv_o,
@@ -1293,13 +1304,13 @@
         x, dy = hidden[0], d_out[0]
         rows, dm = x.shape
         par = jnp.concatenate([b.astype(F32).reshape(-1, HEAD_DIM) for b in (norm_gain, b_query, b_key, b_value)])
-        hf, ht, qt, k, kt, v, vt, cs = k1(n_sp, x, positions, par, w_query, w_key, w_value)
-        dyf, at, lse, ao = k2(n_sp, dy, qt, k, vt)
-        y, dx, dwq, dwo, small, kv, kvf = k3(n_sp, x, dy, par, qt, at, ao, lse, k, kt, v, vt, cs, ht, dyf, w_query, w_key, w_value, w_out)
+        hf, ht, qt, k, kt, v, vt, cs, q2 = k1(n_sp, x, positions, par, w_query, w_key, w_value)
+        dyf, at, lse, ao = k2(n_sp, dy, q2, k, vt)
+        y, dx, dwq, dwo, small, kv, kvf = k3(n_sp, x, dy, par, qt, q2, at, ao, lse, k, kt, v, vt, cs, ht, dyf, w_query, w_key, w_value, w_out)
         y, dx, dwq, dwk, dwv, dwo, dg, dbq, dbk, dbv = k4(y, dx, dwq, dwo, small, kv, kvf, ht)
         return y[None], dx[None], dg.reshape(-1), dwq, dbq.reshape(-1), dwk, dbk.reshape(-1), dwv, dbv.reshape(-1), dwo
 
     seq_spec = P('dp', 'sp', None)
-    in_specs = (seq_spec, seq_spec, P('dp', 'sp')) + (P(),) * 8
+    in_specs = (seq_spec, seq_spec, P('dp', 'sp')) + (P(),) * OCTET
     out_specs = (seq_spec, seq_spec, P('dp'), P('dp', None), P('dp'), P('dp', None), P('dp'), P('dp', None), P('dp'), P('dp', None))
     return jax.shard_map(step, mesh=mesh, in_specs=in_specs, out_specs=out_specs, check_vma=False)

time: 413 us -> 410 us (level)
  no operation moved by 1% of the time
where the time goes in v4:
time: 410 us; the launch traced here: 409 us
  Pallas kernels  407 us (99%)
    pallas_call x1, Pallas kernels, k3(): pl.pallas_call(functools.partial(k3_kernel, nblk // PAIR, rows, (nz, n_sp...  178 us
    pallas_call x1, Pallas kernels, k1(): pl.pallas_call(functools.partial(k1_kernel, n_sp), out_shape=outs, in_spe...  104 us
    pallas_call x1, Pallas kernels, k2(): pl.pallas_call(functools.partial(k2_kernel, n_sp), out_shape=outs, in_spe...  91.7 us
    pallas_call x1, Pallas kernels, k4(): pl.pallas_call(k4_kernel, out_shape=outs, in_specs=[ANY] * QUAD + [VM] +...  32.9 us

profile of v4, /device:TPU:21, one launch (start us, length us, event | category | flops | bytes accessed | tf_op | source)
XLA Modules:
  0.0 409.1 jit_solution(9523255095918631251)
XLA Ops:
  0.6 1.3 maximum_convert_fusion.par
  2.0 103.8 %gather_project.1 = (bf16[4096,2048]{1,0:T(8,128)(2,1)}, bf16[2048,4096]{1,0:T(8,128)(2,1)}, bf16[16,128,2048]{2,1,0:T(8,128)(2,1)}, bf16[4096,128]{1,0:T(8,128)...) custom-call(bf16[256,2048]{1,0:T(8,128)(2,1)} %bitcast.14, ...), custom_call_target="tpu_custom_call" | custom-call | tf_op jit(solution)/shard_map/gather_project/pallas_call | solution.py:303
  105.8 91.7 %gather_attend.1 = (bf16[4096,2048]{1,0:T(8,128)(2,1)}, bf16[640,4096]{1,0:T(8,128)(2,1)}, f32[16,8,1280]{2,1,0:T(8,128)}, bf16[640,256]{1,0:T(8,128)(2,1)}) custom-call(bf16[256,2048]{1,0:T(8,128)(2,1)} %bitcast.12, bf16[16,256,2048]{2,1,0:T(8,128)(2,1)} %get-tuple-element.40.q2h, bf16[4096,128]{1,0:T(8,128)(2,1)} %get-tuple-element.41.k_h, ...), custom_call_target="tpu_custom_call" | custom-call | tf_op jit(solution)/shard_map/gather_attend/pallas_call | solution.py:729
  197.6 178.4 %attend_back.1 = (bf16[256,2048]{1,0:T(8,128)(2,1)}, bf16[256,2048]{1,0:T(8,128)(2,1)}, f32[2048,2048]{1,0:T(8,128)}, f32[2048,2048]{1,0:T(8,128)}, f32[40,128]{...) custom-call(bf16[256,2048]{1,0:T(8,128)(2,1)} %bitcast.15, bf16[256,2048]{1,0:T(8,128)(2,1)} %bitcast.13, ...), custom_call_target="tpu_custom_call" | custom-call | tf_op jit(solution)/shard_map/attend_back/pallas_call | solution.py:1205
  376.0 32.9 %place.1 = (bf16[256,2048]{1,0:T(8,128)(2,1)}, bf16[256,2048]{1,0:T(8,128)(2,1)}, f32[2048,2048]{1,0:T(8,128)}, f32[2048,256]{1,0:T(8,128)}, f32[2048,256]{1,0:T...) custom-call(bf16[256,2048]{1,0:T(8,128)(2,1)} %get-tuple-element.51., ...), custom_call_target="tpu_custom_call" | custom-call | tf_op jit(solution)/shard_map/place/pallas_call | solution.py:1293
